TPU v7x, 512 devices: a whole 4x8x8 slice. The times are simulated.
512 devices in a mesh: group: 16 (over z, core), dom: 32 (over x, y).
Axes of the slice: x: 4, y: 8, z: 8, core: 2. Of those that a mesh axis runs over, the one named last changes fastest.
Arguments:
- hot_rows: bfloat16 [65536, 1024], P(('group', 'dom')), may hold values from -24 to 24
- cold_codes: bfloat16 [65536, 1024], P(('group', 'dom')), may hold values from -127 to 127
- scale_index: int32 [65536], P(('group', 'dom')), may hold values from 0 to 255
- scale_table: float32 [256], replicated, may hold values from 0.004 to 0.04
- stale_rows: bfloat16 [65536, 1024], P(('group', 'dom')), may hold values from -6 to 6
- tile_index: int32 [1024, 3], P(('group', 'dom')), may hold values from 0 to 2
- tile_count: int32 [1024], P(('group', 'dom')), may hold values from 1 to 3
- tile_values: bfloat16 [1024, 3, 128, 128], P(('group', 'dom')), may hold values from -0.3125 to 0.3125
- weight: bfloat16 [1024, 1024], P('dom'), may hold values from -0.1875 to 0.1875
- out_grad: bfloat16 [131072, 1024], P(('group', 'dom')), may hold values from -6 to 6
- stale_grads: bfloat16 [65536, 1024], P(('group', 'dom')), may hold values from -6 to 6
- send_rows: int32 [16384, 4], P(('group', 'dom')), may hold values from 0 to 255
Outputs:
- activations: bfloat16 [131072, 1024], P(('group', 'dom'))
- feature_grad: bfloat16 [131072, 1024], P(('group', 'dom'))
- weight_grad: float32 [1024, 1024], P('dom')
- next_rows: bfloat16 [65536, 1024], P(('group', 'dom'))
- next_grads: bfloat16 [65536, 1024], P(('group', 'dom'))
Inputs may be any that keep to these rules, and one draw needn't show every extreme that they name: `send_rows`: rows may repeat.
All inputs are finite; a program needn't handle non-finite values.
Results may differ from a plain program's by a relative error of at most 0.0061.
Values may be sent and summed in bfloat16 or wider, within the bound.
No kernel may reach another device: no remote copies, remote signals or barrier semaphores. Data moves between devices by JAX's collectives and lax.ppermute only.
A program may use at most 64 MiB of HBM per device.

v0:
```python
import jax
import jax.numpy as jnp
from jax import lax
from jax.sharding import Mesh
from jax.sharding import PartitionSpec as P

DOM = ("dom_0", "dom_1")
GROUP_DOM = ("group", "dom_0", "dom_1")


def joined_along(tiles, dim):
    dims = list(tiles.shape[1:])
    dims[dim] *= tiles.shape[0]
    return jnp.moveaxis(tiles, 0, dim).reshape(dims)


def copy_for_each(shard, axis):
    copies = jnp.broadcast_to(shard, (lax.axis_size(axis), *shard.shape))
    return lax.all_to_all(copies, axis, split_axis=0, concat_axis=0, tiled=True)


def collect(shard, axis, dim):
    return joined_along(copy_for_each(shard, axis), dim)


def sum_by_axis(shard, axes, dim):
    if not axes:
        return shard
    nearer = lax.psum_scatter(shard, axes[0], scatter_dimension=dim, tiled=True)
    return sum_by_axis(nearer, axes[1:], dim)


def gathered_total(shard, axis):
    return lax.all_gather(shard, axis).sum(0)


def dequantize(cold_codes, scale_index, scale_table):
    levels = jnp.arange(scale_table.shape[0], dtype=jnp.int32)
    lookup = jnp.sum(
        jnp.where(
            scale_index[:, None] == levels[None, :],
            scale_table[None, :],
            jnp.zeros_like(scale_table)[None, :],
        ),
        axis=1,
    )
    return (cold_codes.astype(jnp.float32) * lookup[:, None]).astype(jnp.bfloat16)


def silu_parts(preact):
    logistic = jax.nn.sigmoid(preact)
    return (preact * logistic, logistic * (1.0 + preact * (1.0 - logistic)))


def local(
    hot_rows,
    cold_codes,
    scale_index,
    scale_table,
    stale_rows,
    tile_index,
    tile_count,
    tile_values,
    weight,
    out_grad,
    stale_grads,
    send_rows,
):
    tile_slots = tile_values.shape[1]
    cluster_rows = tile_values.shape[2]
    local_rows = jnp.concatenate(
        [hot_rows, dequantize(cold_codes, scale_index, scale_table)], axis=0
    )
    row_count = local_rows.shape[0]
    sends = send_rows.reshape(-1)
    outgoing = jnp.take(local_rows, sends, axis=0)
    next_rows = lax.all_to_all(outgoing, DOM, split_axis=0, concat_axis=0, tiled=True)
    source = jnp.concatenate([local_rows, stale_rows], axis=0)
    src_count = source.shape[0] // cluster_rows
    live_mask = jnp.arange(tile_slots, dtype=jnp.int32)[None, :] < tile_count[:, None]
    masked = jnp.where(
        live_mask[:, :, None, None], tile_values, jnp.zeros_like(tile_values)
    ).astype(jnp.float32)
    selector = (
        tile_index[:, :, None] == jnp.arange(src_count, dtype=jnp.int32)[None, None, :]
    ).astype(jnp.float32)
    operator = jnp.einsum("ckj,ckab->cajb", selector, masked, precision=lax.Precision.HIGHEST)
    operator = operator.reshape(row_count, src_count * cluster_rows)
    hidden = jnp.dot(operator, source.astype(jnp.float32), precision=lax.Precision.HIGHEST)
    hidden = hidden.astype(jnp.bfloat16)
    whole = collect(weight, DOM, 0)
    preact = jnp.dot(hidden, whole, preferred_element_type=jnp.float32)
    activ, slope = silu_parts(preact)
    activations = activ.astype(jnp.bfloat16)
    pre_grad = (out_grad.astype(jnp.float32) * slope).astype(jnp.bfloat16)
    hid_grad = lax.dot_general(
        pre_grad, whole, (((1,), (1,)), ((), ())), preferred_element_type=jnp.float32
    )
    hid_grad = hid_grad.astype(jnp.bfloat16)
    partial_value = lax.dot_general(
        hidden, pre_grad, (((0,), (0,)), ((), ())), preferred_element_type=jnp.float32
    )
    block_sum = sum_by_axis(partial_value, DOM, 0)
    weight_grad = gathered_total(block_sum, "group")
    src_grad = lax.dot_general(
        operator,
        hid_grad.astype(jnp.float32),
        (((0,), (0,)), ((), ())),
        precision=lax.Precision.HIGHEST,
    )
    bound_grad = src_grad[row_count:].astype(jnp.bfloat16)
    next_grads = lax.all_to_all(bound_grad, DOM, split_axis=0, concat_axis=0, tiled=True)
    placing = (jnp.arange(row_count, dtype=jnp.int32)[:, None] == sends[None, :]).astype(
        jnp.bfloat16
    )
    returned = jnp.dot(placing, stale_grads, preferred_element_type=jnp.float32)
    feature_grad = (src_grad[:row_count] + returned).astype(jnp.bfloat16)
    return (activations, feature_grad, weight_grad, next_rows, next_grads)


def solution(mesh):
    torus = Mesh(mesh.devices.reshape(mesh.shape["group"], 4, 8), ("group", "dom_0", "dom_1"))
    placed = (
        P(GROUP_DOM, None),
        P(GROUP_DOM, None),
        P(GROUP_DOM),
        P(),
        P(GROUP_DOM, None),
        P(GROUP_DOM, None),
        P(GROUP_DOM),
        P(GROUP_DOM, None, None, None),
        P(DOM, None),
        P(GROUP_DOM, None),
        P(GROUP_DOM, None),
        P(GROUP_DOM, None),
    )
    return jax.shard_map(
        local,
        mesh=torus,
        in_specs=placed,
        out_specs=(
            P(GROUP_DOM, None),
            P(GROUP_DOM, None),
            P(DOM, None),
            P(GROUP_DOM, None),
            P(GROUP_DOM, None),
        ),
        check_vma=False,
    )
```

profile of v0, /device:TPU:1, one launch (start us, length us, event | category | flops | bytes accessed | tf_op | source)
XLA Modules:
  0.0 226.6 jit_solution(6670356674611456764)
XLA Ops:
  7.2 0.0 copy-start
  7.2 2.5 %broadcast_in_dim.54 = bf16[32,32,1024]{2,1,0:T(8,128)(2,1)} broadcast(bf16[32,1024]{1,0:T(8,128)(2,1)} %param.20), dimensions={1,2} | broadcast | bytes 2162688 | tf_op jit(solution)/shard_map/broadcast_in_dim | solution.py:18
  9.7 0.0 copy-start.8
  9.7 0.0 copy-start.9
  9.7 0.0 copy-start.10
  9.7 0.0 copy-start.5
  9.7 0.0 copy-start.4
  9.7 0.0 copy-start.7
  9.7 10.6 %all-to-all-start = ((bf16[32,32,1024]{2,1,0:T(8,128)(2,1)}), bf16[32,32,1024]{2,1,0:T(8,128)(2,1)S(1)}, u32[]{:S(2)}, u32[]{:S(2)}) async-start(bf16[32,32,1024]{2,1,0:T(8,128)(2,1)} %broadcast_in_dim.54), calls=%async_computation | async-start | bytes 4194304 | tf_op jit(solution)/shard_map/all_to_all | solution.py:19
  20.3 0.0 reduce-scatter.3.cloned.1.call-start
  20.4 0.0 copy-done.8
  20.4 0.0 copy-done.9
  20.4 0.2 select_reduce_fusion
  20.6 0.0 copy-done.10
  20.6 0.1 iota_compare_fusion.4
  20.7 0.0 copy-done.5
  20.7 0.1 broadcast_select_fusion.1
  20.8 0.0 copy-done.4
  20.8 0.1 multiply_convert_fusion.2
  20.9 0.0 copy-done.7
  20.9 0.0 copy-start.2
  20.9 0.3 fusion.11
  21.2 0.4 copy-done.2
  21.6 2.0 convolution_convert_fusion
  23.6 45.6 %all-to-all-done = bf16[32,32,1024]{2,1,0:T(8,128)(2,1)S(1)} async-done(((bf16[32,32,1024]{2,1,0:T(8,128)(2,1)}), bf16[32,32,1024]{2,1,0:T(8,128)(2,1)S(1)}, u32[]{:S(2)}, u32[]{:S(2)}) %all-to-all-start) | async-done | bytes 2097184 | tf_op jit(solution)/shard_map/all_to_all | solution.py:19
  69.2 0.0 copy-start.3
  69.2 1.6 multiply_convert_fusion.1
  70.8 0.0 copy-start.1
  70.8 1.0 copy-done.1
  71.8 0.0 copy-done.3
  71.8 2.9 %fusion.19 = f32[1024,1024]{1,0:T(8,128)} fusion(bf16[256,1024]{1,0:T(8,128)(2,1)S(1)} %convolution_convert_fusion, f32[256,1024]{1,0:T(8,128)S(1)} %get-tuple-element.6, bf16[256,1024]{1,0:T(8,128)(2,1)S(1)} %copy-done.3), kind=kOutput, calls=%fused_computation.39 | convolution fusion | flops 539492352 | bytes 6291456 | tf_op jit(solution)/shard_map/dot_general | solution.py:100
  74.7 0.0 copy-start.6
  74.7 0.0 reduce-scatter.3.cloned.1.call-update
  74.7 0.0 reduce-scatter.5.cloned.1.call-start
  74.8 54.4 %reduce-scatter.3.cloned.1.call-done = f32[256,1024]{1,0:T(8,128)} async-done(((f32[1024,1024]{1,0:T(8,128)}), f32[256,1024]{1,0:T(8,128)}) %reduce-scatter.3.cloned.1.call-update) | async-done | bytes 1048592 | tf_op jit(solution)/shard_map/reduce_scatter | solution.py:29
  129.2 0.0 reduce-scatter.5.cloned.1.call-update
  129.2 0.0 all-gather.3.cloned.1.call-start
  129.3 38.9 %reduce-scatter.5.cloned.1.call-done = f32[32,1024]{1,0:T(8,128)} async-done(((f32[256,1024]{1,0:T(8,128)}), f32[32,1024]{1,0:T(8,128)}) %reduce-scatter.5.cloned.1.call-update) | async-done | bytes 131088 | tf_op jit(solution)/shard_map/reduce_scatter | solution.py:29
  168.2 0.0 all-gather.3.cloned.1.call-update
  168.2 0.0 copy-done.6
  168.3 0.1 copy.28
  168.4 0.1 copy.29
  168.5 0.1 reshape.90
  168.6 1.1 pad_maximum_fusion
  169.7 1.6 gather_fusion
  171.2 1.1 gather.7
  172.3 0.9 broadcast_select_fusion
  173.2 7.4 %all-to-all-start.1 = ((bf16[32,4,1024]{2,1,0:T(4,128)(2,1)}), bf16[32,4,1024]{2,1,0:T(4,128)(2,1)S(1)}, u32[]{:S(2)}, u32[]{:S(2)}) async-start(bf16[32,4,1024]{2,1,0:T(4,128)(2,1)} %broadcast_select_fusion), calls=%async_computation.3 | async-start | bytes 524288 | tf_op jit(solution)/shard_map/all_to_all | solution.py:77
  180.6 2.2 convolution_convert_fusion.1
  182.9 0.8 fusion.7
  183.7 0.8 all_to_all.20
  184.5 5.7 %all-to-all-done.1 = bf16[32,4,1024]{2,1,0:T(4,128)(2,1)S(1)} async-done(((bf16[32,4,1024]{2,1,0:T(4,128)(2,1)}), bf16[32,4,1024]{2,1,0:T(4,128)(2,1)S(1)}, u32[]{:S(2)}, u32[]{:S(2)}) %all-to-all-start.1) | async-done | bytes 262176 | tf_op jit(solution)/shard_map/all_to_all | solution.py:77
  190.3 4.5 %all-to-all-start.2 = ((bf16[32,4,1024]{2,1,0:T(4,128)(2,1)}), bf16[32,4,1024]{2,1,0:T(4,128)(2,1)S(1)}, u32[]{:S(2)}, u32[]{:S(2)}) async-start(bf16[32,4,1024]{2,1,0:T(4,128)(2,1)} %all_to_all.20), calls=%async_computation.4 | async-start | bytes 524288 | tf_op jit(solution)/shard_map/all_to_all | solution.py:112
  194.7 0.1 eq.48
  194.8 0.8 all_to_all.19
  195.6 0.0 copy-done
  195.6 1.1 fusion
  196.7 7.7 %all-to-all-done.2 = bf16[32,4,1024]{2,1,0:T(4,128)(2,1)S(1)} async-done(((bf16[32,4,1024]{2,1,0:T(4,128)(2,1)}), bf16[32,4,1024]{2,1,0:T(4,128)(2,1)S(1)}, u32[]{:S(2)}, u32[]{:S(2)}) %all-to-all-start.2) | async-done | bytes 262176 | tf_op jit(solution)/shard_map/all_to_all | solution.py:112
  204.4 0.8 all_to_all.22
  205.2 12.6 %all-gather.3.cloned.1.call-done = f32[512,1024]{1,0:T(8,128)} async-done(((f32[32,1024]{1,0:T(8,128)}), f32[512,1024]{1,0:T(8,128)}) %all-gather.3.cloned.1.call-update) | async-done | bytes 2097168 | tf_op jit(solution)/shard_map/all_gather | solution.py:34
  217.7 2.4 %reduce_sum.19 = f32[32,1024]{1,0:T(8,128)} reduce(f32[16,32,1024]{2,1,0:T(8,128)} %bitcast.23, f32[]{:T(128)} %constant.8.clone.1), dimensions={0}, to_apply=%region_3.4 | reduce | flops 491520 | bytes 2228228 | tf_op jit(solution)/shard_map/reduce_sum | solution.py:34
  (4 shorter events, 0.0 us)
Async XLA Ops:
  7.2 188.5 %copy-start = (bf16[128,1024]{1,0:T(8,128)(2,1)S(1)}, bf16[128,1024]{1,0:T(8,128)(2,1)}, u32[]{:S(2)}) copy-start(bf16[128,1024]{1,0:T(8,128)(2,1)} %param.22) | copy-start | bytes 786436
  9.7 10.7 %copy-start.8 = (f32[256]{0:T(256)S(1)}, f32[256]{0:T(256)}, u32[]{:S(2)}) copy-start(f32[256]{0:T(256)} %param.15) | copy-start | bytes 3076
  9.7 10.7 %copy-start.9 = (s32[128]{0:T(128)S(1)}, s32[128]{0:T(128)}, u32[]{:S(2)}) copy-start(s32[128]{0:T(128)} %param.14) | copy-start | bytes 1540
  9.7 10.9 %copy-start.10 = (s32[2]{0:T(128)S(1)}, s32[2]{0:T(128)}, u32[]{:S(2)}) copy-start(s32[2]{0:T(128)} %param.18) | copy-start | bytes 28
  9.7 11.0 %copy-start.5 = (bf16[2,3,128,128]{3,2,1,0:T(8,128)(2,1)S(1)}, bf16[2,3,128,128]{3,2,1,0:T(8,128)(2,1)}, u32[]{:S(2)}) copy-start(bf16[2,3,128,128]{3,2,1,0:T(8,128)(2,1)} %param.19) | copy-start | bytes 589828
  9.7 11.1 %copy-start.4 = (bf16[128,1024]{1,0:T(8,128)(2,1)S(1)}, bf16[128,1024]{1,0:T(8,128)(2,1)}, u32[]{:S(2)}) copy-start(bf16[128,1024]{1,0:T(8,128)(2,1)} %param.13) | copy-start | bytes 786436
  9.7 11.2 %copy-start.7 = (s32[2,3]{1,0:T(2,128)S(1)}, s32[2,3]{1,0:T(2,128)}, u32[]{:S(2)}) copy-start(s32[2,3]{1,0:T(2,128)} %param.17) | copy-start | bytes 76
  9.7 59.5 %all-to-all-start = ((bf16[32,32,1024]{2,1,0:T(8,128)(2,1)}), bf16[32,32,1024]{2,1,0:T(8,128)(2,1)S(1)}, u32[]{:S(2)}, u32[]{:S(2)}) async-start(bf16[32,32,1024]{2,1,0:T(8,128)(2,1)} %broadcast_in_dim.54), calls=%async_computation | async-start | bytes 4194304 | tf_op jit(solution)/shard_map/all_to_all | solution.py:19
  20.3 108.9 %reduce-scatter.3.cloned.1.call-start = ((), (), s32[]{:S(2)}) async-start(), calls=%async_computation.5 | async-start | bytes 5242880 | tf_op jit(solution)/shard_map/reduce_scatter | solution.py:29
  20.9 0.7 copy-start.2
  69.2 2.6 %copy-start.3 = (bf16[256,1024]{1,0:T(8,128)(2,1)S(1)}, bf16[256,1024]{1,0:T(8,128)(2,1)}, u32[]{:S(2)}) copy-start(bf16[256,1024]{1,0:T(8,128)(2,1)} %param.21) | copy-start | bytes 1572868
  70.8 1.0 copy-start.1
  74.7 93.6 %copy-start.6 = (s32[32,4]{0,1:T(4,128)S(1)}, s32[32,4]{0,1:T(4,128)}, u32[]{:S(2)}) copy-start(s32[32,4]{0,1:T(4,128)} %param.23) | copy-start | bytes 1540
  74.7 93.5 %reduce-scatter.5.cloned.1.call-start = ((), (), s32[]{:S(2)}) async-start(), calls=%async_computation.6 | async-start | bytes 1179648 | tf_op jit(solution)/shard_map/reduce_scatter | solution.py:29
  129.2 88.5 %all-gather.3.cloned.1.call-start = ((), (), s32[]{:S(2)}) async-start(), calls=%async_computation.7 | async-start | bytes 2228224 | tf_op jit(solution)/shard_map/all_gather | solution.py:34
  173.2 17.1 %all-to-all-start.1 = ((bf16[32,4,1024]{2,1,0:T(4,128)(2,1)}), bf16[32,4,1024]{2,1,0:T(4,128)(2,1)S(1)}, u32[]{:S(2)}, u32[]{:S(2)}) async-start(bf16[32,4,1024]{2,1,0:T(4,128)(2,1)} %broadcast_select_fusion), calls=%async_computation.3 | async-start | bytes 524288 | tf_op jit(solution)/shard_map/all_to_all | solution.py:77
  190.3 14.1 %all-to-all-start.2 = ((bf16[32,4,1024]{2,1,0:T(4,128)(2,1)}), bf16[32,4,1024]{2,1,0:T(4,128)(2,1)S(1)}, u32[]{:S(2)}, u32[]{:S(2)}) async-start(bf16[32,4,1024]{2,1,0:T(4,128)(2,1)} %all_to_all.20), calls=%async_computation.4 | async-start | bytes 524288 | tf_op jit(solution)/shard_map/all_to_all | solution.py:112
Sparse Core Ops, SparseCore 0:
  74.8 54.3 reduce-scatter.2
  132.0 36.1 reduce-scatter.4
  170.3 47.3 all-gather.2
where the time goes:
time: 227 us
  waiting for transfers between devices  165 us (73%)
  starting transfers between devices  22.6 us (10%)
  between operations  13.9 us (6%)
  matrix products  10.9 us (5%)
  local copies, waits for them, and re-layouts  9.29 us (4%)
  other arithmetic  4.8 us (2%)
    reduce_scatter x2, waiting for transfers between devices, sum_by_axis(): nearer = lax.psum_scatter(shard, axes[0], scatter_dimension=dim, tiled=True)  93.4 us
    all_to_all x1, waiting for transfers between devices, copy_for_each(): return lax.all_to_all(copies, axis, split_axis=0, concat_axis=0, tiled=True)  45.6 us
    all_gather x1, waiting for transfers between devices, gathered_total(): return lax.all_gather(shard, axis).sum(0)  12.6 us
    all_to_all x1, starting transfers between devices, copy_for_each(): return lax.all_to_all(copies, axis, split_axis=0, concat_axis=0, tiled=True)  10.6 us
    all_to_all x1, waiting for transfers between devices, local(): lax.all_to_all(bound_grad, DOM, split_axis=0, concat_axis=0, tiled=True)  7.69 us
    all_to_all x1, starting transfers between devices, local(): lax.all_to_all(outgoing, DOM, split_axis=0, concat_axis=0, tiled=True)  7.42 us
    all_to_all x1, waiting for transfers between devices, local(): lax.all_to_all(outgoing, DOM, split_axis=0, concat_axis=0, tiled=True)  5.73 us
  transfers between devices with their start and end apart: 6, of which 6 were waited for; matrix products, arithmetic and copies ran while one was open for 5% of the time, Pallas kernels for 0%

commit v1 on v0

v1 whole, which is shorter than its diff:
```python
import jax
import jax.numpy as jnp
from jax import lax
from jax.sharding import Mesh
from jax.sharding import PartitionSpec as P

AXES = ("z", "core", "dx", "dy")
DOM = ("dx", "dy")
SWAP = [(0, 1), (1, 0)]


def dequantize(cold_codes, scale_index, scale_table):
    levels = jnp.arange(scale_table.shape[0], dtype=jnp.int32)
    lookup = jnp.sum(
        jnp.where(scale_index[:, None] == levels[None, :], scale_table[None, :], 0.0), axis=1
    )
    return (cold_codes.astype(jnp.float32) * lookup[:, None]).astype(jnp.bfloat16)


def silu_parts(preact):
    logistic = jax.nn.sigmoid(preact)
    return (preact * logistic, logistic * (1.0 + preact * (1.0 - logistic)))


def dot(a, b, ca, cb):
    return lax.dot_general(a, b, (((ca,), (cb,)), ((), ())), preferred_element_type=jnp.float32)


def fold_index(peers, slots):
    row = jnp.arange(peers * 2 * slots, dtype=jnp.int32)
    peer, half, slot = row // (2 * slots), (row // slots) % 2, row % slots
    return peer * slots + slot, half


def unfold(folded, peers, slots):
    source, half = fold_index(peers, slots)
    flat = folded.reshape(peers * 2 * slots, -1)
    want = jnp.arange(peers * slots, dtype=jnp.int32)[:, None] == source[None, :]
    parts = [
        dot((want & (half == h)[None, :]).astype(jnp.bfloat16), flat, 1, 0).astype(jnp.bfloat16)
        for h in (0, 1)
    ]
    return jnp.concatenate(parts, axis=1)


def pick_half(both, half, width):
    return jnp.where((half == 0)[:, None], both[:, :width], both[:, width:])


def local(
    hot_rows,
    cold_codes,
    scale_index,
    scale_table,
    stale_rows,
    tile_index,
    tile_count,
    tile_values,
    weight,
    out_grad,
    stale_grads,
    send_rows,
):
    core = lax.axis_index("core")
    first = core == 0
    tile_slots = tile_values.shape[1]
    cluster_rows = tile_values.shape[2]
    peers, slots = send_rows.shape
    width = weight.shape[1]
    half_w = width // 2
    block = weight.shape[0]

    local_rows = jnp.concatenate(
        [hot_rows, dequantize(cold_codes, scale_index, scale_table)], axis=0
    )
    row_count = local_rows.shape[0]
    sends = send_rows.reshape(-1)
    slot_of, half_of = fold_index(peers, slots)
    folded_sends = jnp.broadcast_to(send_rows[:, None, :], (peers, 2, slots)).reshape(-1)
    picker = (folded_sends[:, None] == jnp.arange(row_count, dtype=jnp.int32)[None, :]).astype(
        jnp.bfloat16
    )
    outgoing = pick_half(dot(picker, local_rows, 1, 0), half_of, half_w).astype(jnp.bfloat16)
    outgoing = outgoing.reshape(peers, 2 * slots, half_w)

    my_half = jnp.where(first, weight[:, :half_w], weight[:, half_w:])
    send_w = jnp.concatenate(
        [jnp.broadcast_to(my_half[None], (peers, block, half_w)), outgoing], axis=1
    )
    got_w = lax.all_to_all(send_w, DOM, split_axis=0, concat_axis=0, tiled=True)
    w_own = got_w[:, :block].reshape(peers * block, half_w)
    next_rows = unfold(got_w[:, block:], peers, slots)
    w_oth = lax.ppermute(w_own, "core", SWAP)

    source = jnp.concatenate([local_rows, stale_rows], axis=0)
    src_count = source.shape[0] // cluster_rows
    live_mask = jnp.arange(tile_slots, dtype=jnp.int32)[None, :] < tile_count[:, None]
    masked = jnp.where(live_mask[:, :, None, None], tile_values, jnp.zeros_like(tile_values))
    selector = tile_index[:, :, None] == jnp.arange(src_count, dtype=jnp.int32)[None, None, :]
    operator = jnp.sum(
        jnp.where(
            selector[:, :, None, :, None], masked[:, :, :, None, :].astype(jnp.float32), 0.0
        ),
        axis=1,
    )
    operator = operator.reshape(row_count, src_count * cluster_rows)
    hidden = jnp.dot(operator, source.astype(jnp.float32), precision=lax.Precision.HIGHEST)
    hidden = hidden.astype(jnp.bfloat16)

    og = (out_grad[:, :half_w], out_grad[:, half_w:])
    acts, grads = [], []
    for w, flip in ((w_own, False), (w_oth, True)):
        preact = dot(hidden, w, 1, 0)
        activ, slope = silu_parts(preact)
        acts.append(activ.astype(jnp.bfloat16))
        grad = jnp.where(first != flip, og[0], og[1]).astype(jnp.float32)
        grads.append((grad * slope).astype(jnp.bfloat16))
    activations = jnp.concatenate(
        [jnp.where(first, acts[0], acts[1]), jnp.where(first, acts[1], acts[0])], axis=1
    )

    part_oth = dot(hidden, grads[1], 0, 0).astype(jnp.bfloat16)
    part_in = lax.ppermute(part_oth, "core", SWAP)
    part = (dot(hidden, grads[0], 0, 0) + part_in.astype(jnp.float32)).astype(jnp.bfloat16)

    hid_grad = dot(grads[0], w_own, 1, 1) + dot(grads[1], w_oth, 1, 1)
    hid_grad = hid_grad.astype(jnp.bfloat16)
    src_grad = lax.dot_general(
        operator,
        hid_grad.astype(jnp.float32),
        (((0,), (0,)), ((), ())),
        precision=lax.Precision.HIGHEST,
    )
    bound_grad = src_grad[row_count:].astype(jnp.bfloat16)
    folder = (
        slot_of[:, None] == jnp.arange(peers * slots, dtype=jnp.int32)[None, :]
    ).astype(jnp.bfloat16)
    back = pick_half(dot(folder, bound_grad, 1, 0), half_of, half_w).astype(jnp.bfloat16)
    send_p = jnp.concatenate(
        [part.reshape(peers, block, half_w), back.reshape(peers, 2 * slots, half_w)], axis=1
    )
    got_p = lax.all_to_all(send_p, DOM, split_axis=0, concat_axis=0, tiled=True)
    next_grads = unfold(got_p[:, block:], peers, slots)
    plane = jnp.sum(got_p[:, :block].astype(jnp.float32), axis=0).astype(jnp.bfloat16)
    planes = lax.axis_size("z")
    stack = lax.all_to_all(
        jnp.broadcast_to(plane[None], (planes, *plane.shape)), "z", 0, 0, tiled=True
    )
    total = jnp.sum(stack.astype(jnp.float32), axis=0)
    other = lax.ppermute(total, "core", SWAP)
    weight_grad = jnp.concatenate(
        [jnp.where(first, total, other), jnp.where(first, other, total)], axis=1
    )

    placing = (jnp.arange(row_count, dtype=jnp.int32)[:, None] == sends[None, :]).astype(
        jnp.bfloat16
    )
    returned = dot(placing, stale_grads, 1, 0)
    feature_grad = (src_grad[:row_count] + returned).astype(jnp.bfloat16)
    return (activations, feature_grad, weight_grad, next_rows, next_grads)


def solution(mesh):
    shape = (mesh.shape["group"] // 2, 2, 4, mesh.shape["dom"] // 4)
    torus = Mesh(mesh.devices.reshape(shape), AXES)
    rows = P(AXES, None)
    placed = (
        rows,
        rows,
        P(AXES),
        P(),
        rows,
        rows,
        P(AXES),
        P(AXES, None, None, None),
        P(DOM, None),
        rows,
        rows,
        rows,
    )
    return jax.shard_map(
        local,
        mesh=torus,
        in_specs=placed,
        out_specs=(rows, rows, P(DOM, None), rows, rows),
        check_vma=False,
    )
```

time: 227 us -> 135 us (0.59)
  waiting for transfers between devices: 165 us -> 35.8 us
  blocking collectives: 0 us -> 42.8 us
  between operations: 13.9 us -> 1.03 us
  local copies, waits for them, and re-layouts: 9.29 us -> 2.26 us
  starting transfers between devices: 22.6 us -> 28.5 us
  other arithmetic: 4.8 us -> 9.44 us
  matrix products: 10.9 us -> 14.5 us
    reduce_scatter x2 -> x0, waiting for transfers between devices: 93.4 us -> none  [sum_by_axis(): nearer = lax.psum_scatter(shard, axes[0], scatter_dimension=dim, tiled=True)]
    all_to_all x0 -> x1, blocking collectives: none -> 42.8 us  [local(): got_w = lax.all_to_all(send_w, DOM, split_axis=0, concat_axis=0, tiled=True)]
    all_to_all x3 -> x2, waiting for transfers between devices: 59 us -> 35.6 us  [the longest x1 28.4 us: local(): got_p = lax.all_to_all(send_p, DOM, split_axis=0, concat_axis=0, tiled=True)]
    ppermute x0 -> x3, starting transfers between devices: none -> 13.7 us  [the longest x1 6.44 us: local(): other = lax.ppermute(total, 'core', SWAP)]
    all_gather x1 -> x0, waiting for transfers between devices: 12.6 us -> none  [gathered_total(): return lax.all_gather(shard, axis).sum(0)]
    all_to_all x3 -> x2, starting transfers between devices: 22.5 us -> 14.8 us  [the longest x1 10 us: local(): lax.all_to_all(jnp.broadcast_to(plane[None], (planes, *plane.shape)), 'z'...]
    dot_general x5 -> x13, matrix products: 8.09 us -> 11.6 us  [dot(): lax.dot_general(a, b, (((ca,), (cb,)), ((), ())), preferred_element_type=...]
    concatenate x1 -> x6, other arithmetic: 1.07 us -> 4.28 us  [the longest x2 1.46 us: unfold(): return jnp.concatenate(parts, axis=1)]
  transfers between devices with their start and end apart: 6 -> 5, of which waited for: 6 -> 3; matrix products, arithmetic and copies ran while one was open for 5% -> 9% of each run, Pallas kernels for 0% -> 0%
where the time goes in v1:
time: 135 us; the launch traced here: 134 us
  blocking collectives  42.8 us (32%)
  waiting for transfers between devices  35.8 us (27%)
  starting transfers between devices  28.5 us (21%)
  matrix products  14.5 us (11%)
  other arithmetic  9.44 us (7%)
  local copies, waits for them, and re-layouts  2.26 us (2%)
    all_to_all x1, blocking collectives, local(): got_w = lax.all_to_all(send_w, DOM, split_axis=0, concat_axis=0, tiled=True)  42.8 us
    all_to_all x1, waiting for transfers between devices, local(): got_p = lax.all_to_all(send_p, DOM, split_axis=0, concat_axis=0, tiled=True)  28.4 us
    dot_general x13, matrix products, dot(): lax.dot_general(a, b, (((ca,), (cb,)), ((), ())), preferred_element_type=...  11.6 us
    all_to_all x1, starting transfers between devices, local(): lax.all_to_all(jnp.broadcast_to(plane[None], (planes, *plane.shape)), 'z'...  10 us
    all_to_all x1, waiting for transfers between devices, local(): lax.all_to_all(jnp.broadcast_to(plane[None], (planes, *plane.shape)), 'z'...  7.23 us
    ppermute x1, starting transfers between devices, local(): other = lax.ppermute(total, 'core', SWAP)  6.44 us
    ppermute x1, starting transfers between devices, local(): w_oth = lax.ppermute(w_own, 'core', SWAP)  5.3 us
    all_to_all x1, starting transfers between devices, local(): got_p = lax.all_to_all(send_p, DOM, split_axis=0, concat_axis=0, tiled=True)  4.81 us
  transfers between devices with their start and end apart: 5, of which 3 were waited for; matrix products, arithmetic and copies ran while one was open for 9% of the time, Pallas kernels for 0%

profile of v1, /device:TPU:1, one launch (start us, length us, event | category | flops | bytes accessed | tf_op | source)
XLA Modules:
  0.0 134.3 jit_solution(6192820330193045600)
XLA Ops:
  0.6 0.0 copy-start
  0.7 0.0 copy-start.6
  0.7 0.8 copy.22
  1.5 0.1 eq.159
  1.6 0.9 select_reduce_fusion.1
  2.5 0.8 slice_select_fusion.2
  3.3 1.1 multiply_convert_fusion.4
  4.3 0.0 copy-start.2
  4.3 1.4 %fusion.9 = bf16[256,1024]{1,0:T(8,128)(2,1)S(1)} fusion(bf16[128,1024]{1,0:T(8,128)(2,1)S(1)} %multiply_convert_fusion.4, bf16[128,1024]{1,0:T(8,128)(2,1)} %param.12, s32[256]{0:T(256)S(1)} %eq.159), kind=kOutput, calls=%fused_computation.25 | convolution fusion | flops 135331840 | bytes 1049600 | tf_op jit(solution)/shard_map/dot_general | solution.py:26
  5.7 0.1 fusion.18
  5.8 0.0 copy-done.6
  5.9 0.0 copy-done.2
  5.9 0.1 broadcast_in_dim.68
  6.0 0.1 pad_maximum_fusion
  6.1 42.8 %all_to_all.15 = bf16[32,40,512]{2,1,0:T(8,128)(2,1)S(1)} all-to-all(bf16[32,40,512]{2,1,0:T(8,128)(2,1)S(1)} %pad_maximum_fusion), channel_id=1, replica_groups=mesh['z'=8,'core'=2,'dx'=4,'dy'=8] {'dx','dy'}, dimensions={0} | all-to-all | bytes 2621440 | tf_op jit(solution)/shard_map/all_to_all | solution.py:90
  48.9 0.1 slice.59
  49.1 5.3 %collective-permute-start = (bf16[1024,512]{1,0:T(8,128)(2,1)S(1)}, bf16[1024,512]{1,0:T(8,128)(2,1)}, u32[]{:S(2)}, u32[]{:S(2)}) collective-permute-start(bf16[1024,512]{1,0:T(8,128)(2,1)S(1)} %bitcast.37), channel_id=1, source_target_pairs={{0,32},{32,0},{1,33},{33,1},{2,34},{34,2},{3,35},{35,3},{4,36},{36... | collective-permute-start | bytes 3145736 | tf_op jit(solution)/shard_map/ppermute | solution.py:93
  54.4 0.0 copy-done.12
  54.4 0.1 iota_compare_fusion.9
  54.4 0.0 copy-done.11
  54.4 0.1 iota_compare_fusion.8
  54.5 0.0 copy-done.5
  54.5 0.1 select_convert_fusion
  54.6 0.1 select_reduce_fusion
  54.8 0.2 copy.21
  55.0 0.0 copy-start.9
  55.0 2.1 %convolution_convert_fusion.1 = bf16[256,1024]{1,0:T(8,128)(2,1)S(1)} fusion(bf16[128,1024]{1,0:T(8,128)(2,1)} %param.16, bf16[128,1024]{1,0:T(8,128)(2,1)} %copy-done.2, bf16[128,1024]{1,0:T(8,128)(2,1)} %param.12, f32[48,8,2,128]{3,2,1,0:T(2,128)S(1)} %bitcast.41), kind=kOutput, calls=%fused_computation.6 | convolution fusion | flops 1210580992 | bytes 1703936 | tf_op jit(solution)/shard_map/dot_general | solution.py:107
  57.1 0.0 collective-permute-done
  57.2 1.7 %fusion.46 = f32[256,512]{1,0:T(8,128)S(1)} fusion(bf16[256,1024]{1,0:T(8,128)(2,1)S(1)} %convolution_convert_fusion.1, bf16[1024,512]{1,0:T(8,128)(2,1)} %collective-permute-done), kind=kOutput, calls=%fused_computation.99 | convolution fusion | flops 268435456 | bytes 2097152 | tf_op jit(solution)/shard_map/dot_general | solution.py:26
  58.8 0.0 copy-start.1
  58.8 1.4 %broadcast_select_fusion.1 = (bf16[256,512]{1,0:T(8,128)(2,1)}, bf16[256,512]{1,0:T(8,128)(2,1)}, f32[256,512]{1,0:T(8,128)S(1)}) fusion(pred[]{:T(512)S(6)} %eq.151, f32[256,512]{1,0:T(8,128)S(1)} %fusion.46, bf16[256,1024]{1,0:T(8,128)(2,1)S(1)} %convolution_convert_fusion.1, bf16[1024,512]{1,0:T(8,128)(2,1)S(1)} %bitcast.38), kind=kOutput, calls=%fused_computation.52 | convolution fusion | flops 270008320 | bytes 3145729 | tf_op jit(solution)/shard_map/dot_general | solution.py:26
  60.2 0.0 copy-done.1
  60.2 0.4 multiply_convert_fusion
  60.7 0.5 fusion.47
  61.1 0.5 convolution_convert_fusion
  61.6 1.9 %collective-permute-start.1 = (bf16[1024,512]{1,0:T(8,128)(2,1)S(1)}, bf16[1024,512]{1,0:T(8,128)(2,1)S(1)}, u32[]{:S(2)}, u32[]{:S(2)}) collective-permute-start(bf16[1024,512]{1,0:T(8,128)(2,1)S(1)} %convolution_convert_fusion), channel_id=1, source_target_pairs={{0,32},{32,0},{1,33},{33,1},{2,34},{34,2},{3,35},{35,3},{4,36},{36... | collective-permute-start | bytes 3145736 | tf_op jit(solution)/shard_map/ppermute | solution.py:123
  63.5 1.7 %fusion = bf16[256,1024]{1,0:T(8,128)(2,1)S(1)} fusion(f32[256,1024]{1,0:T(8,128)S(1)} %fusion.47, bf16[256,512]{1,0:T(8,128)(2,1)S(1)} %get-tuple-element.7, bf16[1024,512]{1,0:T(8,128)(2,1)} %collective-permute-done), kind=kOutput, calls=%fused_computation.7 | convolution fusion | flops 268959744 | bytes 2883584 | tf_op jit(solution)/shard_map/dot_general | solution.py:26
  65.2 0.0 copy-start.7
  65.3 0.8 fusion.13
  66.1 0.3 fusion.19
  66.4 0.1 fusion.20
  66.5 0.0 collective-permute-done.1
  66.5 0.5 add_convert_fusion
  67.0 1.2 pad_maximum_fusion.1
  68.2 4.8 %all-to-all-start.1 = ((bf16[32,40,512]{2,1,0:T(8,128)(2,1)}), bf16[32,40,512]{2,1,0:T(8,128)(2,1)}, u32[]{:S(2)}, u32[]{:S(2)}) async-start(bf16[32,40,512]{2,1,0:T(8,128)(2,1)} %pad_maximum_fusion.1), calls=%async_computation.1 | async-start | bytes 2621440 | tf_op jit(solution)/shard_map/all_to_all | solution.py:142
  73.0 0.0 copy-start.3
  73.0 0.1 eq.164
  73.1 0.0 copy-start.4
  73.2 0.2 convolution_convert_fusion.5
  73.4 0.2 convolution_convert_fusion.4
  73.5 0.7 pad_maximum_fusion.3
  74.3 0.9 pad_maximum_fusion.2
  75.2 1.1 fusion.1
  76.2 28.4 %all-to-all-done.1 = bf16[32,40,512]{2,1,0:T(8,128)(2,1)} async-done(((bf16[32,40,512]{2,1,0:T(8,128)(2,1)}), bf16[32,40,512]{2,1,0:T(8,128)(2,1)}, u32[]{:S(2)}, u32[]{:S(2)}) %all-to-all-start.1) | async-done | bytes 1310752 | tf_op jit(solution)/shard_map/all_to_all | solution.py:142
  104.6 1.4 %slice_reduce_fusion = bf16[32,512]{1,0:T(8,128)(2,1)S(1)} fusion(bf16[32,40,512]{2,1,0:T(8,128)(2,1)} %all-to-all-done.1), kind=kLoop, calls=%fused_computation.14 | loop fusion | flops 507904 | bytes 1081344 | tf_op jit(solution)/shard_map/reduce_sum | solution.py:144
  106.0 0.7 broadcast_in_dim.71
  106.8 10.0 %all-to-all-start.2 = ((bf16[8,32,512]{2,1,0:T(8,128)(2,1)}), bf16[8,32,512]{2,1,0:T(8,128)(2,1)S(1)}, u32[]{:S(2)}, u32[]{:S(2)}) async-start(bf16[8,32,512]{2,1,0:T(8,128)(2,1)} %broadcast_in_dim.71), calls=%async_computation.2 | async-start | bytes 524288 | tf_op jit(solution)/shard_map/all_to_all | solution.py:146
  116.8 1.1 convolution_convert_fusion.2
  117.9 1.1 convolution_convert_fusion.3
  119.1 7.2 %all-to-all-done.2 = bf16[8,32,512]{2,1,0:T(8,128)(2,1)S(1)} async-done(((bf16[8,32,512]{2,1,0:T(8,128)(2,1)}), bf16[8,32,512]{2,1,0:T(8,128)(2,1)S(1)}, u32[]{:S(2)}, u32[]{:S(2)}) %all-to-all-start.2) | async-done | bytes 262176 | tf_op jit(solution)/shard_map/all_to_all | solution.py:146
  126.3 6.4 %collective-permute-start.2 = (f32[32,512]{1,0:T(8,128)S(1)}, f32[32,512]{1,0:T(8,128)S(1)}, u32[]{:S(2)}, u32[]{:S(2)}) collective-permute-start(f32[32,512]{1,0:T(8,128)S(1)} %convert_reduce_fusion), channel_id=1, source_target_pairs={{0,32},{32,0},{1,33},{33,1},{2,34},{34,2},{3,35},{35,3},{4,36},{36... | collective-permute-start | bytes 196616 | tf_op jit(solution)/shard_map/ppermute | solution.py:150
  132.8 0.7 pad_maximum_fusion.4
  133.5 0.1 collective-permute-done.2
  133.7 0.7 pad_maximum_fusion.5
  (18 shorter events, 0.1 us)
Async XLA Ops:
  0.6 74.5 %copy-start = (bf16[128,1024]{1,0:T(8,128)(2,1)S(1)}, bf16[128,1024]{1,0:T(8,128)(2,1)}, u32[]{:S(2)}) copy-start(bf16[128,1024]{1,0:T(8,128)(2,1)} %param.22) | copy-start | bytes 786436
  0.7 5.2 %copy-start.6 = (pred[256]{0:T(512)(128)(4,1)}, pred[256]{0:T(512)(128)(4,1)S(1)}, u32[]{:S(2)}) copy-start(pred[256]{0:T(512)(128)(4,1)S(1)} %broadcast_compare_fusion) | copy-start | bytes 772
  4.3 1.5 %copy-start.2 = (bf16[128,1024]{1,0:T(8,128)(2,1)}, bf16[128,1024]{1,0:T(8,128)(2,1)S(1)}, u32[]{:S(2)}) copy-start(bf16[128,1024]{1,0:T(8,128)(2,1)S(1)} %multiply_convert_fusion.4) | copy-start | bytes 786436
  48.9 5.4 %copy-start.12 = (s32[2]{0:T(128)S(1)}, s32[2]{0:T(128)}, u32[]{:S(2)}) copy-start(s32[2]{0:T(128)} %param.18) | copy-start | bytes 28
  48.9 5.5 %copy-start.11 = (s32[2,3]{1,0:T(2,128)S(1)}, s32[2,3]{1,0:T(2,128)}, u32[]{:S(2)}) copy-start(s32[2,3]{1,0:T(2,128)} %param.17) | copy-start | bytes 76
  48.9 5.6 %copy-start.5 = (bf16[2,3,128,128]{3,2,1,0:T(8,128)(2,1)S(1)}, bf16[2,3,128,128]{3,2,1,0:T(8,128)(2,1)}, u32[]{:S(2)}) copy-start(bf16[2,3,128,128]{3,2,1,0:T(8,128)(2,1)} %param.19) | copy-start | bytes 589828
  49.1 8.1 %collective-permute-start = (bf16[1024,512]{1,0:T(8,128)(2,1)S(1)}, bf16[1024,512]{1,0:T(8,128)(2,1)}, u32[]{:S(2)}, u32[]{:S(2)}) collective-permute-start(bf16[1024,512]{1,0:T(8,128)(2,1)S(1)} %bitcast.37), channel_id=1, source_target_pairs={{0,32},{32,0},{1,33},{33,1},{2,34},{34,2},{3,35},{35,3},{4,36},{36... | collective-permute-start | bytes 3145736 | tf_op jit(solution)/shard_map/ppermute | solution.py:93
  55.0 11.1 %copy-start.9 = (s32[256]{0:T(256)}, s32[256]{0:T(256)S(1)}, u32[]{:S(2)}) copy-start(s32[256]{0:T(256)S(1)} %fusion.40) | copy-start | bytes 3076
  58.8 1.4 %copy-start.1 = (bf16[256,1024]{1,0:T(8,128)(2,1)S(1)}, bf16[256,1024]{1,0:T(8,128)(2,1)}, u32[]{:S(2)}) copy-start(bf16[256,1024]{1,0:T(8,128)(2,1)} %param.21) | copy-start | bytes 1572868
  61.6 4.9 %collective-permute-start.1 = (bf16[1024,512]{1,0:T(8,128)(2,1)S(1)}, bf16[1024,512]{1,0:T(8,128)(2,1)S(1)}, u32[]{:S(2)}, u32[]{:S(2)}) collective-permute-start(bf16[1024,512]{1,0:T(8,128)(2,1)S(1)} %convolution_convert_fusion), channel_id=1, source_target_pairs={{0,32},{32,0},{1,33},{33,1},{2,34},{34,2},{3,35},{35,3},{4,36},{36... | collective-permute-start | bytes 3145736 | tf_op jit(solution)/shard_map/ppermute | solution.py:123
  65.2 1.2 copy-start.7
  68.2 5.0 %copy-start.8 = (pred[256]{0:T(512)(128)(4,1)S(1)}, pred[256]{0:T(512)(128)(4,1)}, u32[]{:S(2)}) copy-start(pred[256]{0:T(512)(128)(4,1)} %copy-done.6) | copy-start | bytes 772
  68.2 5.0 %copy-start.10 = (s32[256]{0:T(256)S(1)}, s32[256]{0:T(256)}, u32[]{:S(2)}) copy-start(s32[256]{0:T(256)} %copy-done.9) | copy-start | bytes 3076
  68.2 36.5 %all-to-all-start.1 = ((bf16[32,40,512]{2,1,0:T(8,128)(2,1)}), bf16[32,40,512]{2,1,0:T(8,128)(2,1)}, u32[]{:S(2)}, u32[]{:S(2)}) async-start(bf16[32,40,512]{2,1,0:T(8,128)(2,1)} %pad_maximum_fusion.1), calls=%async_computation.1 | async-start | bytes 2621440 | tf_op jit(solution)/shard_map/all_to_all | solution.py:142
  73.0 1.3 copy-start.3
  73.1 1.2 copy-start.4
  106.8 19.5 %all-to-all-start.2 = ((bf16[8,32,512]{2,1,0:T(8,128)(2,1)}), bf16[8,32,512]{2,1,0:T(8,128)(2,1)S(1)}, u32[]{:S(2)}, u32[]{:S(2)}) async-start(bf16[8,32,512]{2,1,0:T(8,128)(2,1)} %broadcast_in_dim.71), calls=%async_computation.2 | async-start | bytes 524288 | tf_op jit(solution)/shard_map/all_to_all | solution.py:146
  126.3 7.3 %collective-permute-start.2 = (f32[32,512]{1,0:T(8,128)S(1)}, f32[32,512]{1,0:T(8,128)S(1)}, u32[]{:S(2)}, u32[]{:S(2)}) collective-permute-start(f32[32,512]{1,0:T(8,128)S(1)} %convert_reduce_fusion), channel_id=1, source_target_pairs={{0,32},{32,0},{1,33},{33,1},{2,34},{34,2},{3,35},{35,3},{4,36},{36... | collective-permute-start | bytes 196616 | tf_op jit(solution)/shard_map/ppermute | solution.py:150

commit v2 on v1

v2 whole, which is shorter than its diff:
```python
import jax
import jax.numpy as jnp
from jax import lax
from jax.experimental import pallas as pl
from jax.sharding import Mesh
from jax.sharding import PartitionSpec as P


AXES = ("z", "core", "dx", "dy")
DOM = ("dx", "dy")
SWAP = [(0, 1), (1, 0)]
BF = jnp.bfloat16


def dequantize(cold_codes, scale_index, scale_table):
    levels = jnp.arange(scale_table.shape[0], dtype=jnp.int32)
    lookup = jnp.sum(
        jnp.where(scale_index[:, None] == levels[None, :], scale_table[None, :], 0.0), axis=1
    )
    return (cold_codes.astype(jnp.float32) * lookup[:, None]).astype(BF)


def silu_parts(preact):
    logistic = jax.nn.sigmoid(preact)
    return (preact * logistic, logistic * (1.0 + preact * (1.0 - logistic)))


def dot(a, b, ca, cb):
    return lax.dot_general(a, b, (((ca,), (cb,)), ((), ())), preferred_element_type=jnp.float32)


def swap_core(value):
    return lax.ppermute(value, "core", SWAP)


def halves(array, first):
    width = array.shape[1] // 2
    low, high = array[:, :width], array[:, width:]
    return jnp.where(first, low, high), jnp.where(first, high, low)


def ordered(mine, other, first):
    return jnp.concatenate(
        [jnp.where(first, mine, other), jnp.where(first, other, mine)], axis=1
    )


def core_products(hidden, hidden_peer, grad, grad_peer, w):
    rows, width = grad.shape
    depth = hidden.shape[1]

    def body(h_ref, hp_ref, g_ref, gp_ref, w_ref, act_ref, actp_ref, pre_ref, prep_ref, part_ref):
        w_all = w_ref[...]
        for h, g, a, p in (
            (h_ref, g_ref, act_ref, pre_ref),
            (hp_ref, gp_ref, actp_ref, prep_ref),
        ):
            activ, slope = silu_parts(dot(h[...], w_all, 1, 0))
            a[...] = activ.astype(BF)
            p[...] = (g[...].astype(jnp.float32) * slope).astype(BF)
        part_ref[...] = (
            dot(h_ref[...], pre_ref[...], 0, 0) + dot(hp_ref[...], prep_ref[...], 0, 0)
        ).astype(BF)

    small = jax.ShapeDtypeStruct((rows, width), BF)
    return pl.pallas_call(
        body,
        out_shape=(small, small, small, small, jax.ShapeDtypeStruct((depth, width), BF)),
        cost_estimate=pl.CostEstimate(
            flops=8 * rows * depth * width, bytes_accessed=6 * depth * width, transcendentals=0
        ),
        name="core_products",
    )(hidden, hidden_peer, grad, grad_peer, w)


def local(
    hot_rows,
    cold_codes,
    scale_index,
    scale_table,
    stale_rows,
    tile_index,
    tile_count,
    tile_values,
    weight,
    out_grad,
    stale_grads,
    send_rows,
):
    first = lax.axis_index("core") == 0
    nx, ny, nz = lax.axis_size("dx"), lax.axis_size("dy"), lax.axis_size("z")
    tile_slots = tile_values.shape[1]
    cluster_rows = tile_values.shape[2]
    slots = send_rows.shape[1]
    block = weight.shape[0]
    half_w = weight.shape[1] // 2

    def spread(value, axis, count):
        copies = jnp.broadcast_to(value[None], (count, *value.shape))
        return lax.all_to_all(copies, axis, split_axis=0, concat_axis=0, tiled=True)

    my_cols = halves(weight, first)[0]
    column = spread(my_cols, "dy", ny).reshape(ny * block, half_w)
    w = spread(column, "dx", nx).reshape(nx * ny * block, half_w)

    local_rows = jnp.concatenate(
        [hot_rows, dequantize(cold_codes, scale_index, scale_table)], axis=0
    )
    row_count = local_rows.shape[0]
    source = jnp.concatenate([local_rows, stale_rows], axis=0)
    src_count = source.shape[0] // cluster_rows
    live_mask = jnp.arange(tile_slots, dtype=jnp.int32)[None, :] < tile_count[:, None]
    masked = jnp.where(live_mask[:, :, None, None], tile_values, jnp.zeros_like(tile_values))
    selector = tile_index[:, :, None] == jnp.arange(src_count, dtype=jnp.int32)[None, None, :]
    operator = jnp.sum(
        jnp.where(
            selector[:, :, None, :, None], masked[:, :, :, None, :].astype(jnp.float32), 0.0
        ),
        axis=1,
    )
    operator = operator.reshape(row_count, src_count * cluster_rows)
    hidden = jnp.dot(operator, source.astype(jnp.float32), precision=lax.Precision.HIGHEST)
    hidden = hidden.astype(BF)
    grad_mine, grad_give = halves(out_grad, first)
    hidden_peer = swap_core(hidden)
    grad_peer = swap_core(grad_give)
    sends = send_rows.reshape(-1)
    row_ids = jnp.arange(row_count, dtype=jnp.int32)
    outgoing = dot((sends[:, None] == row_ids[None, :]).astype(BF), local_rows, 1, 0).astype(BF)

    act_mine, act_give, pre_mine, pre_peer, part = core_products(
        hidden, hidden_peer, grad_mine, grad_peer, w
    )
    got_x = lax.all_to_all(
        part.reshape(nx, ny * block, half_w), "dx", split_axis=0, concat_axis=0, tiled=True
    )

    hid_give = dot(pre_peer, w, 1, 1).astype(BF)
    hid_got = swap_core(hid_give)
    hid_grad = (dot(pre_mine, w, 1, 1) + hid_got.astype(jnp.float32)).astype(BF)
    act_got = swap_core(act_give)
    activations = ordered(act_mine, act_got, first)
    src_grad = lax.dot_general(
        operator,
        hid_grad.astype(jnp.float32),
        (((0,), (0,)), ((), ())),
        precision=lax.Precision.HIGHEST,
    )
    bound_grad = src_grad[row_count:].astype(BF)
    peers = nx * ny
    riders = jnp.concatenate(
        [outgoing.reshape(peers, slots, -1), bound_grad.reshape(peers, slots, -1)], axis=1
    )

    summed = jnp.sum(got_x.astype(jnp.float32), axis=0).astype(BF).reshape(ny, block, half_w)
    got_y = lax.all_to_all(summed, "dy", split_axis=0, concat_axis=0, tiled=True)
    total = jnp.sum(got_y.astype(jnp.float32), axis=0)
    for reach in (1, -1, 3):
        pairs = [(i, (i + (reach if i % 2 == 0 else -reach)) % nz) for i in range(nz)]
        total = total + lax.ppermute(total, "z", pairs)
    got_r = lax.all_to_all(riders, DOM, split_axis=0, concat_axis=0, tiled=True)
    next_rows = got_r[:, :slots].reshape(peers * slots, -1)
    next_grads = got_r[:, slots:].reshape(peers * slots, -1)

    weight_grad = ordered(total, swap_core(total), first)

    placing = row_ids[:, None] == sends[None, :]
    returned = dot(placing.astype(BF), stale_grads, 1, 0)
    feature_grad = (src_grad[:row_count] + returned).astype(BF)
    return (activations, feature_grad, weight_grad, next_rows, next_grads)


def solution(mesh):
    shape = (mesh.shape["group"] // 2, 2, 4, mesh.shape["dom"] // 4)
    torus = Mesh(mesh.devices.reshape(shape), AXES)
    rows = P(AXES, None)
    placed = (
        rows,
        rows,
        P(AXES),
        P(),
        rows,
        rows,
        P(AXES),
        P(AXES, None, None, None),
        P(DOM, None),
        rows,
        rows,
        rows,
    )
    return jax.shard_map(
        local,
        mesh=torus,
        in_specs=placed,
        out_specs=(rows, rows, P(DOM, None), rows, rows),
        check_vma=False,
    )
```

time: 135 us -> 114 us (0.84)
  blocking collectives: 42.8 us -> 0 us
  starting transfers between devices: 28.5 us -> 64.1 us
  waiting for transfers between devices: 35.8 us -> 20.9 us
  matrix products: 14.5 us -> 6.97 us
  Pallas kernels: 0 us -> 4.35 us
  local copies, waits for them, and re-layouts: 2.26 us -> 6.12 us
    all_to_all x1 -> x0, blocking collectives: 42.8 us -> none  [local(): got_w = lax.all_to_all(send_w, DOM, split_axis=0, concat_axis=0, tiled=True)]
    ppermute x3 -> x8, starting transfers between devices: 13.7 us -> 37.9 us  [the longest x5 22.3 us: swap_core(): return lax.ppermute(value, 'core', SWAP)]
    all_to_all x2 -> x5, waiting for transfers between devices: 35.6 us -> 14.9 us  [the longest x2 8.02 us: spread(): return lax.all_to_all(copies, axis, split_axis=0, concat_axis=0, tiled=True)]
    all_to_all x2 -> x5, starting transfers between devices: 14.8 us -> 26.2 us  [the longest x2 12.8 us: spread(): return lax.all_to_all(copies, axis, split_axis=0, concat_axis=0, tiled=True)]
    dot_general x13 -> x4, matrix products: 11.6 us -> 5.15 us  [dot(): lax.dot_general(a, b, (((ca,), (cb,)), ((), ())), preferred_element_type=...]
    ppermute x3 -> x8, waiting for transfers between devices: 0.15 us -> 5.95 us  [the longest x3 4.44 us: local(): total = total + lax.ppermute(total, 'z', pairs)]
    pallas_call x0 -> x1, Pallas kernels: none -> 4.35 us  [core_products(): pl.pallas_call(body, out_shape=(small, small, small, small, jax.ShapeDtyp...]
    reshape x0 -> x4, local copies, waits for them, and re-layouts: none -> 2.69 us  [the longest x1 1.05 us: local(): outgoing.reshape(peers, slots, -1)]
  transfers between devices with their start and end apart: 5 -> 13, of which waited for: 3 -> 6; matrix products, arithmetic and copies ran while one was open for 9% -> 15% of each run, Pallas kernels for 0% -> 0%
where the time goes in v2:
time: 114 us; the launch traced here: 113 us
  starting transfers between devices  64.1 us (56%)
  waiting for transfers between devices  20.9 us (18%)
  other arithmetic  9.83 us (9%)
  matrix products  6.97 us (6%)
  local copies, waits for them, and re-layouts  6.12 us (5%)
  Pallas kernels  4.35 us (4%)
    ppermute x5, starting transfers between devices, swap_core(): return lax.ppermute(value, 'core', SWAP)  22.3 us
    ppermute x3, starting transfers between devices, local(): total = total + lax.ppermute(total, 'z', pairs)  15.6 us
    all_to_all x2, starting transfers between devices, spread(): return lax.all_to_all(copies, axis, split_axis=0, concat_axis=0, tiled=True)  12.8 us
    all_to_all x2, waiting for transfers between devices, spread(): return lax.all_to_all(copies, axis, split_axis=0, concat_axis=0, tiled=True)  8.02 us
    all_to_all x1, waiting for transfers between devices, local(): lax.all_to_all(summed, 'dy', split_axis=0, concat_axis=0, tiled=True)  6.88 us
    all_to_all x1, starting transfers between devices, local(): lax.all_to_all(summed, 'dy', split_axis=0, concat_axis=0, tiled=True)  5.77 us
    dot_general x4, matrix products, dot(): lax.dot_general(a, b, (((ca,), (cb,)), ((), ())), preferred_element_type=...  5.15 us
    ppermute x3, waiting for transfers between devices, local(): total = total + lax.ppermute(total, 'z', pairs)  4.44 us
  transfers between devices with their start and end apart: 13, of which 6 were waited for; matrix products, arithmetic and copies ran while one was open for 15% of the time, Pallas kernels for 0%

profile of v2, /device:TPU:1, one launch (start us, length us, event | category | flops | bytes accessed | tf_op | source)
XLA Modules:
  0.0 113.2 jit_solution(4882724276824952506)
XLA Ops:
  0.6 0.0 copy-start
  0.6 0.0 copy-start.7
  0.7 0.9 slice_select_fusion
  1.5 0.7 broadcast_in_dim.76
  2.2 7.6 %all-to-all-start = ((bf16[8,32,512]{2,1,0:T(8,128)(2,1)}), bf16[8,32,512]{2,1,0:T(8,128)(2,1)S(1)}, u32[]{:S(2)}, u32[]{:S(2)}) async-start(bf16[8,32,512]{2,1,0:T(8,128)(2,1)} %broadcast_in_dim.76), calls=%async_computation | async-start | bytes 524288 | tf_op jit(solution)/shard_map/all_to_all | solution.py:100
  9.9 0.8 iota_compare_fusion.7
  10.6 0.9 select_reduce_fusion.1
  11.5 1.1 multiply_convert_fusion
  12.6 0.8 iota_compare_fusion.8
  13.3 0.1 select_convert_fusion
  13.4 5.9 %all-to-all-done = bf16[8,32,512]{2,1,0:T(8,128)(2,1)S(1)} async-done(((bf16[8,32,512]{2,1,0:T(8,128)(2,1)}), bf16[8,32,512]{2,1,0:T(8,128)(2,1)S(1)}, u32[]{:S(2)}, u32[]{:S(2)}) %all-to-all-start) | async-done | bytes 262176 | tf_op jit(solution)/shard_map/all_to_all | solution.py:100
  19.3 1.1 broadcast_in_dim.78
  20.4 5.2 %all-to-all-start.1 = ((bf16[4,256,512]{2,1,0:T(8,128)(2,1)}), bf16[4,256,512]{2,1,0:T(8,128)(2,1)S(1)}, u32[]{:S(2)}, u32[]{:S(2)}) async-start(bf16[4,256,512]{2,1,0:T(8,128)(2,1)} %broadcast_in_dim.78), calls=%async_computation.1 | async-start | bytes 2097152 | tf_op jit(solution)/shard_map/all_to_all | solution.py:100
  25.6 0.1 select_reduce_fusion
  25.8 0.0 copy-start.3
  25.8 0.2 copy.19
  26.0 1.0 convolution_convert_fusion.1.h_ref
  27.1 0.0 copy-start.9
  27.1 4.5 %collective-permute-start = (bf16[256,1024]{1,0:T(8,128)(2,1)S(1)}, bf16[256,1024]{1,0:T(8,128)(2,1)S(1)}, u32[]{:S(2)}, u32[]{:S(2)}) collective-permute-start(bf16[256,1024]{1,0:T(8,128)(2,1)S(1)} %convolution_convert_fusion.1.h_ref), channel_id=1, source_target_pairs={{0,32},{32,0},{1,33},{33,1},{2,34},{34,2},{3,35},{35,3},{4,36},{36... | collective-permute-start | bytes 1572872 | tf_op jit(solution)/shard_map/ppermute | solution.py:33
  31.6 0.0 copy-done.3
  31.6 0.7 broadcast_select_fusion.2
  32.3 1.9 %collective-permute-start.1 = (bf16[256,512]{1,0:T(8,128)(2,1)S(1)}, bf16[256,512]{1,0:T(8,128)(2,1)S(1)}, u32[]{:S(2)}, u32[]{:S(2)}) collective-permute-start(bf16[256,512]{1,0:T(8,128)(2,1)S(1)} %get-tuple-element.19), channel_id=1, source_target_pairs={{0,32},{32,0},{1,33},{33,1},{2,34},{34,2},{3,35},{35,3},{4,36},{36... | collective-permute-start | bytes 786440 | tf_op jit(solution)/shard_map/ppermute | solution.py:33
  34.3 1.5 %collective-permute-done.1.gp_ref = bf16[256,512]{1,0:T(8,128)(2,1)S(1)} collective-permute-done((bf16[256,512]{1,0:T(8,128)(2,1)S(1)}, bf16[256,512]{1,0:T(8,128)(2,1)S(1)}, u32[]{:S(2)}, u32[]{:S(2)}) %collective-permute-start.1) | collective-permute-done | bytes 262176 | tf_op jit(solution)/shard_map/ppermute | solution.py:33
  35.8 0.0 collective-permute-done.hp_ref
  35.8 2.1 %all-to-all-done.1 = bf16[4,256,512]{2,1,0:T(8,128)(2,1)S(1)} async-done(((bf16[4,256,512]{2,1,0:T(8,128)(2,1)}), bf16[4,256,512]{2,1,0:T(8,128)(2,1)S(1)}, u32[]{:S(2)}, u32[]{:S(2)}) %all-to-all-start.1) | async-done | bytes 1048608 | tf_op jit(solution)/shard_map/all_to_all | solution.py:100
  37.9 1.0 copy-done.1
  38.9 4.3 %core_products.1 = (bf16[256,512]{1,0:T(8,128)(2,1)}, bf16[256,512]{1,0:T(8,128)(2,1)}, bf16[256,512]{1,0:T(8,128)(2,1)}, bf16[256,512]{1,0:T(8,128)(2,1)}, bf16[1024,512]{1,0:T(8,128)(2,1)}) custom-call(bf16[256,1024]{1,0:T(8,128)(2,1)} %copy-done.9, bf16[256,1024]{1,0:T(8,128)(2,1)} %copy-done.10, bf16[256,512]{1,0:T(8,128)(2,1)} %get-tuple-element.20.g_ref, ...), custom_call_target="tpu_custom_call" | custom-call | flops 1073741824 | bytes 3145728 | tf_op jit(solution)/shard_map/core_products/pallas_call | solution.py:66
  43.2 3.7 %all-to-all-start.2 = ((bf16[4,256,512]{2,1,0:T(8,128)(2,1)}), bf16[4,256,512]{2,1,0:T(8,128)(2,1)S(1)}, u32[]{:S(2)}, u32[]{:S(2)}) async-start(bf16[4,256,512]{2,1,0:T(8,128)(2,1)} %bitcast.25), calls=%async_computation.2 | async-start | bytes 2097152 | tf_op jit(solution)/shard_map/all_to_all | solution.py:134
  46.9 0.0 copy-done.2
  46.9 0.0 copy-done.4
  46.9 0.5 convolution_convert_fusion
  47.4 5.7 %collective-permute-start.3 = (bf16[256,1024]{1,0:T(8,128)(2,1)S(1)}, bf16[256,1024]{1,0:T(8,128)(2,1)}, u32[]{:S(2)}, u32[]{:S(2)}) collective-permute-start(bf16[256,1024]{1,0:T(8,128)(2,1)S(1)} %convolution_convert_fusion), channel_id=1, source_target_pairs={{0,32},{32,0},{1,33},{33,1},{2,34},{34,2},{3,35},{35,3},{4,36},{36... | collective-permute-start | bytes 1572872 | tf_op jit(solution)/shard_map/ppermute | solution.py:33
  53.1 0.1 copy.20
  53.2 0.1 eq.69
  53.3 2.0 %convolution_convert_fusion.2 = bf16[128,1024]{1,0:T(8,128)(2,1)} fusion(bf16[128,1024]{1,0:T(8,128)(2,1)} %copy-done.5, bf16[128,1024]{1,0:T(8,128)(2,1)} %param.12, s32[128]{0:T(128)S(1)} %eq.69), kind=kOutput, calls=%fused_computation.4 | convolution fusion | flops 68321280 | bytes 786944 | tf_op jit(solution)/shard_map/dot_general | solution.py:29
  55.3 1.1 reshape.72
  56.3 1.9 %collective-permute-start.2 = (bf16[256,512]{1,0:T(8,128)(2,1)}, bf16[256,512]{1,0:T(8,128)(2,1)}, u32[]{:S(2)}, u32[]{:S(2)}) collective-permute-start(bf16[256,512]{1,0:T(8,128)(2,1)} %get-tuple-element.11), channel_id=1, source_target_pairs={{0,32},{32,0},{1,33},{33,1},{2,34},{34,2},{3,35},{35,3},{4,36},{36... | collective-permute-start | bytes 786440 | tf_op jit(solution)/shard_map/ppermute | solution.py:33
  58.3 0.0 all-to-all-done.2
  58.3 0.9 reduce_sum.41
  59.2 5.8 %all-to-all-start.3 = ((bf16[8,32,512]{2,1,0:T(8,128)(2,1)}), bf16[8,32,512]{2,1,0:T(8,128)(2,1)S(1)}, u32[]{:S(2)}, u32[]{:S(2)}) async-start(bf16[8,32,512]{2,1,0:T(8,128)(2,1)} %bitcast.3), calls=%async_computation.3 | async-start | bytes 524288 | tf_op jit(solution)/shard_map/all_to_all | solution.py:156
  65.0 0.0 collective-permute-done.3
  65.0 1.6 %fusion = bf16[256,1024]{1,0:T(8,128)(2,1)S(1)} fusion(bf16[256,512]{1,0:T(8,128)(2,1)} %get-tuple-element.12, bf16[1024,512]{1,0:T(8,128)(2,1)S(1)} %bitcast.21, bf16[256,1024]{1,0:T(8,128)(2,1)} %collective-permute-done.3), kind=kOutput, calls=%fused_computation.3 | convolution fusion | flops 269221888 | bytes 2359296 | tf_op jit(solution)/shard_map/dot_general | solution.py:29
  66.6 0.8 fusion.10
  67.4 0.1 reshape.73
  67.5 6.9 %all-to-all-done.3 = bf16[8,32,512]{2,1,0:T(8,128)(2,1)S(1)} async-done(((bf16[8,32,512]{2,1,0:T(8,128)(2,1)}), bf16[8,32,512]{2,1,0:T(8,128)(2,1)S(1)}, u32[]{:S(2)}, u32[]{:S(2)}) %all-to-all-start.3) | async-done | bytes 262176 | tf_op jit(solution)/shard_map/all_to_all | solution.py:156
  74.4 4.0 %collective-permute-start.4 = (f32[32,512]{1,0:T(8,128)S(1)}, f32[32,512]{1,0:T(8,128)S(1)}, u32[]{:S(2)}, u32[]{:S(2)}) collective-permute-start(f32[32,512]{1,0:T(8,128)S(1)} %convert_reduce_fusion), channel_id=1, source_target_pairs={{0,64},{64,0},{128,192},{192,128},{256,320},{320,256},{384,448},{4... | collective-permute-start | bytes 196616 | tf_op jit(solution)/shard_map/ppermute | solution.py:160
  78.4 1.1 pad_maximum_fusion.1
  79.5 3.9 %all-to-all-start.4 = ((bf16[32,8,1024]{2,1,0:T(8,128)(2,1)}), bf16[32,8,1024]{2,1,0:T(8,128)(2,1)S(1)}, u32[]{:S(2)}, u32[]{:S(2)}) async-start(bf16[32,8,1024]{2,1,0:T(8,128)(2,1)} %pad_maximum_fusion.1), calls=%async_computation.4 | async-start | bytes 1048576 | tf_op jit(solution)/shard_map/all_to_all | solution.py:161
  83.4 0.0 collective-permute-done.4
  83.4 8.8 %collective-permute-start.5 = (f32[32,512]{1,0:T(8,128)S(1)}, f32[32,512]{1,0:T(8,128)S(1)}, u32[]{:S(2)}, u32[]{:S(2)}) collective-permute-start(f32[32,512]{1,0:T(8,128)S(1)} %add.17), channel_id=1, source_target_pairs={{0,448},{64,128},{128,64},{192,256},{256,192},{320,384},{384,320},... | collective-permute-start | bytes 196616 | tf_op jit(solution)/shard_map/ppermute | solution.py:160
  92.3 0.0 collective-permute-done.2
  92.3 1.0 broadcast_select_fusion.1
  93.3 0.9 collective-permute-done.5
  94.2 2.8 %collective-permute-start.6 = (f32[32,512]{1,0:T(8,128)S(1)}, f32[32,512]{1,0:T(8,128)S(1)}, u32[]{:S(2)}, u32[]{:S(2)}) collective-permute-start(f32[32,512]{1,0:T(8,128)S(1)} %add.18), channel_id=1, source_target_pairs={{0,192},{64,384},{128,320},{192,0},{256,448},{320,128},{384,64},{4... | collective-permute-start | bytes 196616 | tf_op jit(solution)/shard_map/ppermute | solution.py:160
  97.0 0.9 pad_maximum_fusion
  97.9 3.5 %collective-permute-done.6 = f32[32,512]{1,0:T(8,128)S(1)} collective-permute-done((f32[32,512]{1,0:T(8,128)S(1)}, f32[32,512]{1,0:T(8,128)S(1)}, u32[]{:S(2)}, u32[]{:S(2)}) %collective-permute-start.6) | collective-permute-done | bytes 65568 | tf_op jit(solution)/shard_map/ppermute | solution.py:160
  101.4 8.3 %collective-permute-start.7 = (f32[32,512]{1,0:T(8,128)S(1)}, f32[32,512]{1,0:T(8,128)S(1)}, u32[]{:S(2)}, u32[]{:S(2)}) collective-permute-start(f32[32,512]{1,0:T(8,128)S(1)} %add.19), channel_id=1, source_target_pairs={{0,32},{32,0},{1,33},{33,1},{2,34},{34,2},{3,35},{35,3},{4,36},{36... | collective-permute-start | bytes 196616 | tf_op jit(solution)/shard_map/ppermute | solution.py:33
  109.7 1.1 fusion.1
  110.8 0.0 collective-permute-done.7
  110.8 0.7 pad_maximum_fusion.2
  111.5 0.0 all-to-all-done.4
  111.5 0.2 fusion.20
  111.7 0.8 reshape.74
  112.4 0.8 reshape.75
  (26 shorter events, 0.2 us)
Async XLA Ops:
  0.6 109.1 %copy-start = (bf16[128,1024]{1,0:T(8,128)(2,1)S(1)}, bf16[128,1024]{1,0:T(8,128)(2,1)}, u32[]{:S(2)}) copy-start(bf16[128,1024]{1,0:T(8,128)(2,1)} %param.22) | copy-start | bytes 786436
  0.6 12.7 %copy-start.7 = (bf16[2,3,128,128]{3,2,1,0:T(8,128)(2,1)S(1)}, bf16[2,3,128,128]{3,2,1,0:T(8,128)(2,1)}, u32[]{:S(2)}) copy-start(bf16[2,3,128,128]{3,2,1,0:T(8,128)(2,1)} %param.19) | copy-start | bytes 589828
  2.2 17.1 %all-to-all-start = ((bf16[8,32,512]{2,1,0:T(8,128)(2,1)}), bf16[8,32,512]{2,1,0:T(8,128)(2,1)S(1)}, u32[]{:S(2)}, u32[]{:S(2)}) async-start(bf16[8,32,512]{2,1,0:T(8,128)(2,1)} %broadcast_in_dim.76), calls=%async_computation | async-start | bytes 524288 | tf_op jit(solution)/shard_map/all_to_all | solution.py:100
  12.6 13.4 %copy-start.5 = (bf16[128,1024]{1,0:T(8,128)(2,1)}, bf16[128,1024]{1,0:T(8,128)(2,1)S(1)}, u32[]{:S(2)}) copy-start(bf16[128,1024]{1,0:T(8,128)(2,1)S(1)} %multiply_convert_fusion) | copy-start | bytes 786436
  20.4 5.6 %copy-start.11 = (bf16[128,1024]{1,0:T(8,128)(2,1)S(1)}, bf16[128,1024]{1,0:T(8,128)(2,1)}, u32[]{:S(2)}) copy-start(bf16[128,1024]{1,0:T(8,128)(2,1)} %param.16) | copy-start | bytes 786436
  20.4 5.6 %copy-start.12 = (bf16[128,1024]{1,0:T(8,128)(2,1)S(1)}, bf16[128,1024]{1,0:T(8,128)(2,1)}, u32[]{:S(2)}) copy-start(bf16[128,1024]{1,0:T(8,128)(2,1)} %param.12) | copy-start | bytes 786436
  20.4 17.5 %all-to-all-start.1 = ((bf16[4,256,512]{2,1,0:T(8,128)(2,1)}), bf16[4,256,512]{2,1,0:T(8,128)(2,1)S(1)}, u32[]{:S(2)}, u32[]{:S(2)}) async-start(bf16[4,256,512]{2,1,0:T(8,128)(2,1)} %broadcast_in_dim.78), calls=%async_computation.1 | async-start | bytes 2097152 | tf_op jit(solution)/shard_map/all_to_all | solution.py:100
  25.8 5.8 %copy-start.3 = (bf16[256,1024]{1,0:T(8,128)(2,1)S(1)}, bf16[256,1024]{1,0:T(8,128)(2,1)}, u32[]{:S(2)}) copy-start(bf16[256,1024]{1,0:T(8,128)(2,1)} %param.21) | copy-start | bytes 1572868
  27.1 10.9 %copy-start.9 = (bf16[256,1024]{1,0:T(8,128)(2,1)}, bf16[256,1024]{1,0:T(8,128)(2,1)S(1)}, u32[]{:S(2)}) copy-start(bf16[256,1024]{1,0:T(8,128)(2,1)S(1)} %convolution_convert_fusion.1.h_ref) | copy-start | bytes 1572868
  27.1 8.7 %collective-permute-start = (bf16[256,1024]{1,0:T(8,128)(2,1)S(1)}, bf16[256,1024]{1,0:T(8,128)(2,1)S(1)}, u32[]{:S(2)}, u32[]{:S(2)}) collective-permute-start(bf16[256,1024]{1,0:T(8,128)(2,1)S(1)} %convolution_convert_fusion.1.h_ref), channel_id=1, source_target_pairs={{0,32},{32,0},{1,33},{33,1},{2,34},{34,2},{3,35},{35,3},{4,36},{36... | collective-permute-start | bytes 1572872 | tf_op jit(solution)/shard_map/ppermute | solution.py:33
  32.3 3.4 %collective-permute-start.1 = (bf16[256,512]{1,0:T(8,128)(2,1)S(1)}, bf16[256,512]{1,0:T(8,128)(2,1)S(1)}, u32[]{:S(2)}, u32[]{:S(2)}) collective-permute-start(bf16[256,512]{1,0:T(8,128)(2,1)S(1)} %get-tuple-element.19), channel_id=1, source_target_pairs={{0,32},{32,0},{1,33},{33,1},{2,34},{34,2},{3,35},{35,3},{4,36},{36... | collective-permute-start | bytes 786440 | tf_op jit(solution)/shard_map/ppermute | solution.py:33
  35.8 2.1 %copy-start.13 = (bf16[256,512]{1,0:T(8,128)(2,1)}, bf16[256,512]{1,0:T(8,128)(2,1)S(1)}, u32[]{:S(2)}) copy-start(bf16[256,512]{1,0:T(8,128)(2,1)S(1)} %collective-permute-done.1.gp_ref) | copy-start | bytes 786436
  35.8 2.1 %copy-start.10 = (bf16[256,1024]{1,0:T(8,128)(2,1)}, bf16[256,1024]{1,0:T(8,128)(2,1)S(1)}, u32[]{:S(2)}) copy-start(bf16[256,1024]{1,0:T(8,128)(2,1)S(1)} %collective-permute-done.hp_ref) | copy-start | bytes 1572868
  37.9 1.0 copy-start.1
  43.2 3.7 %copy-start.2 = (bf16[4,256,512]{2,1,0:T(8,128)(2,1)S(1)}, bf16[4,256,512]{2,1,0:T(8,128)(2,1)}, u32[]{:S(2)}) copy-start(bf16[4,256,512]{2,1,0:T(8,128)(2,1)} %copy-done.1) | copy-start | bytes 3145732
  43.2 3.7 %copy-start.4 = (bf16[256,512]{1,0:T(8,128)(2,1)S(1)}, bf16[256,512]{1,0:T(8,128)(2,1)}, u32[]{:S(2)}) copy-start(bf16[256,512]{1,0:T(8,128)(2,1)} %get-tuple-element.13) | copy-start | bytes 786436
  43.2 9.9 %copy-start.8 = (s32[32,4]{0,1:T(4,128)S(1)}, s32[32,4]{0,1:T(4,128)}, u32[]{:S(2)}) copy-start(s32[32,4]{0,1:T(4,128)} %param.23) | copy-start | bytes 1540
  43.2 15.0 %all-to-all-start.2 = ((bf16[4,256,512]{2,1,0:T(8,128)(2,1)}), bf16[4,256,512]{2,1,0:T(8,128)(2,1)S(1)}, u32[]{:S(2)}, u32[]{:S(2)}) async-start(bf16[4,256,512]{2,1,0:T(8,128)(2,1)} %bitcast.25), calls=%async_computation.2 | async-start | bytes 2097152 | tf_op jit(solution)/shard_map/all_to_all | solution.py:134
  47.4 17.6 %collective-permute-start.3 = (bf16[256,1024]{1,0:T(8,128)(2,1)S(1)}, bf16[256,1024]{1,0:T(8,128)(2,1)}, u32[]{:S(2)}, u32[]{:S(2)}) collective-permute-start(bf16[256,1024]{1,0:T(8,128)(2,1)S(1)} %convolution_convert_fusion), channel_id=1, source_target_pairs={{0,32},{32,0},{1,33},{33,1},{2,34},{34,2},{3,35},{35,3},{4,36},{36... | collective-permute-start | bytes 1572872 | tf_op jit(solution)/shard_map/ppermute | solution.py:33
  56.3 35.9 %collective-permute-start.2 = (bf16[256,512]{1,0:T(8,128)(2,1)}, bf16[256,512]{1,0:T(8,128)(2,1)}, u32[]{:S(2)}, u32[]{:S(2)}) collective-permute-start(bf16[256,512]{1,0:T(8,128)(2,1)} %get-tuple-element.11), channel_id=1, source_target_pairs={{0,32},{32,0},{1,33},{33,1},{2,34},{34,2},{3,35},{35,3},{4,36},{36... | collective-permute-start | bytes 786440 | tf_op jit(solution)/shard_map/ppermute | solution.py:33
  59.2 15.2 %all-to-all-start.3 = ((bf16[8,32,512]{2,1,0:T(8,128)(2,1)}), bf16[8,32,512]{2,1,0:T(8,128)(2,1)S(1)}, u32[]{:S(2)}, u32[]{:S(2)}) async-start(bf16[8,32,512]{2,1,0:T(8,128)(2,1)} %bitcast.3), calls=%async_computation.3 | async-start | bytes 524288 | tf_op jit(solution)/shard_map/all_to_all | solution.py:156
  67.4 24.9 %copy-start.6 = (bf16[256,512]{1,0:T(8,128)(2,1)S(1)}, bf16[256,512]{1,0:T(8,128)(2,1)}, u32[]{:S(2)}) copy-start(bf16[256,512]{1,0:T(8,128)(2,1)} %get-tuple-element.10) | copy-start | bytes 786436
  74.4 9.0 %collective-permute-start.4 = (f32[32,512]{1,0:T(8,128)S(1)}, f32[32,512]{1,0:T(8,128)S(1)}, u32[]{:S(2)}, u32[]{:S(2)}) collective-permute-start(f32[32,512]{1,0:T(8,128)S(1)} %convert_reduce_fusion), channel_id=1, source_target_pairs={{0,64},{64,0},{128,192},{192,128},{256,320},{320,256},{384,448},{4... | collective-permute-start | bytes 196616 | tf_op jit(solution)/shard_map/ppermute | solution.py:160
  79.5 32.0 %all-to-all-start.4 = ((bf16[32,8,1024]{2,1,0:T(8,128)(2,1)}), bf16[32,8,1024]{2,1,0:T(8,128)(2,1)S(1)}, u32[]{:S(2)}, u32[]{:S(2)}) async-start(bf16[32,8,1024]{2,1,0:T(8,128)(2,1)} %pad_maximum_fusion.1), calls=%async_computation.4 | async-start | bytes 1048576 | tf_op jit(solution)/shard_map/all_to_all | solution.py:161
  83.4 10.8 %collective-permute-start.5 = (f32[32,512]{1,0:T(8,128)S(1)}, f32[32,512]{1,0:T(8,128)S(1)}, u32[]{:S(2)}, u32[]{:S(2)}) collective-permute-start(f32[32,512]{1,0:T(8,128)S(1)} %add.17), channel_id=1, source_target_pairs={{0,448},{64,128},{128,64},{192,256},{256,192},{320,384},{384,320},... | collective-permute-start | bytes 196616 | tf_op jit(solution)/shard_map/ppermute | solution.py:160
  94.2 7.2 %collective-permute-start.6 = (f32[32,512]{1,0:T(8,128)S(1)}, f32[32,512]{1,0:T(8,128)S(1)}, u32[]{:S(2)}, u32[]{:S(2)}) collective-permute-start(f32[32,512]{1,0:T(8,128)S(1)} %add.18), channel_id=1, source_target_pairs={{0,192},{64,384},{128,320},{192,0},{256,448},{320,128},{384,64},{4... | collective-permute-start | bytes 196616 | tf_op jit(solution)/shard_map/ppermute | solution.py:160
  101.4 9.4 %collective-permute-start.7 = (f32[32,512]{1,0:T(8,128)S(1)}, f32[32,512]{1,0:T(8,128)S(1)}, u32[]{:S(2)}, u32[]{:S(2)}) collective-permute-start(f32[32,512]{1,0:T(8,128)S(1)} %add.19), channel_id=1, source_target_pairs={{0,32},{32,0},{1,33},{33,1},{2,34},{34,2},{3,35},{35,3},{4,36},{36... | collective-permute-start | bytes 196616 | tf_op jit(solution)/shard_map/ppermute | solution.py:33

commit v3 on v2

--- a/solution.py
+++ b/solution.py
@@ -2,6 +2,7 @@
 import jax.numpy as jnp
 from jax import lax
 from jax.experimental import pallas as pl
+from jax.experimental.pallas import tpu as pltpu
 from jax.sharding import Mesh
 from jax.sharding import PartitionSpec as P
 
@@ -69,6 +70,7 @@
         cost_estimate=pl.CostEstimate(
             flops=8 * rows * depth * width, bytes_accessed=6 * depth * width, transcendentals=0
         ),
+        compiler_params=pltpu.CompilerParams(vmem_limit_bytes=16 * 2**20),
         name="core_products",
     )(hidden, hidden_peer, grad, grad_peer, w)
 
@@ -99,7 +101,7 @@
         copies = jnp.broadcast_to(value[None], (count, *value.shape))
         return lax.all_to_all(copies, axis, split_axis=0, concat_axis=0, tiled=True)
 
-    my_cols = halves(weight, first)[0]
+    my_cols = lax.dynamic_slice_in_dim(weight, lax.axis_index("core") * half_w, half_w, axis=1)
     column = spread(my_cols, "dy", ny).reshape(ny * block, half_w)
     w = spread(column, "dx", nx).reshape(nx * ny * block, half_w)
 
@@ -155,14 +157,20 @@
     summed = jnp.sum(got_x.astype(jnp.float32), axis=0).astype(BF).reshape(ny, block, half_w)
     got_y = lax.all_to_all(summed, "dy", split_axis=0, concat_axis=0, tiled=True)
     total = jnp.sum(got_y.astype(jnp.float32), axis=0)
-    for reach in (1, -1, 3):
-        pairs = [(i, (i + (reach if i % 2 == 0 else -reach)) % nz) for i in range(nz)]
-        total = total + lax.ppermute(total, "z", pairs)
+    stack = lax.all_gather(total.astype(BF), ("z", "core"))
+    total = jnp.sum(stack.reshape(nz, 2, block, half_w).astype(jnp.float32), axis=0)
+    weight_grad = jnp.concatenate([total[0], total[1]], axis=1)
     got_r = lax.all_to_all(riders, DOM, split_axis=0, concat_axis=0, tiled=True)
-    next_rows = got_r[:, :slots].reshape(peers * slots, -1)
-    next_grads = got_r[:, slots:].reshape(peers * slots, -1)
-
-    weight_grad = ordered(total, swap_core(total), first)
+    flat_r = got_r.reshape(peers * 2 * slots, -1)
+    slot_row = jnp.arange(peers * slots, dtype=jnp.int32)
+    slot_row = slot_row + slot_row // slots * slots
+    flat_ids = jnp.arange(peers * 2 * slots, dtype=jnp.int32)
+
+    def unfold(kind):
+        pick = (slot_row + kind * slots)[:, None] == flat_ids[None, :]
+        return dot(pick.astype(BF), flat_r, 1, 0).astype(BF)
+
+    next_rows, next_grads = unfold(0), unfold(1)
 
     placing = row_ids[:, None] == sends[None, :]
     returned = dot(placing.astype(BF), stale_grads, 1, 0)

time: 114 us -> 117 us (1.026)
  blocking collectives: 0 us -> 26.6 us
  starting transfers between devices: 64.1 us -> 38 us
  waiting for transfers between devices: 20.9 us -> 24.1 us
  Pallas kernels: 4.35 us -> 2.63 us
  other arithmetic: 9.83 us -> 11 us
    all_gather x0 -> x1, blocking collectives: none -> 26.6 us  [local(): stack = lax.all_gather(total.astype(BF), ('z', 'core'))]
    ppermute x3 -> x0, starting transfers between devices: 15.6 us -> none  [local(): total = total + lax.ppermute(total, 'z', pairs)]
    all_to_all x1, waiting for transfers between devices: 0.01 us -> 9.73 us  [local(): lax.all_to_all(part.reshape(nx, ny * block, half_w), 'dx', split_axis=0,...]
    ppermute x5 -> x4, starting transfers between devices: 22.3 us -> 14 us  [swap_core(): return lax.ppermute(value, 'core', SWAP)]
    ppermute x3 -> x0, waiting for transfers between devices: 4.44 us -> none  [local(): total = total + lax.ppermute(total, 'z', pairs)]
    all_to_all x1, starting transfers between devices: 5.77 us -> 3.54 us  [local(): lax.all_to_all(summed, 'dy', split_axis=0, concat_axis=0, tiled=True)]
    all_to_all x2, waiting for transfers between devices: 8.02 us -> 6.05 us  [spread(): return lax.all_to_all(copies, axis, split_axis=0, concat_axis=0, tiled=True)]
    pallas_call x1, Pallas kernels: 4.35 us -> 2.63 us  [core_products(): pl.pallas_call(body, out_shape=(small, small, small, small, jax.ShapeDtyp...]
  transfers between devices with their start and end apart: 13 -> 9, of which waited for: 6 -> 5; matrix products, arithmetic and copies ran while one was open for 15% -> 15% of each run, Pallas kernels for 0% -> 0%
where the time goes in v3:
time: 117 us; the launch traced here: 116 us
  starting transfers between devices  38 us (32%)
  blocking collectives  26.6 us (23%)
  waiting for transfers between devices  24.1 us (21%)
  other arithmetic  11 us (9%)
  matrix products  7.87 us (7%)
  local copies, waits for them, and re-layouts  4.96 us (4%)
  Pallas kernels  2.63 us (2%)
    all_gather x1, blocking collectives, local(): stack = lax.all_gather(total.astype(BF), ('z', 'core'))  26.6 us
    ppermute x4, starting transfers between devices, swap_core(): return lax.ppermute(value, 'core', SWAP)  14 us
    all_to_all x2, starting transfers between devices, spread(): return lax.all_to_all(copies, axis, split_axis=0, concat_axis=0, tiled=True)  12.8 us
    all_to_all x1, waiting for transfers between devices, local(): lax.all_to_all(part.reshape(nx, ny * block, half_w), 'dx', split_axis=0,...  9.73 us
    all_to_all x1, waiting for transfers between devices, local(): lax.all_to_all(summed, 'dy', split_axis=0, concat_axis=0, tiled=True)  7 us
    dot_general x6, matrix products, dot(): lax.dot_general(a, b, (((ca,), (cb,)), ((), ())), preferred_element_type=...  6.07 us
    all_to_all x2, waiting for transfers between devices, spread(): return lax.all_to_all(copies, axis, split_axis=0, concat_axis=0, tiled=True)  6.05 us
    all_to_all x1, starting transfers between devices, local(): got_r = lax.all_to_all(riders, DOM, split_axis=0, concat_axis=0, tiled=True)  3.89 us
  transfers between devices with their start and end apart: 9, of which 5 were waited for; matrix products, arithmetic and copies ran while one was open for 15% of the time, Pallas kernels for 0%

profile of v3, /device:TPU:1, one launch (start us, length us, event | category | flops | bytes accessed | tf_op | source)
XLA Modules:
  0.0 116.1 jit_solution(989224158022863804)
XLA Ops:
  0.6 0.0 copy-start
  0.7 0.8 constant_dynamic-slice_fusion
  1.5 0.7 broadcast_in_dim.80
  2.2 7.6 %all-to-all-start = ((bf16[8,32,512]{2,1,0:T(8,128)(2,1)}), bf16[8,32,512]{2,1,0:T(8,128)(2,1)S(1)}, u32[]{:S(2)}, u32[]{:S(2)}) async-start(bf16[8,32,512]{2,1,0:T(8,128)(2,1)} %broadcast_in_dim.80), calls=%async_computation | async-start | bytes 524288 | tf_op jit(solution)/shard_map/all_to_all | solution.py:102
  9.8 0.8 iota_compare_fusion.11
  10.6 0.9 select_reduce_fusion.1
  11.4 1.1 multiply_convert_fusion
  12.5 0.0 copy-start.7
  12.5 0.8 iota_compare_fusion.12
  13.3 1.0 select_convert_fusion
  14.3 5.0 %all-to-all-done = bf16[8,32,512]{2,1,0:T(8,128)(2,1)S(1)} async-done(((bf16[8,32,512]{2,1,0:T(8,128)(2,1)}), bf16[8,32,512]{2,1,0:T(8,128)(2,1)S(1)}, u32[]{:S(2)}, u32[]{:S(2)}) %all-to-all-start) | async-done | bytes 262176 | tf_op jit(solution)/shard_map/all_to_all | solution.py:102
  19.3 1.1 broadcast_in_dim.82
  20.3 5.2 %all-to-all-start.1 = ((bf16[4,256,512]{2,1,0:T(8,128)(2,1)}), bf16[4,256,512]{2,1,0:T(8,128)(2,1)S(1)}, u32[]{:S(2)}, u32[]{:S(2)}) async-start(bf16[4,256,512]{2,1,0:T(8,128)(2,1)} %broadcast_in_dim.82), calls=%async_computation.1 | async-start | bytes 2097152 | tf_op jit(solution)/shard_map/all_to_all | solution.py:102
  25.5 0.1 select_reduce_fusion
  25.7 0.2 copy.19
  25.9 0.0 copy-start.3
  25.9 0.0 copy-done.7
  25.9 0.0 copy-done.10
  25.9 0.0 copy-done.11
  25.9 0.0 copy-start.9
  25.9 1.0 convolution_convert_fusion.1.h_ref
  27.0 4.5 %collective-permute-start = (bf16[256,1024]{1,0:T(8,128)(2,1)S(1)}, bf16[256,1024]{1,0:T(8,128)(2,1)S(1)}, u32[]{:S(2)}, u32[]{:S(2)}) collective-permute-start(bf16[256,1024]{1,0:T(8,128)(2,1)S(1)} %convolution_convert_fusion.1.h_ref), channel_id=1, source_target_pairs={{0,32},{32,0},{1,33},{33,1},{2,34},{34,2},{3,35},{35,3},{4,36},{36... | collective-permute-start | bytes 1572872 | tf_op jit(solution)/shard_map/ppermute | solution.py:34
  31.5 1.1 broadcast_select_fusion.2
  32.6 0.0 copy-done.3
  32.6 1.9 %collective-permute-start.1 = (bf16[256,512]{1,0:T(8,128)(2,1)S(1)}, bf16[256,512]{1,0:T(8,128)(2,1)S(1)}, u32[]{:S(2)}, u32[]{:S(2)}) collective-permute-start(bf16[256,512]{1,0:T(8,128)(2,1)S(1)} %get-tuple-element.17), channel_id=1, source_target_pairs={{0,32},{32,0},{1,33},{33,1},{2,34},{34,2},{3,35},{35,3},{4,36},{36... | collective-permute-start | bytes 786440 | tf_op jit(solution)/shard_map/ppermute | solution.py:34
  34.5 0.0 copy-done.9
  34.5 0.1 copy.20
  34.6 0.1 eq.95
  34.7 1.3 %collective-permute-done.1.gp_ref = bf16[256,512]{1,0:T(8,128)(2,1)S(1)} collective-permute-done((bf16[256,512]{1,0:T(8,128)(2,1)S(1)}, bf16[256,512]{1,0:T(8,128)(2,1)S(1)}, u32[]{:S(2)}, u32[]{:S(2)}) %collective-permute-start.1) | collective-permute-done | bytes 262176 | tf_op jit(solution)/shard_map/ppermute | solution.py:34
  36.0 0.7 copy-done.1
  36.7 0.0 collective-permute-done.hp_ref
  36.7 1.1 all-to-all-done.1
  37.8 0.9 copy-done.2
  38.8 2.6 %core_products.1 = (bf16[256,512]{1,0:T(8,128)(2,1)S(1)}, bf16[256,512]{1,0:T(8,128)(2,1)}, bf16[256,512]{1,0:T(8,128)(2,1)S(1)}, bf16[256,512]{1,0:T(8,128)(2,1)S(1)}, bf16[1024,512]{1,0:T(8,128)(2,1)}) custom-call(bf16[256,1024]{1,0:T(8,128)(2,1)S(1)} %convolution_convert_fusion.1.h_ref, bf16[256,1024]{1,0:T(8,128)(2,1)S(1)} %collective-permute-done.hp_ref, ...), custom_call_target="tpu_custom_call" | custom-call | flops 1073741824 | bytes 3145728 | tf_op jit(solution)/shard_map/core_products/pallas_call | solution.py:67
  41.4 5.7 %collective-permute-start.2 = (bf16[256,512]{1,0:T(8,128)(2,1)}, bf16[256,512]{1,0:T(8,128)(2,1)}, u32[]{:S(2)}, u32[]{:S(2)}) collective-permute-start(bf16[256,512]{1,0:T(8,128)(2,1)} %get-tuple-element.11), channel_id=1, source_target_pairs={{0,32},{32,0},{1,33},{33,1},{2,34},{34,2},{3,35},{35,3},{4,36},{36... | collective-permute-start | bytes 786440 | tf_op jit(solution)/shard_map/ppermute | solution.py:34
  47.1 0.0 copy-start.8
  47.1 3.7 %all-to-all-start.2 = ((bf16[4,256,512]{2,1,0:T(8,128)(2,1)}), bf16[4,256,512]{2,1,0:T(8,128)(2,1)S(1)}, u32[]{:S(2)}, u32[]{:S(2)}) async-start(bf16[4,256,512]{2,1,0:T(8,128)(2,1)} %bitcast.2), calls=%async_computation.2 | async-start | bytes 2097152 | tf_op jit(solution)/shard_map/all_to_all | solution.py:136
  50.7 0.0 copy-start.12
  50.8 1.3 %convolution_convert_fusion = bf16[256,1024]{1,0:T(8,128)(2,1)} fusion(bf16[256,512]{1,0:T(8,128)(2,1)S(1)} %get-tuple-element.13, bf16[1024,512]{1,0:T(8,128)(2,1)S(1)} %bitcast.31), kind=kOutput, calls=%fused_computation.1 | convolution fusion | flops 268697600 | bytes 1835008 | tf_op jit(solution)/shard_map/dot_general | solution.py:30
  52.0 1.9 %collective-permute-start.3 = (bf16[256,1024]{1,0:T(8,128)(2,1)}, bf16[256,1024]{1,0:T(8,128)(2,1)}, u32[]{:S(2)}, u32[]{:S(2)}) collective-permute-start(bf16[256,1024]{1,0:T(8,128)(2,1)} %convolution_convert_fusion), channel_id=1, source_target_pairs={{0,32},{32,0},{1,33},{33,1},{2,34},{34,2},{3,35},{35,3},{4,36},{36... | collective-permute-start | bytes 1572872 | tf_op jit(solution)/shard_map/ppermute | solution.py:34
  54.0 0.3 convolution_convert_fusion.4
  54.2 0.1 reshape.91
  54.4 0.0 collective-permute-done.2
  54.4 1.8 %broadcast_select_fusion.1 = (bf16[256,512]{1,0:T(8,128)(2,1)}, bf16[256,512]{1,0:T(8,128)(2,1)}) fusion(bf16[256,512]{1,0:T(8,128)(2,1)S(1)} %get-tuple-element.10, bf16[256,512]{1,0:T(8,128)(2,1)} %collective-permute-done.2, pred[]{:T(512)S(6)} %eq.87), kind=kLoop, calls=%fused_computation.31 | loop fusion | flops 262144 | bytes 1048577 | tf_op jit(solution)/shard_map/jit(_where)/select_n | solution.py:45
  56.2 9.7 %all-to-all-done.2 = bf16[4,256,512]{2,1,0:T(8,128)(2,1)S(1)} async-done(((bf16[4,256,512]{2,1,0:T(8,128)(2,1)}), bf16[4,256,512]{2,1,0:T(8,128)(2,1)S(1)}, u32[]{:S(2)}, u32[]{:S(2)}) %all-to-all-start.2) | async-done | bytes 1048608 | tf_op jit(solution)/shard_map/all_to_all | solution.py:136
  65.9 0.9 reduce_sum.53
  66.8 3.5 %all-to-all-start.3 = ((bf16[8,32,512]{2,1,0:T(8,128)(2,1)}), bf16[8,32,512]{2,1,0:T(8,128)(2,1)S(1)}, u32[]{:S(2)}, u32[]{:S(2)}) async-start(bf16[8,32,512]{2,1,0:T(8,128)(2,1)} %bitcast.3), calls=%async_computation.3 | async-start | bytes 524288 | tf_op jit(solution)/shard_map/all_to_all | solution.py:158
  70.3 0.0 collective-permute-done.3
  70.4 1.5 %fusion = bf16[256,1024]{1,0:T(8,128)(2,1)S(1)} fusion(bf16[256,512]{1,0:T(8,128)(2,1)S(1)} %get-tuple-element.12, bf16[1024,512]{1,0:T(8,128)(2,1)S(1)} %bitcast.32, bf16[256,1024]{1,0:T(8,128)(2,1)} %collective-permute-done.3), kind=kOutput, calls=%fused_computation.3 | convolution fusion | flops 269221888 | bytes 2359296 | tf_op jit(solution)/shard_map/dot_general | solution.py:30
  71.9 0.8 fusion.12
  72.7 0.0 copy-start.5
  72.7 0.0 copy-start.6
  72.7 0.1 reshape.92
  72.9 1.1 pad_maximum_fusion.1
  73.9 7.0 %all-to-all-done.3 = bf16[8,32,512]{2,1,0:T(8,128)(2,1)S(1)} async-done(((bf16[8,32,512]{2,1,0:T(8,128)(2,1)}), bf16[8,32,512]{2,1,0:T(8,128)(2,1)S(1)}, u32[]{:S(2)}, u32[]{:S(2)}) %all-to-all-start.3) | async-done | bytes 262176 | tf_op jit(solution)/shard_map/all_to_all | solution.py:158
  80.9 3.9 %all-to-all-start.4 = ((bf16[32,8,1024]{2,1,0:T(8,128)(2,1)}), bf16[32,8,1024]{2,1,0:T(8,128)(2,1)S(1)}, u32[]{:S(2)}, u32[]{:S(2)}) async-start(bf16[32,8,1024]{2,1,0:T(8,128)(2,1)} %pad_maximum_fusion.1), calls=%async_computation.4 | async-start | bytes 1048576 | tf_op jit(solution)/shard_map/all_to_all | solution.py:163
  84.8 0.9 pad_maximum_fusion
  85.7 1.1 fusion.1
  86.8 26.6 %all-gather = bf16[512,512]{1,0:T(8,128)(2,1)S(1)} all-gather(bf16[32,512]{1,0:T(8,128)(2,1)S(1)} %reduce_sum.54), channel_id=2, replica_groups=mesh['z'=8,'core'=2,'dx'=4,'dy'=8] {'z','core'}, dimensions={0}, use_global_device_ids=true | all-gather | bytes 557056 | tf_op jit(solution)/shard_map/all_gather | solution.py:160
  113.4 0.1 convert_reduce_fusion
  113.5 0.7 pad_maximum_fusion.2
  114.2 0.0 all-to-all-done.4
  114.2 1.0 convolution_convert_fusion.2
  115.2 1.0 convolution_convert_fusion.3
  (16 shorter events, 0.1 us)
Async XLA Ops:
  0.6 85.1 %copy-start = (bf16[128,1024]{1,0:T(8,128)(2,1)S(1)}, bf16[128,1024]{1,0:T(8,128)(2,1)}, u32[]{:S(2)}) copy-start(bf16[128,1024]{1,0:T(8,128)(2,1)} %param.22) | copy-start | bytes 786436
  2.2 17.1 %all-to-all-start = ((bf16[8,32,512]{2,1,0:T(8,128)(2,1)}), bf16[8,32,512]{2,1,0:T(8,128)(2,1)S(1)}, u32[]{:S(2)}, u32[]{:S(2)}) async-start(bf16[8,32,512]{2,1,0:T(8,128)(2,1)} %broadcast_in_dim.80), calls=%async_computation | async-start | bytes 524288 | tf_op jit(solution)/shard_map/all_to_all | solution.py:102
  12.5 13.4 %copy-start.7 = (bf16[128,1024]{1,0:T(8,128)(2,1)}, bf16[128,1024]{1,0:T(8,128)(2,1)S(1)}, u32[]{:S(2)}) copy-start(bf16[128,1024]{1,0:T(8,128)(2,1)S(1)} %multiply_convert_fusion) | copy-start | bytes 786436
  20.3 5.6 %copy-start.10 = (bf16[128,1024]{1,0:T(8,128)(2,1)S(1)}, bf16[128,1024]{1,0:T(8,128)(2,1)}, u32[]{:S(2)}) copy-start(bf16[128,1024]{1,0:T(8,128)(2,1)} %param.16) | copy-start | bytes 786436
  20.3 5.6 %copy-start.11 = (bf16[128,1024]{1,0:T(8,128)(2,1)S(1)}, bf16[128,1024]{1,0:T(8,128)(2,1)}, u32[]{:S(2)}) copy-start(bf16[128,1024]{1,0:T(8,128)(2,1)} %param.12) | copy-start | bytes 786436
  20.3 17.5 %all-to-all-start.1 = ((bf16[4,256,512]{2,1,0:T(8,128)(2,1)}), bf16[4,256,512]{2,1,0:T(8,128)(2,1)S(1)}, u32[]{:S(2)}, u32[]{:S(2)}) async-start(bf16[4,256,512]{2,1,0:T(8,128)(2,1)} %broadcast_in_dim.82), calls=%async_computation.1 | async-start | bytes 2097152 | tf_op jit(solution)/shard_map/all_to_all | solution.py:102
  25.9 6.7 %copy-start.3 = (f32[2,128,3,128]{1,0,3,2:T(2,128)}, f32[2,128,3,128]{1,0,3,2:T(2,128)S(1)}, u32[]{:S(2)}) copy-start(f32[2,128,3,128]{1,0,3,2:T(2,128)S(1)} %copy.19) | copy-start | bytes 1179652
  25.9 8.6 %copy-start.9 = (s32[32,4]{0,1:T(4,128)S(1)}, s32[32,4]{0,1:T(4,128)}, u32[]{:S(2)}) copy-start(s32[32,4]{0,1:T(4,128)} %param.23) | copy-start | bytes 1540
  27.0 9.8 %collective-permute-start = (bf16[256,1024]{1,0:T(8,128)(2,1)S(1)}, bf16[256,1024]{1,0:T(8,128)(2,1)S(1)}, u32[]{:S(2)}, u32[]{:S(2)}) collective-permute-start(bf16[256,1024]{1,0:T(8,128)(2,1)S(1)} %convolution_convert_fusion.1.h_ref), channel_id=1, source_target_pairs={{0,32},{32,0},{1,33},{33,1},{2,34},{34,2},{3,35},{35,3},{4,36},{36... | collective-permute-start | bytes 1572872 | tf_op jit(solution)/shard_map/ppermute | solution.py:34
  32.6 3.4 %collective-permute-start.1 = (bf16[256,512]{1,0:T(8,128)(2,1)S(1)}, bf16[256,512]{1,0:T(8,128)(2,1)S(1)}, u32[]{:S(2)}, u32[]{:S(2)}) collective-permute-start(bf16[256,512]{1,0:T(8,128)(2,1)S(1)} %get-tuple-element.17), channel_id=1, source_target_pairs={{0,32},{32,0},{1,33},{33,1},{2,34},{34,2},{3,35},{35,3},{4,36},{36... | collective-permute-start | bytes 786440 | tf_op jit(solution)/shard_map/ppermute | solution.py:34
  36.0 0.7 copy-start.1
  37.8 1.0 copy-start.2
  41.4 13.0 %collective-permute-start.2 = (bf16[256,512]{1,0:T(8,128)(2,1)}, bf16[256,512]{1,0:T(8,128)(2,1)}, u32[]{:S(2)}, u32[]{:S(2)}) collective-permute-start(bf16[256,512]{1,0:T(8,128)(2,1)} %get-tuple-element.11), channel_id=1, source_target_pairs={{0,32},{32,0},{1,33},{33,1},{2,34},{34,2},{3,35},{35,3},{4,36},{36... | collective-permute-start | bytes 786440 | tf_op jit(solution)/shard_map/ppermute | solution.py:34
  47.1 6.9 %copy-start.8 = (bf16[128,1024]{1,0:T(8,128)(2,1)S(1)}, bf16[128,1024]{1,0:T(8,128)(2,1)}, u32[]{:S(2)}) copy-start(bf16[128,1024]{1,0:T(8,128)(2,1)} %copy-done.7) | copy-start | bytes 786436
  47.1 18.8 %all-to-all-start.2 = ((bf16[4,256,512]{2,1,0:T(8,128)(2,1)}), bf16[4,256,512]{2,1,0:T(8,128)(2,1)S(1)}, u32[]{:S(2)}, u32[]{:S(2)}) async-start(bf16[4,256,512]{2,1,0:T(8,128)(2,1)} %bitcast.2), calls=%async_computation.2 | async-start | bytes 2097152 | tf_op jit(solution)/shard_map/all_to_all | solution.py:136
  50.7 3.2 %copy-start.12 = (bf16[128,1024]{1,0:T(8,128)(2,1)S(1)}, bf16[128,1024]{1,0:T(8,128)(2,1)}, u32[]{:S(2)}) copy-start(bf16[128,1024]{1,0:T(8,128)(2,1)} %param.12) | copy-start | bytes 786436
  52.0 18.3 %collective-permute-start.3 = (bf16[256,1024]{1,0:T(8,128)(2,1)}, bf16[256,1024]{1,0:T(8,128)(2,1)}, u32[]{:S(2)}, u32[]{:S(2)}) collective-permute-start(bf16[256,1024]{1,0:T(8,128)(2,1)} %convolution_convert_fusion), channel_id=1, source_target_pairs={{0,32},{32,0},{1,33},{33,1},{2,34},{34,2},{3,35},{35,3},{4,36},{36... | collective-permute-start | bytes 1572872 | tf_op jit(solution)/shard_map/ppermute | solution.py:34
  66.8 5.1 %copy-start.4 = (f32[2,128,3,128]{1,0,3,2:T(2,128)S(1)}, f32[2,128,3,128]{1,0,3,2:T(2,128)}, u32[]{:S(2)}) copy-start(f32[2,128,3,128]{1,0,3,2:T(2,128)} %copy-done.3) | copy-start | bytes 1179652
  66.8 14.1 %all-to-all-start.3 = ((bf16[8,32,512]{2,1,0:T(8,128)(2,1)}), bf16[8,32,512]{2,1,0:T(8,128)(2,1)S(1)}, u32[]{:S(2)}, u32[]{:S(2)}) async-start(bf16[8,32,512]{2,1,0:T(8,128)(2,1)} %bitcast.3), calls=%async_computation.3 | async-start | bytes 524288 | tf_op jit(solution)/shard_map/all_to_all | solution.py:158
  72.7 12.1 %copy-start.5 = (bf16[256,512]{1,0:T(8,128)(2,1)S(1)}, bf16[256,512]{1,0:T(8,128)(2,1)}, u32[]{:S(2)}) copy-start(bf16[256,512]{1,0:T(8,128)(2,1)} %get-tuple-element.15) | copy-start | bytes 786436
  72.7 12.1 %copy-start.6 = (bf16[256,512]{1,0:T(8,128)(2,1)S(1)}, bf16[256,512]{1,0:T(8,128)(2,1)}, u32[]{:S(2)}) copy-start(bf16[256,512]{1,0:T(8,128)(2,1)} %get-tuple-element.16) | copy-start | bytes 786436
  80.9 33.3 %all-to-all-start.4 = ((bf16[32,8,1024]{2,1,0:T(8,128)(2,1)}), bf16[32,8,1024]{2,1,0:T(8,128)(2,1)S(1)}, u32[]{:S(2)}, u32[]{:S(2)}) async-start(bf16[32,8,1024]{2,1,0:T(8,128)(2,1)} %pad_maximum_fusion.1), calls=%async_computation.4 | async-start | bytes 1048576 | tf_op jit(solution)/shard_map/all_to_all | solution.py:163

commit v4 on v2

--- a/solution.py
+++ b/solution.py
@@ -2,6 +2,7 @@
 import jax.numpy as jnp
 from jax import lax
 from jax.experimental import pallas as pl
+from jax.experimental.pallas import tpu as pltpu
 from jax.sharding import Mesh
 from jax.sharding import PartitionSpec as P
 
@@ -45,32 +46,89 @@
     )
 
 
-def core_products(hidden, hidden_peer, grad, grad_peer, w):
+def kernel(body, flops, moved, mib, *shapes):
+    return pl.pallas_call(
+        body,
+        out_shape=tuple(jax.ShapeDtypeStruct(*shape) for shape in shapes),
+        cost_estimate=pl.CostEstimate(flops=flops, bytes_accessed=moved, transcendentals=0),
+        compiler_params=pltpu.CompilerParams(vmem_limit_bytes=mib * 2**20),
+    )
+
+
+def pre_grad(h, g, w):
+    activ, slope = silu_parts(dot(h, w, 1, 0))
+    return activ, (g.astype(jnp.float32) * slope).astype(BF)
+
+
+def weight_products(hidden, grad, peer, w):
     rows, width = grad.shape
     depth = hidden.shape[1]
 
-    def body(h_ref, hp_ref, g_ref, gp_ref, w_ref, act_ref, actp_ref, pre_ref, prep_ref, part_ref):
+    def body(h_ref, g_ref, peer_ref, w_ref, part_ref):
         w_all = w_ref[...]
-        for h, g, a, p in (
-            (h_ref, g_ref, act_ref, pre_ref),
-            (hp_ref, gp_ref, actp_ref, prep_ref),
-        ):
-            activ, slope = silu_parts(dot(h[...], w_all, 1, 0))
-            a[...] = activ.astype(BF)
-            p[...] = (g[...].astype(jnp.float32) * slope).astype(BF)
-        part_ref[...] = (
-            dot(h_ref[...], pre_ref[...], 0, 0) + dot(hp_ref[...], prep_ref[...], 0, 0)
-        ).astype(BF)
-
-    small = jax.ShapeDtypeStruct((rows, width), BF)
-    return pl.pallas_call(
+        pre = pre_grad(h_ref[...], g_ref[...], w_all)[1]
+        total = dot(h_ref[...], pre, 0, 0)
+        pre = pre_grad(peer_ref[:, :depth], peer_ref[:, depth:], w_all)[1]
+        part_ref[...] = (total + dot(peer_ref[:, :depth], pre, 0, 0)).astype(BF)
+
+    return kernel(
+        body, 8 * rows * depth * width, 6 * depth * width, 16, ((depth, width), BF)
+    )(hidden, grad, peer, w)[0]
+
+
+def row_products(hidden, grad, peer, w):
+    rows, depth = hidden.shape
+    width = w.shape[1]
+
+    def body(h_ref, g_ref, peer_ref, w_ref, act_ref, actp_ref, hid_ref, hidp_ref):
+        w_all = w_ref[...]
+        activ, pre = pre_grad(peer_ref[:, :depth], peer_ref[:, depth:], w_all)
+        actp_ref[...] = activ.astype(BF)
+        hidp_ref[...] = dot(pre, w_all, 1, 1).astype(BF)
+        activ, pre = pre_grad(h_ref[...], g_ref[...], w_all)
+        act_ref[...] = activ.astype(BF)
+        hid_ref[...] = dot(pre, w_all, 1, 1)
+
+    return kernel(
         body,
-        out_shape=(small, small, small, small, jax.ShapeDtypeStruct((depth, width), BF)),
-        cost_estimate=pl.CostEstimate(
-            flops=8 * rows * depth * width, bytes_accessed=6 * depth * width, transcendentals=0
-        ),
-        name="core_products",
-    )(hidden, hidden_peer, grad, grad_peer, w)
+        16 * rows * depth * width,
+        6 * depth * width,
+        16,
+        ((rows, width), BF),
+        ((rows, width), BF),
+        ((rows, depth), jnp.float32),
+        ((rows, depth), BF),
+    )(hidden, grad, peer, w)
+
+
+def finish(stack, riders):
+    members, block, half_w = stack.shape
+    peers, both, width = riders.shape
+    slots = both // 2
+
+    def body(stack_ref, riders_ref, grad_ref, rows_ref, grads_ref):
+        for core in (0, 1):
+            total = stack_ref[core].astype(jnp.float32)
+            for plane in range(1, members // 2):
+                total = total + stack_ref[2 * plane + core].astype(jnp.float32)
+            grad_ref[:, core * half_w : (core + 1) * half_w] = total
+        flat = riders_ref[...]
+        row = lax.broadcasted_iota(jnp.int32, (peers * slots, peers * both), 0)
+        place = lax.broadcasted_iota(jnp.int32, (peers * slots, peers * both), 1)
+        wanted = row + lax.div(row, slots) * slots
+        for kind, out in enumerate((rows_ref, grads_ref)):
+            pick = jnp.where(place == wanted + kind * slots, 1.0, 0.0).astype(BF)
+            out[...] = dot(pick, flat, 1, 0).astype(BF)
+
+    return kernel(
+        body,
+        4 * peers * slots * peers * both * width,
+        members * block * half_w * 2,
+        12,
+        ((block, 2 * half_w), jnp.float32),
+        ((peers * slots, width), BF),
+        ((peers * slots, width), BF),
+    )(stack, riders.reshape(peers * both, width))
 
 
 def local(
@@ -88,7 +146,7 @@
     send_rows,
 ):
     first = lax.axis_index("core") == 0
-    nx, ny, nz = lax.axis_size("dx"), lax.axis_size("dy"), lax.axis_size("z")
+    nx, ny = lax.axis_size("dx"), lax.axis_size("dy")
     tile_slots = tile_values.shape[1]
     cluster_rows = tile_values.shape[2]
     slots = send_rows.shape[1]
@@ -99,8 +157,10 @@
         copies = jnp.broadcast_to(value[None], (count, *value.shape))
         return lax.all_to_all(copies, axis, split_axis=0, concat_axis=0, tiled=True)
 
-    my_cols = halves(weight, first)[0]
-    column = spread(my_cols, "dy", ny).reshape(ny * block, half_w)
+    copies = jnp.broadcast_to(weight[None], (ny, *weight.shape))
+    copies = lax.dynamic_slice_in_dim(copies, lax.axis_index("core") * half_w, half_w, axis=2)
+    column = lax.all_to_all(copies, "dy", split_axis=0, concat_axis=0, tiled=True)
+    column = column.reshape(ny * block, half_w)
     w = spread(column, "dx", nx).reshape(nx * ny * block, half_w)
 
     local_rows = jnp.concatenate(
@@ -122,22 +182,19 @@
     hidden = jnp.dot(operator, source.astype(jnp.float32), precision=lax.Precision.HIGHEST)
     hidden = hidden.astype(BF)
     grad_mine, grad_give = halves(out_grad, first)
-    hidden_peer = swap_core(hidden)
-    grad_peer = swap_core(grad_give)
+    peer = swap_core(jnp.concatenate([hidden, grad_give], axis=1))
     sends = send_rows.reshape(-1)
     row_ids = jnp.arange(row_count, dtype=jnp.int32)
     outgoing = dot((sends[:, None] == row_ids[None, :]).astype(BF), local_rows, 1, 0).astype(BF)
 
-    act_mine, act_give, pre_mine, pre_peer, part = core_products(
-        hidden, hidden_peer, grad_mine, grad_peer, w
-    )
+    part = weight_products(hidden, grad_mine, peer, w)
     got_x = lax.all_to_all(
         part.reshape(nx, ny * block, half_w), "dx", split_axis=0, concat_axis=0, tiled=True
     )
 
-    hid_give = dot(pre_peer, w, 1, 1).astype(BF)
+    act_mine, act_give, hid_mine, hid_give = row_products(hidden, grad_mine, peer, w)
     hid_got = swap_core(hid_give)
-    hid_grad = (dot(pre_mine, w, 1, 1) + hid_got.astype(jnp.float32)).astype(BF)
+    hid_grad = (hid_mine + hid_got.astype(jnp.float32)).astype(BF)
     act_got = swap_core(act_give)
     activations = ordered(act_mine, act_got, first)
     src_grad = lax.dot_general(
@@ -155,14 +212,9 @@
     summed = jnp.sum(got_x.astype(jnp.float32), axis=0).astype(BF).reshape(ny, block, half_w)
     got_y = lax.all_to_all(summed, "dy", split_axis=0, concat_axis=0, tiled=True)
     total = jnp.sum(got_y.astype(jnp.float32), axis=0)
-    for reach in (1, -1, 3):
-        pairs = [(i, (i + (reach if i % 2 == 0 else -reach)) % nz) for i in range(nz)]
-        total = total + lax.ppermute(total, "z", pairs)
+    stack = lax.all_gather(total.astype(BF), ("z", "core"))
     got_r = lax.all_to_all(riders, DOM, split_axis=0, concat_axis=0, tiled=True)
-    next_rows = got_r[:, :slots].reshape(peers * slots, -1)
-    next_grads = got_r[:, slots:].reshape(peers * slots, -1)
-
-    weight_grad = ordered(total, swap_core(total), first)
+    weight_grad, next_rows, next_grads = finish(stack, got_r)
 
     placing = row_ids[:, None] == sends[None, :]
     returned = dot(placing.astype(BF), stale_grads, 1, 0)

time: 114 us -> 114 us (level)
  blocking collectives: 0 us -> 23.4 us
  starting transfers between devices: 64.1 us -> 50.1 us
  waiting for transfers between devices: 20.9 us -> 14.1 us
  matrix products: 6.97 us -> 4.21 us
  other arithmetic: 9.83 us -> 8.08 us
  Pallas kernels: 4.35 us -> 5.69 us
    all_gather x0 -> x1, blocking collectives: none -> 23.4 us  [local(): stack = lax.all_gather(total.astype(BF), ('z', 'core'))]
    ppermute x3 -> x0, starting transfers between devices: 15.6 us -> none  [local(): total = total + lax.ppermute(total, 'z', pairs)]
    all_to_all x2 -> x1, starting transfers between devices: 12.8 us -> 4.28 us  [spread(): return lax.all_to_all(copies, axis, split_axis=0, concat_axis=0, tiled=True)]
    ppermute x5 -> x3, starting transfers between devices: 22.3 us -> 14.2 us  [swap_core(): return lax.ppermute(value, 'core', SWAP)]
    all_to_all x0 -> x1, starting transfers between devices: none -> 7.77 us  [local(): lax.all_to_all(copies, 'dy', split_axis=0, concat_axis=0, tiled=True)]
    all_to_all x1, starting transfers between devices: 5.77 us -> 12.1 us  [local(): lax.all_to_all(summed, 'dy', split_axis=0, concat_axis=0, tiled=True)]
    all_to_all x1, waiting for transfers between devices: 6.88 us -> 0.61 us  [local(): lax.all_to_all(summed, 'dy', split_axis=0, concat_axis=0, tiled=True)]
    ppermute x3 -> x0, waiting for transfers between devices: 4.44 us -> none  [local(): total = total + lax.ppermute(total, 'z', pairs)]
  transfers between devices with their start and end apart: 13 -> 8, of which waited for: 6 -> 3; matrix products, arithmetic and copies ran while one was open for 15% -> 12% of each run, Pallas kernels for 0% -> 2%
where the time goes in v4:
time: 114 us; the launch traced here: 113 us
  starting transfers between devices  50.1 us (44%)
  blocking collectives  23.4 us (21%)
  waiting for transfers between devices  14.1 us (12%)
  other arithmetic  8.08 us (7%)
  local copies, waits for them, and re-layouts  6.72 us (6%)
  Pallas kernels  5.69 us (5%)
  matrix products  4.21 us (4%)
    all_gather x1, blocking collectives, local(): stack = lax.all_gather(total.astype(BF), ('z', 'core'))  23.4 us
    ppermute x3, starting transfers between devices, swap_core(): return lax.ppermute(value, 'core', SWAP)  14.2 us
    all_to_all x1, waiting for transfers between devices, spread(): return lax.all_to_all(copies, axis, split_axis=0, concat_axis=0, tiled=True)  12.3 us
    all_to_all x1, starting transfers between devices, local(): lax.all_to_all(summed, 'dy', split_axis=0, concat_axis=0, tiled=True)  12.1 us
    all_to_all x1, starting transfers between devices, local(): lax.all_to_all(copies, 'dy', split_axis=0, concat_axis=0, tiled=True)  7.77 us
    all_to_all x1, starting transfers between devices, local(): got_r = lax.all_to_all(riders, DOM, split_axis=0, concat_axis=0, tiled=True)  7.44 us
    all_to_all x1, starting transfers between devices, spread(): return lax.all_to_all(copies, axis, split_axis=0, concat_axis=0, tiled=True)  4.28 us
    all_to_all x1, starting transfers between devices, local(): lax.all_to_all(part.reshape(nx, ny * block, half_w), 'dx', split_axis=0,...  4.26 us
  transfers between devices with their start and end apart: 8, of which 3 were waited for; matrix products, arithmetic and copies ran while one was open for 12% of the time, Pallas kernels for 2%

profile of v4, /device:TPU:1, one launch (start us, length us, event | category | flops | bytes accessed | tf_op | source)
XLA Modules:
  0.0 113.3 jit_solution(14994186006775079544)
XLA Ops:
  0.6 0.0 copy-start
  0.6 0.0 copy-start.14
  0.7 0.0 copy-start.15
  0.7 0.0 copy-start.10
  0.7 0.8 constant_dynamic-slice_fusion
  1.5 0.7 broadcast_in_dim.76
  2.2 7.8 %all-to-all-start = ((bf16[8,32,512]{2,1,0:T(8,128)(2,1)}), bf16[8,32,512]{2,1,0:T(8,128)(2,1)S(1)}, u32[]{:S(2)}, u32[]{:S(2)}) async-start(bf16[8,32,512]{2,1,0:T(8,128)(2,1)} %broadcast_in_dim.76), calls=%async_computation | async-start | bytes 524288 | tf_op jit(solution)/shard_map/all_to_all | solution.py:162
  10.0 0.7 iota_compare_fusion.8
  10.7 0.8 iota_compare_fusion.7
  11.5 1.0 select_convert_fusion
  12.5 0.1 select_reduce_fusion
  12.7 0.2 copy.19
  12.9 0.0 copy-done.14
  12.9 0.0 copy-done.15
  12.9 0.0 copy-start.7
  12.9 0.0 copy-start.9
  12.9 0.2 select_reduce_fusion.1
  13.1 0.0 copy-done.10
  13.1 0.1 multiply_convert_fusion
  13.2 0.0 copy-start.11
  13.2 0.4 copy-done.7
  13.6 0.0 copy-done.17
  13.7 1.0 convolution_convert_fusion.h_ref
  14.7 0.0 copy-done.9
  14.7 0.0 copy-done.11
  14.7 1.0 pad_maximum_fusion
  15.7 4.5 %collective-permute-start = (bf16[256,1536]{1,0:T(8,128)(2,1)}, bf16[256,1536]{1,0:T(8,128)(2,1)S(1)}, u32[]{:S(2)}, u32[]{:S(2)}) collective-permute-start(bf16[256,1536]{1,0:T(8,128)(2,1)} %pad_maximum_fusion), channel_id=1, source_target_pairs={{0,32},{32,0},{1,33},{33,1},{2,34},{34,2},{3,35},{35,3},{4,36},{36... | collective-permute-start | bytes 2359304 | tf_op jit(solution)/shard_map/ppermute | solution.py:34
  20.2 0.0 all-to-all-done
  20.2 1.1 broadcast_in_dim.78
  21.3 4.3 %all-to-all-start.1 = ((bf16[4,256,512]{2,1,0:T(8,128)(2,1)}), bf16[4,256,512]{2,1,0:T(8,128)(2,1)S(1)}, u32[]{:S(2)}, u32[]{:S(2)}) async-start(bf16[4,256,512]{2,1,0:T(8,128)(2,1)} %broadcast_in_dim.78), calls=%async_computation.1 | async-start | bytes 2097152 | tf_op jit(solution)/shard_map/all_to_all | solution.py:158
  25.6 0.0 collective-permute-done.peer_ref
  25.6 12.3 %all-to-all-done.1 = bf16[4,256,512]{2,1,0:T(8,128)(2,1)S(1)} async-done(((bf16[4,256,512]{2,1,0:T(8,128)(2,1)}), bf16[4,256,512]{2,1,0:T(8,128)(2,1)S(1)}, u32[]{:S(2)}, u32[]{:S(2)}) %all-to-all-start.1) | async-done | bytes 1048608 | tf_op jit(solution)/shard_map/all_to_all | solution.py:158
  37.9 2.5 %shard_map.156 = bf16[1024,512]{1,0:T(8,128)(2,1)} custom-call(bf16[256,1024]{1,0:T(8,128)(2,1)S(1)} %convolution_convert_fusion.h_ref, bf16[256,512]{1,0:T(8,128)(2,1)S(1)} %get-tuple-element.22.g_ref, bf16[256,1536]{1,0:T(8,128)(2,1)S(1)} %collective-permute-done.peer_ref, bf16[1024,512]{1,0:T(8,128)(2,1)S(1)} %bitcast.18), custom_call_target="tpu_custom_call" | custom-call | flops 1073741824 | bytes 3145728 | tf_op jit(solution)/shard_map/pallas_call | solution.py:74
  40.4 0.0 copy-done.1
  40.4 4.3 %all-to-all-start.2 = ((bf16[4,256,512]{2,1,0:T(8,128)(2,1)}), bf16[4,256,512]{2,1,0:T(8,128)(2,1)}, u32[]{:S(2)}, u32[]{:S(2)}) async-start(bf16[4,256,512]{2,1,0:T(8,128)(2,1)} %bitcast.2), calls=%async_computation.2 | async-start | bytes 2097152 | tf_op jit(solution)/shard_map/all_to_all | solution.py:191
  44.6 0.0 copy-start.2
  44.6 1.1 copy-done.2
  45.8 2.1 %shard_map.155 = (bf16[256,512]{1,0:T(8,128)(2,1)S(1)}, bf16[256,512]{1,0:T(8,128)(2,1)S(1)}, f32[256,1024]{1,0:T(8,128)S(1)}, bf16[256,1024]{1,0:T(8,128)(2,1)}) custom-call(bf16[256,1024]{1,0:T(8,128)(2,1)S(1)} %convolution_convert_fusion.h_ref, bf16[256,512]{1,0:T(8,128)(2,1)S(1)} %get-tuple-element.22.g_ref, bf16[256,1536]{1,0:T(8,128)(2,1)S(1)} %copy-done.2, ...), custom_call_target="tpu_custom_call" | custom-call | flops 2147483648 | bytes 3145728 | tf_op jit(solution)/shard_map/pallas_call | solution.py:92
  47.9 0.7 copy-done.3
  48.6 5.8 %collective-permute-start.2 = (bf16[256,1024]{1,0:T(8,128)(2,1)}, bf16[256,1024]{1,0:T(8,128)(2,1)}, u32[]{:S(2)}, u32[]{:S(2)}) collective-permute-start(bf16[256,1024]{1,0:T(8,128)(2,1)} %get-tuple-element.15), channel_id=1, source_target_pairs={{0,32},{32,0},{1,33},{33,1},{2,34},{34,2},{3,35},{35,3},{4,36},{36... | collective-permute-start | bytes 1572872 | tf_op jit(solution)/shard_map/ppermute | solution.py:34
  54.4 0.0 copy-done.13
  54.4 0.1 copy.20
  54.5 0.1 eq.69
  54.6 0.0 copy-start.4
  54.6 0.0 copy-start.8
  54.6 1.2 %all-to-all-done.2 = bf16[4,256,512]{2,1,0:T(8,128)(2,1)} async-done(((bf16[4,256,512]{2,1,0:T(8,128)(2,1)}), bf16[4,256,512]{2,1,0:T(8,128)(2,1)}, u32[]{:S(2)}, u32[]{:S(2)}) %all-to-all-start.2) | async-done | bytes 1048608 | tf_op jit(solution)/shard_map/all_to_all | solution.py:191
  55.8 2.2 %reduce_sum.44 = bf16[256,512]{1,0:T(8,128)(2,1)} reduce(bf16[4,256,512]{2,1,0:T(8,128)(2,1)} %all-to-all-done.2, bf16[]{:T(256)} %constant.15.clone.1), dimensions={0}, to_apply=%region_2.3 | reduce | flops 393216 | bytes 1310722 | tf_op jit(solution)/shard_map/reduce_sum | solution.py:212
  58.0 12.1 %all-to-all-start.3 = ((bf16[8,32,512]{2,1,0:T(8,128)(2,1)}), bf16[8,32,512]{2,1,0:T(8,128)(2,1)S(1)}, u32[]{:S(2)}, u32[]{:S(2)}) async-start(bf16[8,32,512]{2,1,0:T(8,128)(2,1)} %bitcast.3), calls=%async_computation.3 | async-start | bytes 524288 | tf_op jit(solution)/shard_map/all_to_all | solution.py:213
  70.1 0.3 convolution_convert_fusion.1
  70.4 0.1 reshape.70
  70.5 3.9 %collective-permute-start.1 = (bf16[256,512]{1,0:T(8,128)(2,1)S(1)}, bf16[256,512]{1,0:T(8,128)(2,1)S(1)}, u32[]{:S(2)}, u32[]{:S(2)}) collective-permute-start(bf16[256,512]{1,0:T(8,128)(2,1)S(1)} %copy-done.4), channel_id=1, source_target_pairs={{0,32},{32,0},{1,33},{33,1},{2,34},{34,2},{3,35},{35,3},{4,36},{36... | collective-permute-start | bytes 786440 | tf_op jit(solution)/shard_map/ppermute | solution.py:34
  74.4 0.0 collective-permute-done.2
  74.5 1.8 %fusion.6 = f32[384,1024]{1,0:T(8,128)S(1)} fusion(f32[256,1024]{1,0:T(8,128)S(1)} %get-tuple-element.14, bf16[256,1024]{1,0:T(8,128)(2,1)} %collective-permute-done.2, f32[48,8,2,128]{3,2,1,0:T(2,128)S(1)} %bitcast.21), kind=kOutput, calls=%fused_computation.12 | convolution fusion | flops 1208745984 | bytes 3538944 | tf_op jit(solution)/shard_map/dot_general | solution.py:200
  76.3 1.1 %copy-done.5 = f32[384,1024]{1,0:T(8,128)} copy-done((f32[384,1024]{1,0:T(8,128)}, f32[384,1024]{1,0:T(8,128)S(1)}, u32[]{:S(2)}) %copy-start.5) | copy-done | bytes 1572888
  77.5 0.1 reshape.71
  77.6 1.1 pad_maximum_fusion.2
  78.7 0.6 all-to-all-done.3
  79.3 7.4 %all-to-all-start.4 = ((bf16[32,8,1024]{2,1,0:T(8,128)(2,1)}), bf16[32,8,1024]{2,1,0:T(8,128)(2,1)S(1)}, u32[]{:S(2)}, u32[]{:S(2)}) async-start(bf16[32,8,1024]{2,1,0:T(8,128)(2,1)} %pad_maximum_fusion.2), calls=%async_computation.4 | async-start | bytes 1048576 | tf_op jit(solution)/shard_map/all_to_all | solution.py:216
  86.7 0.0 collective-permute-done.1
  86.8 0.9 pad_maximum_fusion.1
  87.7 1.1 fusion
  88.8 23.4 %all-gather = bf16[512,512]{1,0:T(8,128)(2,1)S(1)} all-gather(bf16[32,512]{1,0:T(8,128)(2,1)S(1)} %reduce_sum.45), channel_id=2, replica_groups=mesh['z'=8,'core'=2,'dx'=4,'dy'=8] {'z','core'}, dimensions={0}, use_global_device_ids=true | all-gather | bytes 557056 | tf_op jit(solution)/shard_map/all_gather | solution.py:215
  112.2 0.0 all-to-all-done.4
  112.2 1.1 shard_map.157
  (20 shorter events, 0.2 us)
Async XLA Ops:
  0.6 87.0 %copy-start = (bf16[128,1024]{1,0:T(8,128)(2,1)S(1)}, bf16[128,1024]{1,0:T(8,128)(2,1)}, u32[]{:S(2)}) copy-start(bf16[128,1024]{1,0:T(8,128)(2,1)} %param.22) | copy-start | bytes 786436
  0.6 12.2 %copy-start.14 = (f32[256]{0:T(256)S(1)}, f32[256]{0:T(256)}, u32[]{:S(2)}) copy-start(f32[256]{0:T(256)} %param.15) | copy-start | bytes 3076
  0.7 12.2 %copy-start.15 = (s32[128]{0:T(128)S(1)}, s32[128]{0:T(128)}, u32[]{:S(2)}) copy-start(s32[128]{0:T(128)} %param.14) | copy-start | bytes 1540
  0.7 12.4 %copy-start.10 = (bf16[128,1024]{1,0:T(8,128)(2,1)S(1)}, bf16[128,1024]{1,0:T(8,128)(2,1)}, u32[]{:S(2)}) copy-start(bf16[128,1024]{1,0:T(8,128)(2,1)} %param.13) | copy-start | bytes 786436
  2.2 11.4 %copy-start.16 = (bf16[128,1024]{1,0:T(8,128)(2,1)S(1)}, bf16[128,1024]{1,0:T(8,128)(2,1)}, u32[]{:S(2)}) copy-start(bf16[128,1024]{1,0:T(8,128)(2,1)} %param.16) | copy-start | bytes 786436
  2.2 11.4 %copy-start.17 = (bf16[128,1024]{1,0:T(8,128)(2,1)S(1)}, bf16[128,1024]{1,0:T(8,128)(2,1)}, u32[]{:S(2)}) copy-start(bf16[128,1024]{1,0:T(8,128)(2,1)} %param.12) | copy-start | bytes 786436
  2.2 18.0 %all-to-all-start = ((bf16[8,32,512]{2,1,0:T(8,128)(2,1)}), bf16[8,32,512]{2,1,0:T(8,128)(2,1)S(1)}, u32[]{:S(2)}, u32[]{:S(2)}) async-start(bf16[8,32,512]{2,1,0:T(8,128)(2,1)} %broadcast_in_dim.76), calls=%async_computation | async-start | bytes 524288 | tf_op jit(solution)/shard_map/all_to_all | solution.py:162
  12.9 0.7 copy-start.7
  12.9 1.8 %copy-start.9 = (bf16[256,1024]{1,0:T(8,128)(2,1)S(1)}, bf16[256,1024]{1,0:T(8,128)(2,1)}, u32[]{:S(2)}) copy-start(bf16[256,1024]{1,0:T(8,128)(2,1)} %param.21) | copy-start | bytes 1572868
  13.2 1.5 %copy-start.11 = (bf16[128,1024]{1,0:T(8,128)(2,1)}, bf16[128,1024]{1,0:T(8,128)(2,1)S(1)}, u32[]{:S(2)}) copy-start(bf16[128,1024]{1,0:T(8,128)(2,1)S(1)} %multiply_convert_fusion) | copy-start | bytes 786436
  15.7 9.9 %collective-permute-start = (bf16[256,1536]{1,0:T(8,128)(2,1)}, bf16[256,1536]{1,0:T(8,128)(2,1)S(1)}, u32[]{:S(2)}, u32[]{:S(2)}) collective-permute-start(bf16[256,1536]{1,0:T(8,128)(2,1)} %pad_maximum_fusion), channel_id=1, source_target_pairs={{0,32},{32,0},{1,33},{33,1},{2,34},{34,2},{3,35},{35,3},{4,36},{36... | collective-permute-start | bytes 2359304 | tf_op jit(solution)/shard_map/ppermute | solution.py:34
  21.3 16.6 %all-to-all-start.1 = ((bf16[4,256,512]{2,1,0:T(8,128)(2,1)}), bf16[4,256,512]{2,1,0:T(8,128)(2,1)S(1)}, u32[]{:S(2)}, u32[]{:S(2)}) async-start(bf16[4,256,512]{2,1,0:T(8,128)(2,1)} %broadcast_in_dim.78), calls=%async_computation.1 | async-start | bytes 2097152 | tf_op jit(solution)/shard_map/all_to_all | solution.py:158
  25.6 14.8 %copy-start.1 = (bf16[256,1536]{1,0:T(8,128)(2,1)}, bf16[256,1536]{1,0:T(8,128)(2,1)S(1)}, u32[]{:S(2)}) copy-start(bf16[256,1536]{1,0:T(8,128)(2,1)S(1)} %collective-permute-done.peer_ref) | copy-start | bytes 2359300
  40.4 15.5 %all-to-all-start.2 = ((bf16[4,256,512]{2,1,0:T(8,128)(2,1)}), bf16[4,256,512]{2,1,0:T(8,128)(2,1)}, u32[]{:S(2)}, u32[]{:S(2)}) async-start(bf16[4,256,512]{2,1,0:T(8,128)(2,1)} %bitcast.2), calls=%async_computation.2 | async-start | bytes 2097152 | tf_op jit(solution)/shard_map/all_to_all | solution.py:191
  44.6 1.1 %copy-start.2 = (bf16[256,1536]{1,0:T(8,128)(2,1)S(1)}, bf16[256,1536]{1,0:T(8,128)(2,1)}, u32[]{:S(2)}) copy-start(bf16[256,1536]{1,0:T(8,128)(2,1)} %copy-done.1) | copy-start | bytes 2359300
  45.8 8.6 %copy-start.13 = (s32[32,4]{0,1:T(4,128)S(1)}, s32[32,4]{0,1:T(4,128)}, u32[]{:S(2)}) copy-start(s32[32,4]{0,1:T(4,128)} %param.23) | copy-start | bytes 1540
  47.9 0.7 copy-start.3
  48.6 21.5 %copy-start.12 = (bf16[128,1024]{1,0:T(8,128)(2,1)S(1)}, bf16[128,1024]{1,0:T(8,128)(2,1)}, u32[]{:S(2)}) copy-start(bf16[128,1024]{1,0:T(8,128)(2,1)} %copy-done.11) | copy-start | bytes 786436
  48.6 21.5 %copy-start.18 = (bf16[128,1024]{1,0:T(8,128)(2,1)S(1)}, bf16[128,1024]{1,0:T(8,128)(2,1)}, u32[]{:S(2)}) copy-start(bf16[128,1024]{1,0:T(8,128)(2,1)} %param.12) | copy-start | bytes 786436
  48.6 25.8 %collective-permute-start.2 = (bf16[256,1024]{1,0:T(8,128)(2,1)}, bf16[256,1024]{1,0:T(8,128)(2,1)}, u32[]{:S(2)}, u32[]{:S(2)}) collective-permute-start(bf16[256,1024]{1,0:T(8,128)(2,1)} %get-tuple-element.15), channel_id=1, source_target_pairs={{0,32},{32,0},{1,33},{33,1},{2,34},{34,2},{3,35},{35,3},{4,36},{36... | collective-permute-start | bytes 1572872 | tf_op jit(solution)/shard_map/ppermute | solution.py:34
  54.6 15.9 %copy-start.4 = (bf16[256,512]{1,0:T(8,128)(2,1)S(1)}, bf16[256,512]{1,0:T(8,128)(2,1)}, u32[]{:S(2)}) copy-start(bf16[256,512]{1,0:T(8,128)(2,1)} %copy-done.3) | copy-start | bytes 786436
  54.6 19.8 %copy-start.8 = (f32[2,128,3,128]{1,0,3,2:T(2,128)S(1)}, f32[2,128,3,128]{1,0,3,2:T(2,128)}, u32[]{:S(2)}) copy-start(f32[2,128,3,128]{1,0,3,2:T(2,128)} %copy-done.7) | copy-start | bytes 1179652
  58.0 21.3 %all-to-all-start.3 = ((bf16[8,32,512]{2,1,0:T(8,128)(2,1)}), bf16[8,32,512]{2,1,0:T(8,128)(2,1)S(1)}, u32[]{:S(2)}, u32[]{:S(2)}) async-start(bf16[8,32,512]{2,1,0:T(8,128)(2,1)} %bitcast.3), calls=%async_computation.3 | async-start | bytes 524288 | tf_op jit(solution)/shard_map/all_to_all | solution.py:213
  70.5 16.2 %collective-permute-start.1 = (bf16[256,512]{1,0:T(8,128)(2,1)S(1)}, bf16[256,512]{1,0:T(8,128)(2,1)S(1)}, u32[]{:S(2)}, u32[]{:S(2)}) collective-permute-start(bf16[256,512]{1,0:T(8,128)(2,1)S(1)} %copy-done.4), channel_id=1, source_target_pairs={{0,32},{32,0},{1,33},{33,1},{2,34},{34,2},{3,35},{35,3},{4,36},{36... | collective-permute-start | bytes 786440 | tf_op jit(solution)/shard_map/ppermute | solution.py:34
  76.3 1.2 %copy-start.5 = (f32[384,1024]{1,0:T(8,128)}, f32[384,1024]{1,0:T(8,128)S(1)}, u32[]{:S(2)}) copy-start(f32[384,1024]{1,0:T(8,128)S(1)} %fusion.6) | copy-start | bytes 4718596
  78.7 9.0 %copy-start.6 = (f32[384,1024]{1,0:T(8,128)S(1)}, f32[384,1024]{1,0:T(8,128)}, u32[]{:S(2)}) copy-start(f32[384,1024]{1,0:T(8,128)} %copy-done.5) | copy-start | bytes 4718596
  79.3 32.9 %all-to-all-start.4 = ((bf16[32,8,1024]{2,1,0:T(8,128)(2,1)}), bf16[32,8,1024]{2,1,0:T(8,128)(2,1)S(1)}, u32[]{:S(2)}, u32[]{:S(2)}) async-start(bf16[32,8,1024]{2,1,0:T(8,128)(2,1)} %pad_maximum_fusion.2), calls=%async_computation.4 | async-start | bytes 1048576 | tf_op jit(solution)/shard_map/all_to_all | solution.py:216

commit v5 on v4

--- a/solution.py
+++ b/solution.py
@@ -72,7 +72,7 @@
         part_ref[...] = (total + dot(peer_ref[:, :depth], pre, 0, 0)).astype(BF)
 
     return kernel(
-        body, 8 * rows * depth * width, 6 * depth * width, 16, ((depth, width), BF)
+        body, 8 * rows * depth * width, 6 * depth * width, 8, ((depth, width), BF)
     )(hidden, grad, peer, w)[0]
 
 
@@ -93,7 +93,7 @@
         body,
         16 * rows * depth * width,
         6 * depth * width,
-        16,
+        8,
         ((rows, width), BF),
         ((rows, width), BF),
         ((rows, depth), jnp.float32),
@@ -124,7 +124,7 @@
         body,
         4 * peers * slots * peers * both * width,
         members * block * half_w * 2,
-        12,
+        6,
         ((block, 2 * half_w), jnp.float32),
         ((peers * slots, width), BF),
         ((peers * slots, width), BF),

time: 114 us -> 114 us (level)
  no operation moved by 1% of the time
where the time goes in v5:
time: 114 us; the launch traced here: 113 us
  starting transfers between devices  50.1 us (44%)
  blocking collectives  23.4 us (21%)
  waiting for transfers between devices  14.1 us (12%)
  other arithmetic  8.08 us (7%)
  local copies, waits for them, and re-layouts  6.72 us (6%)
  Pallas kernels  5.69 us (5%)
  matrix products  4.21 us (4%)
    all_gather x1, blocking collectives, local(): stack = lax.all_gather(total.astype(BF), ('z', 'core'))  23.4 us
    ppermute x3, starting transfers between devices, swap_core(): return lax.ppermute(value, 'core', SWAP)  14.2 us
    all_to_all x1, waiting for transfers between devices, spread(): return lax.all_to_all(copies, axis, split_axis=0, concat_axis=0, tiled=True)  12.3 us
    all_to_all x1, starting transfers between devices, local(): lax.all_to_all(summed, 'dy', split_axis=0, concat_axis=0, tiled=True)  12.1 us
    all_to_all x1, starting transfers between devices, local(): lax.all_to_all(copies, 'dy', split_axis=0, concat_axis=0, tiled=True)  7.77 us
    all_to_all x1, starting transfers between devices, local(): got_r = lax.all_to_all(riders, DOM, split_axis=0, concat_axis=0, tiled=True)  7.44 us
    all_to_all x1, starting transfers between devices, spread(): return lax.all_to_all(copies, axis, split_axis=0, concat_axis=0, tiled=True)  4.28 us
    all_to_all x1, starting transfers between devices, local(): lax.all_to_all(part.reshape(nx, ny * block, half_w), 'dx', split_axis=0,...  4.26 us
  transfers between devices with their start and end apart: 8, of which 3 were waited for; matrix products, arithmetic and copies ran while one was open for 12% of the time, Pallas kernels for 2%

profile of v5, /device:TPU:1, one launch (start us, length us, event | category | flops | bytes accessed | tf_op | source)
XLA Modules:
  0.0 113.3 jit_solution(8685598562646155397)
XLA Ops:
  0.6 0.0 copy-start
  0.6 0.0 copy-start.14
  0.7 0.0 copy-start.15
  0.7 0.0 copy-start.10
  0.7 0.8 constant_dynamic-slice_fusion
  1.5 0.7 broadcast_in_dim.76
  2.2 7.8 %all-to-all-start = ((bf16[8,32,512]{2,1,0:T(8,128)(2,1)}), bf16[8,32,512]{2,1,0:T(8,128)(2,1)S(1)}, u32[]{:S(2)}, u32[]{:S(2)}) async-start(bf16[8,32,512]{2,1,0:T(8,128)(2,1)} %broadcast_in_dim.76), calls=%async_computation | async-start | bytes 524288 | tf_op jit(solution)/shard_map/all_to_all | solution.py:162
  10.0 0.7 iota_compare_fusion.8
  10.7 0.8 iota_compare_fusion.7
  11.5 1.0 select_convert_fusion
  12.5 0.1 select_reduce_fusion
  12.7 0.2 copy.19
  12.9 0.0 copy-done.14
  12.9 0.0 copy-done.15
  12.9 0.0 copy-start.7
  12.9 0.0 copy-start.9
  12.9 0.2 select_reduce_fusion.1
  13.1 0.0 copy-done.10
  13.1 0.1 multiply_convert_fusion
  13.2 0.0 copy-start.11
  13.2 0.4 copy-done.7
  13.6 0.0 copy-done.17
  13.7 1.0 convolution_convert_fusion.h_ref
  14.7 0.0 copy-done.9
  14.7 0.0 copy-done.11
  14.7 1.0 pad_maximum_fusion
  15.7 4.5 %collective-permute-start = (bf16[256,1536]{1,0:T(8,128)(2,1)}, bf16[256,1536]{1,0:T(8,128)(2,1)S(1)}, u32[]{:S(2)}, u32[]{:S(2)}) collective-permute-start(bf16[256,1536]{1,0:T(8,128)(2,1)} %pad_maximum_fusion), channel_id=1, source_target_pairs={{0,32},{32,0},{1,33},{33,1},{2,34},{34,2},{3,35},{35,3},{4,36},{36... | collective-permute-start | bytes 2359304 | tf_op jit(solution)/shard_map/ppermute | solution.py:34
  20.2 0.0 all-to-all-done
  20.2 1.1 broadcast_in_dim.78
  21.3 4.3 %all-to-all-start.1 = ((bf16[4,256,512]{2,1,0:T(8,128)(2,1)}), bf16[4,256,512]{2,1,0:T(8,128)(2,1)S(1)}, u32[]{:S(2)}, u32[]{:S(2)}) async-start(bf16[4,256,512]{2,1,0:T(8,128)(2,1)} %broadcast_in_dim.78), calls=%async_computation.1 | async-start | bytes 2097152 | tf_op jit(solution)/shard_map/all_to_all | solution.py:158
  25.6 0.0 collective-permute-done.peer_ref
  25.6 12.3 %all-to-all-done.1 = bf16[4,256,512]{2,1,0:T(8,128)(2,1)S(1)} async-done(((bf16[4,256,512]{2,1,0:T(8,128)(2,1)}), bf16[4,256,512]{2,1,0:T(8,128)(2,1)S(1)}, u32[]{:S(2)}, u32[]{:S(2)}) %all-to-all-start.1) | async-done | bytes 1048608 | tf_op jit(solution)/shard_map/all_to_all | solution.py:158
  37.9 2.5 %shard_map.156 = bf16[1024,512]{1,0:T(8,128)(2,1)} custom-call(bf16[256,1024]{1,0:T(8,128)(2,1)S(1)} %convolution_convert_fusion.h_ref, bf16[256,512]{1,0:T(8,128)(2,1)S(1)} %get-tuple-element.22.g_ref, bf16[256,1536]{1,0:T(8,128)(2,1)S(1)} %collective-permute-done.peer_ref, bf16[1024,512]{1,0:T(8,128)(2,1)S(1)} %bitcast.18), custom_call_target="tpu_custom_call" | custom-call | flops 1073741824 | bytes 3145728 | tf_op jit(solution)/shard_map/pallas_call | solution.py:74
  40.4 0.0 copy-done.1
  40.4 4.3 %all-to-all-start.2 = ((bf16[4,256,512]{2,1,0:T(8,128)(2,1)}), bf16[4,256,512]{2,1,0:T(8,128)(2,1)}, u32[]{:S(2)}, u32[]{:S(2)}) async-start(bf16[4,256,512]{2,1,0:T(8,128)(2,1)} %bitcast.2), calls=%async_computation.2 | async-start | bytes 2097152 | tf_op jit(solution)/shard_map/all_to_all | solution.py:191
  44.6 0.0 copy-start.2
  44.6 1.1 copy-done.2
  45.8 2.1 %shard_map.155 = (bf16[256,512]{1,0:T(8,128)(2,1)S(1)}, bf16[256,512]{1,0:T(8,128)(2,1)S(1)}, f32[256,1024]{1,0:T(8,128)S(1)}, bf16[256,1024]{1,0:T(8,128)(2,1)}) custom-call(bf16[256,1024]{1,0:T(8,128)(2,1)S(1)} %convolution_convert_fusion.h_ref, bf16[256,512]{1,0:T(8,128)(2,1)S(1)} %get-tuple-element.22.g_ref, bf16[256,1536]{1,0:T(8,128)(2,1)S(1)} %copy-done.2, ...), custom_call_target="tpu_custom_call" | custom-call | flops 2147483648 | bytes 3145728 | tf_op jit(solution)/shard_map/pallas_call | solution.py:92
  47.9 0.7 copy-done.3
  48.6 5.8 %collective-permute-start.2 = (bf16[256,1024]{1,0:T(8,128)(2,1)}, bf16[256,1024]{1,0:T(8,128)(2,1)}, u32[]{:S(2)}, u32[]{:S(2)}) collective-permute-start(bf16[256,1024]{1,0:T(8,128)(2,1)} %get-tuple-element.15), channel_id=1, source_target_pairs={{0,32},{32,0},{1,33},{33,1},{2,34},{34,2},{3,35},{35,3},{4,36},{36... | collective-permute-start | bytes 1572872 | tf_op jit(solution)/shard_map/ppermute | solution.py:34
  54.4 0.0 copy-done.13
  54.4 0.1 copy.20
  54.5 0.1 eq.69
  54.6 0.0 copy-start.4
  54.6 0.0 copy-start.8
  54.6 1.2 %all-to-all-done.2 = bf16[4,256,512]{2,1,0:T(8,128)(2,1)} async-done(((bf16[4,256,512]{2,1,0:T(8,128)(2,1)}), bf16[4,256,512]{2,1,0:T(8,128)(2,1)}, u32[]{:S(2)}, u32[]{:S(2)}) %all-to-all-start.2) | async-done | bytes 1048608 | tf_op jit(solution)/shard_map/all_to_all | solution.py:191
  55.8 2.2 %reduce_sum.44 = bf16[256,512]{1,0:T(8,128)(2,1)} reduce(bf16[4,256,512]{2,1,0:T(8,128)(2,1)} %all-to-all-done.2, bf16[]{:T(256)} %constant.15.clone.1), dimensions={0}, to_apply=%region_2.3 | reduce | flops 393216 | bytes 1310722 | tf_op jit(solution)/shard_map/reduce_sum | solution.py:212
  58.0 12.1 %all-to-all-start.3 = ((bf16[8,32,512]{2,1,0:T(8,128)(2,1)}), bf16[8,32,512]{2,1,0:T(8,128)(2,1)S(1)}, u32[]{:S(2)}, u32[]{:S(2)}) async-start(bf16[8,32,512]{2,1,0:T(8,128)(2,1)} %bitcast.3), calls=%async_computation.3 | async-start | bytes 524288 | tf_op jit(solution)/shard_map/all_to_all | solution.py:213
  70.1 0.3 convolution_convert_fusion.1
  70.4 0.1 reshape.70
  70.5 3.9 %collective-permute-start.1 = (bf16[256,512]{1,0:T(8,128)(2,1)S(1)}, bf16[256,512]{1,0:T(8,128)(2,1)S(1)}, u32[]{:S(2)}, u32[]{:S(2)}) collective-permute-start(bf16[256,512]{1,0:T(8,128)(2,1)S(1)} %copy-done.4), channel_id=1, source_target_pairs={{0,32},{32,0},{1,33},{33,1},{2,34},{34,2},{3,35},{35,3},{4,36},{36... | collective-permute-start | bytes 786440 | tf_op jit(solution)/shard_map/ppermute | solution.py:34
  74.4 0.0 collective-permute-done.2
  74.5 1.8 %fusion.6 = f32[384,1024]{1,0:T(8,128)S(1)} fusion(f32[256,1024]{1,0:T(8,128)S(1)} %get-tuple-element.14, bf16[256,1024]{1,0:T(8,128)(2,1)} %collective-permute-done.2, f32[48,8,2,128]{3,2,1,0:T(2,128)S(1)} %bitcast.21), kind=kOutput, calls=%fused_computation.12 | convolution fusion | flops 1208745984 | bytes 3538944 | tf_op jit(solution)/shard_map/dot_general | solution.py:200
  76.3 1.1 %copy-done.5 = f32[384,1024]{1,0:T(8,128)} copy-done((f32[384,1024]{1,0:T(8,128)}, f32[384,1024]{1,0:T(8,128)S(1)}, u32[]{:S(2)}) %copy-start.5) | copy-done | bytes 1572888
  77.5 0.1 reshape.71
  77.6 1.1 pad_maximum_fusion.2
  78.7 0.6 all-to-all-done.3
  79.3 7.4 %all-to-all-start.4 = ((bf16[32,8,1024]{2,1,0:T(8,128)(2,1)}), bf16[32,8,1024]{2,1,0:T(8,128)(2,1)S(1)}, u32[]{:S(2)}, u32[]{:S(2)}) async-start(bf16[32,8,1024]{2,1,0:T(8,128)(2,1)} %pad_maximum_fusion.2), calls=%async_computation.4 | async-start | bytes 1048576 | tf_op jit(solution)/shard_map/all_to_all | solution.py:216
  86.7 0.0 collective-permute-done.1
  86.8 0.9 pad_maximum_fusion.1
  87.7 1.1 fusion
  88.8 23.4 %all-gather = bf16[512,512]{1,0:T(8,128)(2,1)S(1)} all-gather(bf16[32,512]{1,0:T(8,128)(2,1)S(1)} %reduce_sum.45), channel_id=2, replica_groups=mesh['z'=8,'core'=2,'dx'=4,'dy'=8] {'z','core'}, dimensions={0}, use_global_device_ids=true | all-gather | bytes 557056 | tf_op jit(solution)/shard_map/all_gather | solution.py:215
  112.2 0.0 all-to-all-done.4
  112.2 1.1 shard_map.157
  (20 shorter events, 0.2 us)
Async XLA Ops:
  0.6 87.0 %copy-start = (bf16[128,1024]{1,0:T(8,128)(2,1)S(1)}, bf16[128,1024]{1,0:T(8,128)(2,1)}, u32[]{:S(2)}) copy-start(bf16[128,1024]{1,0:T(8,128)(2,1)} %param.22) | copy-start | bytes 786436
  0.6 12.2 %copy-start.14 = (f32[256]{0:T(256)S(1)}, f32[256]{0:T(256)}, u32[]{:S(2)}) copy-start(f32[256]{0:T(256)} %param.15) | copy-start | bytes 3076
  0.7 12.2 %copy-start.15 = (s32[128]{0:T(128)S(1)}, s32[128]{0:T(128)}, u32[]{:S(2)}) copy-start(s32[128]{0:T(128)} %param.14) | copy-start | bytes 1540
  0.7 12.4 %copy-start.10 = (bf16[128,1024]{1,0:T(8,128)(2,1)S(1)}, bf16[128,1024]{1,0:T(8,128)(2,1)}, u32[]{:S(2)}) copy-start(bf16[128,1024]{1,0:T(8,128)(2,1)} %param.13) | copy-start | bytes 786436
  2.2 11.4 %copy-start.16 = (bf16[128,1024]{1,0:T(8,128)(2,1)S(1)}, bf16[128,1024]{1,0:T(8,128)(2,1)}, u32[]{:S(2)}) copy-start(bf16[128,1024]{1,0:T(8,128)(2,1)} %param.16) | copy-start | bytes 786436
  2.2 11.4 %copy-start.17 = (bf16[128,1024]{1,0:T(8,128)(2,1)S(1)}, bf16[128,1024]{1,0:T(8,128)(2,1)}, u32[]{:S(2)}) copy-start(bf16[128,1024]{1,0:T(8,128)(2,1)} %param.12) | copy-start | bytes 786436
  2.2 18.0 %all-to-all-start = ((bf16[8,32,512]{2,1,0:T(8,128)(2,1)}), bf16[8,32,512]{2,1,0:T(8,128)(2,1)S(1)}, u32[]{:S(2)}, u32[]{:S(2)}) async-start(bf16[8,32,512]{2,1,0:T(8,128)(2,1)} %broadcast_in_dim.76), calls=%async_computation | async-start | bytes 524288 | tf_op jit(solution)/shard_map/all_to_all | solution.py:162
  12.9 0.7 copy-start.7
  12.9 1.8 %copy-start.9 = (bf16[256,1024]{1,0:T(8,128)(2,1)S(1)}, bf16[256,1024]{1,0:T(8,128)(2,1)}, u32[]{:S(2)}) copy-start(bf16[256,1024]{1,0:T(8,128)(2,1)} %param.21) | copy-start | bytes 1572868
  13.2 1.5 %copy-start.11 = (bf16[128,1024]{1,0:T(8,128)(2,1)}, bf16[128,1024]{1,0:T(8,128)(2,1)S(1)}, u32[]{:S(2)}) copy-start(bf16[128,1024]{1,0:T(8,128)(2,1)S(1)} %multiply_convert_fusion) | copy-start | bytes 786436
  15.7 9.9 %collective-permute-start = (bf16[256,1536]{1,0:T(8,128)(2,1)}, bf16[256,1536]{1,0:T(8,128)(2,1)S(1)}, u32[]{:S(2)}, u32[]{:S(2)}) collective-permute-start(bf16[256,1536]{1,0:T(8,128)(2,1)} %pad_maximum_fusion), channel_id=1, source_target_pairs={{0,32},{32,0},{1,33},{33,1},{2,34},{34,2},{3,35},{35,3},{4,36},{36... | collective-permute-start | bytes 2359304 | tf_op jit(solution)/shard_map/ppermute | solution.py:34
  21.3 16.6 %all-to-all-start.1 = ((bf16[4,256,512]{2,1,0:T(8,128)(2,1)}), bf16[4,256,512]{2,1,0:T(8,128)(2,1)S(1)}, u32[]{:S(2)}, u32[]{:S(2)}) async-start(bf16[4,256,512]{2,1,0:T(8,128)(2,1)} %broadcast_in_dim.78), calls=%async_computation.1 | async-start | bytes 2097152 | tf_op jit(solution)/shard_map/all_to_all | solution.py:158
  25.6 14.8 %copy-start.1 = (bf16[256,1536]{1,0:T(8,128)(2,1)}, bf16[256,1536]{1,0:T(8,128)(2,1)S(1)}, u32[]{:S(2)}) copy-start(bf16[256,1536]{1,0:T(8,128)(2,1)S(1)} %collective-permute-done.peer_ref) | copy-start | bytes 2359300
  40.4 15.5 %all-to-all-start.2 = ((bf16[4,256,512]{2,1,0:T(8,128)(2,1)}), bf16[4,256,512]{2,1,0:T(8,128)(2,1)}, u32[]{:S(2)}, u32[]{:S(2)}) async-start(bf16[4,256,512]{2,1,0:T(8,128)(2,1)} %bitcast.2), calls=%async_computation.2 | async-start | bytes 2097152 | tf_op jit(solution)/shard_map/all_to_all | solution.py:191
  44.6 1.1 %copy-start.2 = (bf16[256,1536]{1,0:T(8,128)(2,1)S(1)}, bf16[256,1536]{1,0:T(8,128)(2,1)}, u32[]{:S(2)}) copy-start(bf16[256,1536]{1,0:T(8,128)(2,1)} %copy-done.1) | copy-start | bytes 2359300
  45.8 8.6 %copy-start.13 = (s32[32,4]{0,1:T(4,128)S(1)}, s32[32,4]{0,1:T(4,128)}, u32[]{:S(2)}) copy-start(s32[32,4]{0,1:T(4,128)} %param.23) | copy-start | bytes 1540
  47.9 0.7 copy-start.3
  48.6 21.5 %copy-start.12 = (bf16[128,1024]{1,0:T(8,128)(2,1)S(1)}, bf16[128,1024]{1,0:T(8,128)(2,1)}, u32[]{:S(2)}) copy-start(bf16[128,1024]{1,0:T(8,128)(2,1)} %copy-done.11) | copy-start | bytes 786436
  48.6 21.5 %copy-start.18 = (bf16[128,1024]{1,0:T(8,128)(2,1)S(1)}, bf16[128,1024]{1,0:T(8,128)(2,1)}, u32[]{:S(2)}) copy-start(bf16[128,1024]{1,0:T(8,128)(2,1)} %param.12) | copy-start | bytes 786436
  48.6 25.8 %collective-permute-start.2 = (bf16[256,1024]{1,0:T(8,128)(2,1)}, bf16[256,1024]{1,0:T(8,128)(2,1)}, u32[]{:S(2)}, u32[]{:S(2)}) collective-permute-start(bf16[256,1024]{1,0:T(8,128)(2,1)} %get-tuple-element.15), channel_id=1, source_target_pairs={{0,32},{32,0},{1,33},{33,1},{2,34},{34,2},{3,35},{35,3},{4,36},{36... | collective-permute-start | bytes 1572872 | tf_op jit(solution)/shard_map/ppermute | solution.py:34
  54.6 15.9 %copy-start.4 = (bf16[256,512]{1,0:T(8,128)(2,1)S(1)}, bf16[256,512]{1,0:T(8,128)(2,1)}, u32[]{:S(2)}) copy-start(bf16[256,512]{1,0:T(8,128)(2,1)} %copy-done.3) | copy-start | bytes 786436
  54.6 19.8 %copy-start.8 = (f32[2,128,3,128]{1,0,3,2:T(2,128)S(1)}, f32[2,128,3,128]{1,0,3,2:T(2,128)}, u32[]{:S(2)}) copy-start(f32[2,128,3,128]{1,0,3,2:T(2,128)} %copy-done.7) | copy-start | bytes 1179652
  58.0 21.3 %all-to-all-start.3 = ((bf16[8,32,512]{2,1,0:T(8,128)(2,1)}), bf16[8,32,512]{2,1,0:T(8,128)(2,1)S(1)}, u32[]{:S(2)}, u32[]{:S(2)}) async-start(bf16[8,32,512]{2,1,0:T(8,128)(2,1)} %bitcast.3), calls=%async_computation.3 | async-start | bytes 524288 | tf_op jit(solution)/shard_map/all_to_all | solution.py:213
  70.5 16.2 %collective-permute-start.1 = (bf16[256,512]{1,0:T(8,128)(2,1)S(1)}, bf16[256,512]{1,0:T(8,128)(2,1)S(1)}, u32[]{:S(2)}, u32[]{:S(2)}) collective-permute-start(bf16[256,512]{1,0:T(8,128)(2,1)S(1)} %copy-done.4), channel_id=1, source_target_pairs={{0,32},{32,0},{1,33},{33,1},{2,34},{34,2},{3,35},{35,3},{4,36},{36... | collective-permute-start | bytes 786440 | tf_op jit(solution)/shard_map/ppermute | solution.py:34
  76.3 1.2 %copy-start.5 = (f32[384,1024]{1,0:T(8,128)}, f32[384,1024]{1,0:T(8,128)S(1)}, u32[]{:S(2)}) copy-start(f32[384,1024]{1,0:T(8,128)S(1)} %fusion.6) | copy-start | bytes 4718596
  78.7 9.0 %copy-start.6 = (f32[384,1024]{1,0:T(8,128)S(1)}, f32[384,1024]{1,0:T(8,128)}, u32[]{:S(2)}) copy-start(f32[384,1024]{1,0:T(8,128)} %copy-done.5) | copy-start | bytes 4718596
  79.3 32.9 %all-to-all-start.4 = ((bf16[32,8,1024]{2,1,0:T(8,128)(2,1)}), bf16[32,8,1024]{2,1,0:T(8,128)(2,1)S(1)}, u32[]{:S(2)}, u32[]{:S(2)}) async-start(bf16[32,8,1024]{2,1,0:T(8,128)(2,1)} %pad_maximum_fusion.2), calls=%async_computation.4 | async-start | bytes 1048576 | tf_op jit(solution)/shard_map/all_to_all | solution.py:216

commit v6 on v5

--- a/solution.py
+++ b/solution.py
@@ -80,11 +80,11 @@
     rows, depth = hidden.shape
     width = w.shape[1]
 
-    def body(h_ref, g_ref, peer_ref, w_ref, act_ref, actp_ref, hid_ref, hidp_ref):
+    def body(h_ref, g_ref, peer_ref, w_ref, act_ref, hid_ref, give_ref):
         w_all = w_ref[...]
         activ, pre = pre_grad(peer_ref[:, :depth], peer_ref[:, depth:], w_all)
-        actp_ref[...] = activ.astype(BF)
-        hidp_ref[...] = dot(pre, w_all, 1, 1).astype(BF)
+        give_ref[:, depth:] = activ.astype(BF)
+        give_ref[:, :depth] = dot(pre, w_all, 1, 1).astype(BF)
         activ, pre = pre_grad(h_ref[...], g_ref[...], w_all)
         act_ref[...] = activ.astype(BF)
         hid_ref[...] = dot(pre, w_all, 1, 1)
@@ -95,10 +95,30 @@
         6 * depth * width,
         8,
         ((rows, width), BF),
-        ((rows, width), BF),
         ((rows, depth), jnp.float32),
-        ((rows, depth), BF),
+        ((rows, depth + width), BF),
     )(hidden, grad, peer, w)
+
+
+def x_sum(terms):
+    count, rows, width = terms.shape
+    tile = rows // 4
+
+    def body(terms_ref, out_ref):
+        total = terms_ref[0].astype(jnp.float32)
+        for i in range(1, count):
+            total = total + terms_ref[i].astype(jnp.float32)
+        out_ref[...] = total.astype(BF)
+
+    return pl.pallas_call(
+        body,
+        grid=(4,),
+        in_specs=[pl.BlockSpec((count, tile, width), lambda i: (0, i, 0))],
+        out_specs=pl.BlockSpec((tile, width), lambda i: (i, 0)),
+        out_shape=jax.ShapeDtypeStruct((rows, width), BF),
+        compiler_params=pltpu.CompilerParams(vmem_limit_bytes=4 * 2**20),
+        name="x_sum",
+    )(terms)
 
 
 def finish(stack, riders):
@@ -192,10 +212,11 @@
         part.reshape(nx, ny * block, half_w), "dx", split_axis=0, concat_axis=0, tiled=True
     )
 
-    act_mine, act_give, hid_mine, hid_give = row_products(hidden, grad_mine, peer, w)
-    hid_got = swap_core(hid_give)
-    hid_grad = (hid_mine + hid_got.astype(jnp.float32)).astype(BF)
-    act_got = swap_core(act_give)
+    act_mine, hid_mine, give = row_products(hidden, grad_mine, peer, w)
+    got = swap_core(give)
+    depth = hidden.shape[1]
+    act_got = got[:, depth:]
+    hid_grad = (hid_mine + got[:, :depth].astype(jnp.float32)).astype(BF)
     activations = ordered(act_mine, act_got, first)
     src_grad = lax.dot_general(
         operator,
@@ -209,7 +230,7 @@
         [outgoing.reshape(peers, slots, -1), bound_grad.reshape(peers, slots, -1)], axis=1
     )
 
-    summed = jnp.sum(got_x.astype(jnp.float32), axis=0).astype(BF).reshape(ny, block, half_w)
+    summed = x_sum(got_x).reshape(ny, block, half_w)
     got_y = lax.all_to_all(summed, "dy", split_axis=0, concat_axis=0, tiled=True)
     total = jnp.sum(got_y.astype(jnp.float32), axis=0)
     stack = lax.all_gather(total.astype(BF), ("z", "core"))

time: 114 us -> 113 us (level)
  starting transfers between devices: 50.1 us -> 41.2 us
  blocking collectives: 23.4 us -> 26.2 us
  local copies, waits for them, and re-layouts: 6.72 us -> 8.73 us
  waiting for transfers between devices: 14.1 us -> 15.9 us
  Pallas kernels: 5.69 us -> 7.22 us
    ppermute x3 -> x2, starting transfers between devices: 14.2 us -> 10.3 us  [swap_core(): return lax.ppermute(value, 'core', SWAP)]
    all_to_all x1, starting transfers between devices: 7.44 us -> 4.15 us  [local(): got_r = lax.all_to_all(riders, DOM, split_axis=0, concat_axis=0, tiled=True)]
    all_to_all x1, waiting for transfers between devices: 0.61 us -> 3.61 us  [local(): lax.all_to_all(summed, 'dy', split_axis=0, concat_axis=0, tiled=True)]
    all_gather x1, blocking collectives: 23.4 us -> 26.2 us  [local(): stack = lax.all_gather(total.astype(BF), ('z', 'core'))]
    reduce_sum x1 -> x0, other arithmetic: 2.15 us -> none  [local(): jnp.sum(got_x.astype(jnp.float32), axis=0).astype(BF)]
    unnamed x39 -> x45, local copies, waits for them, and re-layouts: 3.55 us -> 5.55 us
    pallas_call x0 -> x1, Pallas kernels: none -> 1.46 us  [x_sum(): pl.pallas_call(body, grid=(4,), in_specs=[pl.BlockSpec((count, tile, widt...]
    all_to_all x1, waiting for transfers between devices: 1.2 us -> 0.01 us  [local(): lax.all_to_all(part.reshape(nx, ny * block, half_w), 'dx', split_axis=0,...]
  transfers between devices with their start and end apart: 8 -> 7, of which waited for: 3 -> 2; matrix products, arithmetic and copies ran while one was open for 12% -> 12% of each run, Pallas kernels for 2% -> 3%
where the time goes in v6:
time: 113 us; the launch traced here: 112 us
  starting transfers between devices  41.2 us (36%)
  blocking collectives  26.2 us (23%)
  waiting for transfers between devices  15.9 us (14%)
  local copies, waits for them, and re-layouts  8.73 us (8%)
  Pallas kernels  7.22 us (6%)
  other arithmetic  7.04 us (6%)
  matrix products  5.17 us (5%)
    all_gather x1, blocking collectives, local(): stack = lax.all_gather(total.astype(BF), ('z', 'core'))  26.2 us
    all_to_all x1, waiting for transfers between devices, spread(): return lax.all_to_all(copies, axis, split_axis=0, concat_axis=0, tiled=True)  12.3 us
    all_to_all x1, starting transfers between devices, local(): lax.all_to_all(summed, 'dy', split_axis=0, concat_axis=0, tiled=True)  11.3 us
    ppermute x2, starting transfers between devices, swap_core(): return lax.ppermute(value, 'core', SWAP)  10.3 us
    all_to_all x1, starting transfers between devices, local(): lax.all_to_all(copies, 'dy', split_axis=0, concat_axis=0, tiled=True)  7.77 us
    unnamed x45, local copies, waits for them, and re-layouts  5.55 us
    all_to_all x1, starting transfers between devices, local(): got_r = lax.all_to_all(riders, DOM, split_axis=0, concat_axis=0, tiled=True)  4.15 us
    all_to_all x1, starting transfers between devices, spread(): return lax.all_to_all(copies, axis, split_axis=0, concat_axis=0, tiled=True)  4.07 us
  transfers between devices with their start and end apart: 7, of which 2 were waited for; matrix products, arithmetic and copies ran while one was open for 12% of the time, Pallas kernels for 3%

profile of v6, /device:TPU:1, one launch (start us, length us, event | category | flops | bytes accessed | tf_op | source)
XLA Modules:
  0.0 112.4 jit_solution(12063817729667949393)
XLA Ops:
  0.6 0.0 copy-start
  0.6 0.0 copy-start.18
  0.7 0.0 copy-start.19
  0.7 0.0 copy-start.14
  0.7 0.8 constant_dynamic-slice_fusion
  1.5 0.7 broadcast_in_dim.76
  2.2 7.8 %all-to-all-start = ((bf16[8,32,512]{2,1,0:T(8,128)(2,1)}), bf16[8,32,512]{2,1,0:T(8,128)(2,1)S(1)}, u32[]{:S(2)}, u32[]{:S(2)}) async-start(bf16[8,32,512]{2,1,0:T(8,128)(2,1)} %broadcast_in_dim.76), calls=%async_computation | async-start | bytes 524288 | tf_op jit(solution)/shard_map/all_to_all | solution.py:182
  10.0 0.7 iota_compare_fusion.6
  10.7 0.8 iota_compare_fusion.5
  11.5 1.0 select_convert_fusion
  12.5 0.1 select_reduce_fusion
  12.7 0.2 copy.19
  12.9 0.0 copy-done.18
  12.9 0.0 copy-done.19
  12.9 0.0 copy-start.11
  12.9 0.0 copy-start.13
  12.9 0.2 select_reduce_fusion.1
  13.1 0.0 copy-done.14
  13.1 0.1 multiply_convert_fusion
  13.2 0.0 copy-start.15
  13.2 0.4 copy-done.11
  13.6 0.0 copy-done.21
  13.7 1.0 convolution_convert_fusion.h_ref
  14.7 0.0 copy-done.13
  14.7 0.0 copy-start.1
  14.8 0.0 copy-start.5
  14.8 1.1 %pad_maximum_fusion = bf16[256,1536]{1,0:T(8,128)(2,1)} fusion(bf16[256,512]{1,0:T(8,128)(2,1)S(1)} %get-tuple-element.19, bf16[256,1024]{1,0:T(8,128)(2,1)S(1)} %convolution_convert_fusion.h_ref), kind=kLoop, calls=%fused_computation.11 | loop fusion | flops 1572864 | bytes 1572864 | tf_op jit(solution)/shard_map/concatenate | solution.py:205
  15.9 4.5 %collective-permute-start = (bf16[256,1536]{1,0:T(8,128)(2,1)}, bf16[256,1536]{1,0:T(8,128)(2,1)S(1)}, u32[]{:S(2)}, u32[]{:S(2)}) collective-permute-start(bf16[256,1536]{1,0:T(8,128)(2,1)} %pad_maximum_fusion), channel_id=1, source_target_pairs={{0,32},{32,0},{1,33},{33,1},{2,34},{34,2},{3,35},{35,3},{4,36},{36... | collective-permute-start | bytes 2359304 | tf_op jit(solution)/shard_map/ppermute | solution.py:34
  20.4 0.0 all-to-all-done
  20.4 1.1 broadcast_in_dim.78
  21.5 4.1 %all-to-all-start.1 = ((bf16[4,256,512]{2,1,0:T(8,128)(2,1)}), bf16[4,256,512]{2,1,0:T(8,128)(2,1)S(1)}, u32[]{:S(2)}, u32[]{:S(2)}) async-start(bf16[4,256,512]{2,1,0:T(8,128)(2,1)} %broadcast_in_dim.78), calls=%async_computation.1 | async-start | bytes 2097152 | tf_op jit(solution)/shard_map/all_to_all | solution.py:178
  25.6 0.0 collective-permute-done.peer_ref
  25.6 12.3 %all-to-all-done.1 = bf16[4,256,512]{2,1,0:T(8,128)(2,1)S(1)} async-done(((bf16[4,256,512]{2,1,0:T(8,128)(2,1)}), bf16[4,256,512]{2,1,0:T(8,128)(2,1)S(1)}, u32[]{:S(2)}, u32[]{:S(2)}) %all-to-all-start.1) | async-done | bytes 1048608 | tf_op jit(solution)/shard_map/all_to_all | solution.py:178
  37.9 0.0 copy-done.5
  37.9 2.5 %shard_map.156 = bf16[1024,512]{1,0:T(8,128)(2,1)} custom-call(bf16[256,1024]{1,0:T(8,128)(2,1)S(1)} %convolution_convert_fusion.h_ref, bf16[256,512]{1,0:T(8,128)(2,1)S(1)} %get-tuple-element.20.g_ref, bf16[256,1536]{1,0:T(8,128)(2,1)S(1)} %collective-permute-done.peer_ref, bf16[1024,512]{1,0:T(8,128)(2,1)S(1)} %bitcast.18), custom_call_target="tpu_custom_call" | custom-call | flops 1073741824 | bytes 3145728 | tf_op jit(solution)/shard_map/pallas_call | solution.py:74
  40.4 3.5 %all-to-all-start.2 = ((bf16[4,256,512]{2,1,0:T(8,128)(2,1)}), bf16[4,256,512]{2,1,0:T(8,128)(2,1)S(1)}, u32[]{:S(2)}, u32[]{:S(2)}) async-start(bf16[4,256,512]{2,1,0:T(8,128)(2,1)} %bitcast.2), calls=%async_computation.2 | async-start | bytes 2097152 | tf_op jit(solution)/shard_map/all_to_all | solution.py:211
  43.9 0.0 copy-start.2
  43.9 1.0 copy-done.2
  44.9 0.9 copy-done.6
  45.9 1.1 %copy-done.8 = bf16[256,1536]{1,0:T(8,128)(2,1)S(1)} copy-done((bf16[256,1536]{1,0:T(8,128)(2,1)S(1)}, bf16[256,1536]{1,0:T(8,128)(2,1)}, u32[]{:S(2)}) %copy-start.8) | copy-done | bytes 786456
  47.0 2.2 %shard_map.155 = (bf16[256,512]{1,0:T(8,128)(2,1)S(1)}, f32[256,1024]{1,0:T(8,128)S(1)}, bf16[256,1536]{1,0:T(8,128)(2,1)}) custom-call(bf16[256,1024]{1,0:T(8,128)(2,1)S(1)} %copy-done.2, bf16[256,512]{1,0:T(8,128)(2,1)S(1)} %copy-done.6, bf16[256,1536]{1,0:T(8,128)(2,1)S(1)} %copy-done.8, bf16[1024,512]{1,0:T(8,128)(2,1)S(1)} %bitcast.19), custom_call_target="tpu_custom_call" | custom-call | flops 2147483648 | bytes 3145728 | tf_op jit(solution)/shard_map/pallas_call | solution.py:92
  49.2 0.7 copy-done.3
  49.9 5.8 %collective-permute-start.1 = (bf16[256,1536]{1,0:T(8,128)(2,1)}, bf16[256,1536]{1,0:T(8,128)(2,1)}, u32[]{:S(2)}, u32[]{:S(2)}) collective-permute-start(bf16[256,1536]{1,0:T(8,128)(2,1)} %get-tuple-element.12), channel_id=1, source_target_pairs={{0,32},{32,0},{1,33},{33,1},{2,34},{34,2},{3,35},{35,3},{4,36},{36... | collective-permute-start | bytes 2359304 | tf_op jit(solution)/shard_map/ppermute | solution.py:34
  55.7 0.1 copy.20
  55.8 0.1 eq.69
  55.9 0.0 copy-start.12
  56.0 0.0 all-to-all-done.2.terms_ref
  56.0 1.5 %x_sum.1 = bf16[256,512]{1,0:T(8,128)(2,1)} custom-call(bf16[4,256,512]{2,1,0:T(8,128)(2,1)S(1)} %all-to-all-done.2.terms_ref), custom_call_target="tpu_custom_call" | custom-call | tf_op jit(solution)/shard_map/x_sum/pallas_call | solution.py:113
  57.4 11.3 %all-to-all-start.3 = ((bf16[8,32,512]{2,1,0:T(8,128)(2,1)}), bf16[8,32,512]{2,1,0:T(8,128)(2,1)S(1)}, u32[]{:S(2)}, u32[]{:S(2)}) async-start(bf16[8,32,512]{2,1,0:T(8,128)(2,1)} %bitcast.3), calls=%async_computation.3 | async-start | bytes 524288 | tf_op jit(solution)/shard_map/all_to_all | solution.py:234
  68.8 1.2 %convolution_convert_fusion.1 = bf16[128,1024]{1,0:T(8,128)(2,1)S(1)} fusion(bf16[128,1024]{1,0:T(8,128)(2,1)S(1)} %copy-done.16, bf16[128,1024]{1,0:T(8,128)(2,1)} %param.12, s32[128]{0:T(128)S(1)} %eq.69), kind=kOutput, calls=%fused_computation.3 | convolution fusion | flops 68321280 | bytes 786944 | tf_op jit(solution)/shard_map/dot_general | solution.py:30
  70.0 0.1 reshape.70
  70.1 0.0 collective-permute-done.1
  70.1 1.8 %fusion.6 = f32[384,1024]{1,0:T(8,128)S(1)} fusion(f32[256,1024]{1,0:T(8,128)S(1)} %get-tuple-element.13, bf16[256,1536]{1,0:T(8,128)(2,1)} %collective-permute-done.1, f32[48,8,2,128]{3,2,1,0:T(2,128)S(1)} %bitcast.21), kind=kOutput, calls=%fused_computation.12 | convolution fusion | flops 1208745984 | bytes 3538944 | tf_op jit(solution)/shard_map/dot_general | solution.py:221
  72.0 1.1 %copy-done.9 = f32[384,1024]{1,0:T(8,128)} copy-done((f32[384,1024]{1,0:T(8,128)}, f32[384,1024]{1,0:T(8,128)S(1)}, u32[]{:S(2)}) %copy-start.9) | copy-done | bytes 1572888
  73.2 0.1 reshape.71
  73.3 1.1 pad_maximum_fusion.2
  74.3 3.6 %all-to-all-done.3 = bf16[8,32,512]{2,1,0:T(8,128)(2,1)S(1)} async-done(((bf16[8,32,512]{2,1,0:T(8,128)(2,1)}), bf16[8,32,512]{2,1,0:T(8,128)(2,1)S(1)}, u32[]{:S(2)}, u32[]{:S(2)}) %all-to-all-start.3) | async-done | bytes 262176 | tf_op jit(solution)/shard_map/all_to_all | solution.py:234
  78.0 4.2 %all-to-all-start.4 = ((bf16[32,8,1024]{2,1,0:T(8,128)(2,1)}), bf16[32,8,1024]{2,1,0:T(8,128)(2,1)S(1)}, u32[]{:S(2)}, u32[]{:S(2)}) async-start(bf16[32,8,1024]{2,1,0:T(8,128)(2,1)} %pad_maximum_fusion.2), calls=%async_computation.4 | async-start | bytes 1048576 | tf_op jit(solution)/shard_map/all_to_all | solution.py:237
  82.1 1.0 broadcast_select_fusion.1
  83.1 0.9 pad_maximum_fusion.1
  84.0 1.1 fusion
  85.1 26.2 %all-gather = bf16[512,512]{1,0:T(8,128)(2,1)S(1)} all-gather(bf16[32,512]{1,0:T(8,128)(2,1)S(1)} %reduce_sum.32), channel_id=2, replica_groups=mesh['z'=8,'core'=2,'dx'=4,'dy'=8] {'z','core'}, dimensions={0}, use_global_device_ids=true | all-gather | bytes 557056 | tf_op jit(solution)/shard_map/all_gather | solution.py:236
  111.3 0.0 all-to-all-done.4
  111.3 1.1 shard_map.157
  (24 shorter events, 0.1 us)
Async XLA Ops:
  0.6 83.4 %copy-start = (bf16[128,1024]{1,0:T(8,128)(2,1)S(1)}, bf16[128,1024]{1,0:T(8,128)(2,1)}, u32[]{:S(2)}) copy-start(bf16[128,1024]{1,0:T(8,128)(2,1)} %param.22) | copy-start | bytes 786436
  0.6 12.2 %copy-start.18 = (f32[256]{0:T(256)S(1)}, f32[256]{0:T(256)}, u32[]{:S(2)}) copy-start(f32[256]{0:T(256)} %param.15) | copy-start | bytes 3076
  0.7 12.2 %copy-start.19 = (s32[128]{0:T(128)S(1)}, s32[128]{0:T(128)}, u32[]{:S(2)}) copy-start(s32[128]{0:T(128)} %param.14) | copy-start | bytes 1540
  0.7 12.4 %copy-start.14 = (bf16[128,1024]{1,0:T(8,128)(2,1)S(1)}, bf16[128,1024]{1,0:T(8,128)(2,1)}, u32[]{:S(2)}) copy-start(bf16[128,1024]{1,0:T(8,128)(2,1)} %param.13) | copy-start | bytes 786436
  2.2 11.4 %copy-start.20 = (bf16[128,1024]{1,0:T(8,128)(2,1)S(1)}, bf16[128,1024]{1,0:T(8,128)(2,1)}, u32[]{:S(2)}) copy-start(bf16[128,1024]{1,0:T(8,128)(2,1)} %param.16) | copy-start | bytes 786436
  2.2 11.4 %copy-start.21 = (bf16[128,1024]{1,0:T(8,128)(2,1)S(1)}, bf16[128,1024]{1,0:T(8,128)(2,1)}, u32[]{:S(2)}) copy-start(bf16[128,1024]{1,0:T(8,128)(2,1)} %param.12) | copy-start | bytes 786436
  2.2 18.2 %all-to-all-start = ((bf16[8,32,512]{2,1,0:T(8,128)(2,1)}), bf16[8,32,512]{2,1,0:T(8,128)(2,1)S(1)}, u32[]{:S(2)}, u32[]{:S(2)}) async-start(bf16[8,32,512]{2,1,0:T(8,128)(2,1)} %broadcast_in_dim.76), calls=%async_computation | async-start | bytes 524288 | tf_op jit(solution)/shard_map/all_to_all | solution.py:182
  12.9 0.7 copy-start.11
  12.9 1.8 %copy-start.13 = (bf16[256,1024]{1,0:T(8,128)(2,1)S(1)}, bf16[256,1024]{1,0:T(8,128)(2,1)}, u32[]{:S(2)}) copy-start(bf16[256,1024]{1,0:T(8,128)(2,1)} %param.21) | copy-start | bytes 1572868
  13.2 1.5 %copy-start.15 = (bf16[128,1024]{1,0:T(8,128)(2,1)}, bf16[128,1024]{1,0:T(8,128)(2,1)S(1)}, u32[]{:S(2)}) copy-start(bf16[128,1024]{1,0:T(8,128)(2,1)S(1)} %multiply_convert_fusion) | copy-start | bytes 786436
  14.7 23.2 %copy-start.1 = (bf16[256,1024]{1,0:T(8,128)(2,1)}, bf16[256,1024]{1,0:T(8,128)(2,1)S(1)}, u32[]{:S(2)}) copy-start(bf16[256,1024]{1,0:T(8,128)(2,1)S(1)} %convolution_convert_fusion.h_ref) | copy-start | bytes 1572868
  14.8 23.1 %copy-start.5 = (bf16[256,512]{1,0:T(8,128)(2,1)}, bf16[256,512]{1,0:T(8,128)(2,1)S(1)}, u32[]{:S(2)}) copy-start(bf16[256,512]{1,0:T(8,128)(2,1)S(1)} %get-tuple-element.20.g_ref) | copy-start | bytes 786436
  15.9 9.7 %collective-permute-start = (bf16[256,1536]{1,0:T(8,128)(2,1)}, bf16[256,1536]{1,0:T(8,128)(2,1)S(1)}, u32[]{:S(2)}, u32[]{:S(2)}) collective-permute-start(bf16[256,1536]{1,0:T(8,128)(2,1)} %pad_maximum_fusion), channel_id=1, source_target_pairs={{0,32},{32,0},{1,33},{33,1},{2,34},{34,2},{3,35},{35,3},{4,36},{36... | collective-permute-start | bytes 2359304 | tf_op jit(solution)/shard_map/ppermute | solution.py:34
  21.5 16.4 %all-to-all-start.1 = ((bf16[4,256,512]{2,1,0:T(8,128)(2,1)}), bf16[4,256,512]{2,1,0:T(8,128)(2,1)S(1)}, u32[]{:S(2)}, u32[]{:S(2)}) async-start(bf16[4,256,512]{2,1,0:T(8,128)(2,1)} %broadcast_in_dim.78), calls=%async_computation.1 | async-start | bytes 2097152 | tf_op jit(solution)/shard_map/all_to_all | solution.py:178
  25.6 14.8 %copy-start.7 = (bf16[256,1536]{1,0:T(8,128)(2,1)}, bf16[256,1536]{1,0:T(8,128)(2,1)S(1)}, u32[]{:S(2)}) copy-start(bf16[256,1536]{1,0:T(8,128)(2,1)S(1)} %collective-permute-done.peer_ref) | copy-start | bytes 2359300
  40.4 15.6 %all-to-all-start.2 = ((bf16[4,256,512]{2,1,0:T(8,128)(2,1)}), bf16[4,256,512]{2,1,0:T(8,128)(2,1)S(1)}, u32[]{:S(2)}, u32[]{:S(2)}) async-start(bf16[4,256,512]{2,1,0:T(8,128)(2,1)} %bitcast.2), calls=%async_computation.2 | async-start | bytes 2097152 | tf_op jit(solution)/shard_map/all_to_all | solution.py:211
  43.9 1.0 copy-start.2
  44.9 0.9 copy-start.6
  45.9 1.1 %copy-start.8 = (bf16[256,1536]{1,0:T(8,128)(2,1)S(1)}, bf16[256,1536]{1,0:T(8,128)(2,1)}, u32[]{:S(2)}) copy-start(bf16[256,1536]{1,0:T(8,128)(2,1)} %copy-done.7) | copy-start | bytes 2359300
  47.0 8.7 %copy-start.17 = (s32[32,4]{0,1:T(4,128)S(1)}, s32[32,4]{0,1:T(4,128)}, u32[]{:S(2)}) copy-start(s32[32,4]{0,1:T(4,128)} %param.23) | copy-start | bytes 1540
  49.2 0.7 copy-start.3
  49.9 18.8 %copy-start.16 = (bf16[128,1024]{1,0:T(8,128)(2,1)S(1)}, bf16[128,1024]{1,0:T(8,128)(2,1)}, u32[]{:S(2)}) copy-start(bf16[128,1024]{1,0:T(8,128)(2,1)} %copy-done.15) | copy-start | bytes 786436
  49.9 20.2 %collective-permute-start.1 = (bf16[256,1536]{1,0:T(8,128)(2,1)}, bf16[256,1536]{1,0:T(8,128)(2,1)}, u32[]{:S(2)}, u32[]{:S(2)}) collective-permute-start(bf16[256,1536]{1,0:T(8,128)(2,1)} %get-tuple-element.12), channel_id=1, source_target_pairs={{0,32},{32,0},{1,33},{33,1},{2,34},{34,2},{3,35},{35,3},{4,36},{36... | collective-permute-start | bytes 2359304 | tf_op jit(solution)/shard_map/ppermute | solution.py:34
  55.9 14.2 %copy-start.12 = (f32[2,128,3,128]{1,0,3,2:T(2,128)S(1)}, f32[2,128,3,128]{1,0,3,2:T(2,128)}, u32[]{:S(2)}) copy-start(f32[2,128,3,128]{1,0,3,2:T(2,128)} %copy-done.11) | copy-start | bytes 1179652
  57.4 20.5 %all-to-all-start.3 = ((bf16[8,32,512]{2,1,0:T(8,128)(2,1)}), bf16[8,32,512]{2,1,0:T(8,128)(2,1)S(1)}, u32[]{:S(2)}, u32[]{:S(2)}) async-start(bf16[8,32,512]{2,1,0:T(8,128)(2,1)} %bitcast.3), calls=%async_computation.3 | async-start | bytes 524288 | tf_op jit(solution)/shard_map/all_to_all | solution.py:234
  72.0 1.2 %copy-start.9 = (f32[384,1024]{1,0:T(8,128)}, f32[384,1024]{1,0:T(8,128)S(1)}, u32[]{:S(2)}) copy-start(f32[384,1024]{1,0:T(8,128)S(1)} %fusion.6) | copy-start | bytes 4718596
  73.1 9.0 %copy-start.4 = (bf16[256,512]{1,0:T(8,128)(2,1)S(1)}, bf16[256,512]{1,0:T(8,128)(2,1)}, u32[]{:S(2)}) copy-start(bf16[256,512]{1,0:T(8,128)(2,1)} %copy-done.3) | copy-start | bytes 786436
  74.3 9.7 %copy-start.10 = (f32[384,1024]{1,0:T(8,128)S(1)}, f32[384,1024]{1,0:T(8,128)}, u32[]{:S(2)}) copy-start(f32[384,1024]{1,0:T(8,128)} %copy-done.9) | copy-start | bytes 4718596
  78.0 33.4 %all-to-all-start.4 = ((bf16[32,8,1024]{2,1,0:T(8,128)(2,1)}), bf16[32,8,1024]{2,1,0:T(8,128)(2,1)S(1)}, u32[]{:S(2)}, u32[]{:S(2)}) async-start(bf16[32,8,1024]{2,1,0:T(8,128)(2,1)} %pad_maximum_fusion.2), calls=%async_computation.4 | async-start | bytes 1048576 | tf_op jit(solution)/shard_map/all_to_all | solution.py:237

commit v7 on v6

--- a/solution.py
+++ b/solution.py
@@ -102,7 +102,7 @@
 
 def x_sum(terms):
     count, rows, width = terms.shape
-    tile = rows // 4
+    tile = rows // 2
 
     def body(terms_ref, out_ref):
         total = terms_ref[0].astype(jnp.float32)
@@ -112,7 +112,7 @@
 
     return pl.pallas_call(
         body,
-        grid=(4,),
+        grid=(2,),
         in_specs=[pl.BlockSpec((count, tile, width), lambda i: (0, i, 0))],
         out_specs=pl.BlockSpec((tile, width), lambda i: (i, 0)),
         out_shape=jax.ShapeDtypeStruct((rows, width), BF),
@@ -205,7 +205,8 @@
     peer = swap_core(jnp.concatenate([hidden, grad_give], axis=1))
     sends = send_rows.reshape(-1)
     row_ids = jnp.arange(row_count, dtype=jnp.int32)
-    outgoing = dot((sends[:, None] == row_ids[None, :]).astype(BF), local_rows, 1, 0).astype(BF)
+    picker = (sends[:, None] == row_ids[None, :]).astype(BF)
+    outgoing = dot(picker, local_rows, 1, 0).astype(BF)
 
     part = weight_products(hidden, grad_mine, peer, w)
     got_x = lax.all_to_all(

time: 113 us -> 113 us (level)
  no operation moved by 1% of the time
where the time goes in v7:
time: 113 us; the launch traced here: 112 us
  starting transfers between devices  41.2 us (36%)
  blocking collectives  26.2 us (23%)
  waiting for transfers between devices  15.9 us (14%)
  local copies, waits for them, and re-layouts  8.73 us (8%)
  other arithmetic  7.04 us (6%)
  Pallas kernels  6.67 us (6%)
  matrix products  5.16 us (5%)
    all_gather x1, blocking collectives, local(): stack = lax.all_gather(total.astype(BF), ('z', 'core'))  26.2 us
    all_to_all x1, waiting for transfers between devices, spread(): return lax.all_to_all(copies, axis, split_axis=0, concat_axis=0, tiled=True)  12.3 us
    all_to_all x1, starting transfers between devices, local(): lax.all_to_all(summed, 'dy', split_axis=0, concat_axis=0, tiled=True)  11.3 us
    ppermute x2, starting transfers between devices, swap_core(): return lax.ppermute(value, 'core', SWAP)  10.3 us
    all_to_all x1, starting transfers between devices, local(): lax.all_to_all(copies, 'dy', split_axis=0, concat_axis=0, tiled=True)  7.77 us
    unnamed x45, local copies, waits for them, and re-layouts  5.55 us
    all_to_all x1, starting transfers between devices, local(): got_r = lax.all_to_all(riders, DOM, split_axis=0, concat_axis=0, tiled=True)  4.15 us
    all_to_all x1, starting transfers between devices, spread(): return lax.all_to_all(copies, axis, split_axis=0, concat_axis=0, tiled=True)  4.07 us
  transfers between devices with their start and end apart: 7, of which 2 were waited for; matrix products, arithmetic and copies ran while one was open for 12% of the time, Pallas kernels for 3%

profile of v7, /device:TPU:1, one launch (start us, length us, event | category | flops | bytes accessed | tf_op | source)
XLA Modules:
  0.0 111.8 jit_solution(4162078239149582770)
XLA Ops:
  0.6 0.0 copy-start
  0.7 0.8 constant_dynamic-slice_fusion
  1.5 0.7 broadcast_in_dim.76
  2.2 7.8 %all-to-all-start = ((bf16[8,32,512]{2,1,0:T(8,128)(2,1)}), bf16[8,32,512]{2,1,0:T(8,128)(2,1)S(1)}, u32[]{:S(2)}, u32[]{:S(2)}) async-start(bf16[8,32,512]{2,1,0:T(8,128)(2,1)} %broadcast_in_dim.76), calls=%async_computation | async-start | bytes 524288 | tf_op jit(solution)/shard_map/all_to_all | solution.py:182
  10.0 0.7 iota_compare_fusion.6
  10.7 0.8 iota_compare_fusion.5
  11.5 1.0 select_convert_fusion
  12.5 0.1 select_reduce_fusion
  12.7 0.2 copy.19
  12.9 0.0 copy-done.18
  12.9 0.0 copy-done.19
  12.9 0.0 copy-start.11
  12.9 0.0 copy-start.13
  12.9 0.2 select_reduce_fusion.1
  13.1 0.0 copy-done.14
  13.1 0.1 multiply_convert_fusion
  13.2 0.0 copy-start.15
  13.2 0.4 copy-done.11
  13.6 0.0 copy-done.21
  13.7 1.0 convolution_convert_fusion.h_ref
  14.7 0.0 copy-done.13
  14.7 0.0 copy-start.1
  14.8 0.0 copy-start.5
  14.8 1.1 %pad_maximum_fusion = bf16[256,1536]{1,0:T(8,128)(2,1)} fusion(bf16[256,512]{1,0:T(8,128)(2,1)S(1)} %get-tuple-element.19, bf16[256,1024]{1,0:T(8,128)(2,1)S(1)} %convolution_convert_fusion.h_ref), kind=kLoop, calls=%fused_computation.11 | loop fusion | flops 1572864 | bytes 1572864 | tf_op jit(solution)/shard_map/concatenate | solution.py:205
  15.9 4.5 %collective-permute-start = (bf16[256,1536]{1,0:T(8,128)(2,1)}, bf16[256,1536]{1,0:T(8,128)(2,1)S(1)}, u32[]{:S(2)}, u32[]{:S(2)}) collective-permute-start(bf16[256,1536]{1,0:T(8,128)(2,1)} %pad_maximum_fusion), channel_id=1, source_target_pairs={{0,32},{32,0},{1,33},{33,1},{2,34},{34,2},{3,35},{35,3},{4,36},{36... | collective-permute-start | bytes 2359304 | tf_op jit(solution)/shard_map/ppermute | solution.py:34
  20.4 0.0 all-to-all-done
  20.4 1.1 broadcast_in_dim.78
  21.5 4.1 %all-to-all-start.1 = ((bf16[4,256,512]{2,1,0:T(8,128)(2,1)}), bf16[4,256,512]{2,1,0:T(8,128)(2,1)S(1)}, u32[]{:S(2)}, u32[]{:S(2)}) async-start(bf16[4,256,512]{2,1,0:T(8,128)(2,1)} %broadcast_in_dim.78), calls=%async_computation.1 | async-start | bytes 2097152 | tf_op jit(solution)/shard_map/all_to_all | solution.py:178
  25.6 0.0 collective-permute-done.peer_ref
  25.6 12.3 %all-to-all-done.1 = bf16[4,256,512]{2,1,0:T(8,128)(2,1)S(1)} async-done(((bf16[4,256,512]{2,1,0:T(8,128)(2,1)}), bf16[4,256,512]{2,1,0:T(8,128)(2,1)S(1)}, u32[]{:S(2)}, u32[]{:S(2)}) %all-to-all-start.1) | async-done | bytes 1048608 | tf_op jit(solution)/shard_map/all_to_all | solution.py:178
  37.9 0.0 copy-done.5
  37.9 2.5 %shard_map.156 = bf16[1024,512]{1,0:T(8,128)(2,1)} custom-call(bf16[256,1024]{1,0:T(8,128)(2,1)S(1)} %convolution_convert_fusion.h_ref, bf16[256,512]{1,0:T(8,128)(2,1)S(1)} %get-tuple-element.20.g_ref, bf16[256,1536]{1,0:T(8,128)(2,1)S(1)} %collective-permute-done.peer_ref, bf16[1024,512]{1,0:T(8,128)(2,1)S(1)} %bitcast.18), custom_call_target="tpu_custom_call" | custom-call | flops 1073741824 | bytes 3145728 | tf_op jit(solution)/shard_map/pallas_call | solution.py:74
  40.4 3.5 %all-to-all-start.2 = ((bf16[4,256,512]{2,1,0:T(8,128)(2,1)}), bf16[4,256,512]{2,1,0:T(8,128)(2,1)S(1)}, u32[]{:S(2)}, u32[]{:S(2)}) async-start(bf16[4,256,512]{2,1,0:T(8,128)(2,1)} %bitcast.2), calls=%async_computation.2 | async-start | bytes 2097152 | tf_op jit(solution)/shard_map/all_to_all | solution.py:212
  43.9 0.0 copy-start.2
  43.9 1.0 copy-done.2
  44.9 0.9 copy-done.6
  45.9 1.1 %copy-done.8 = bf16[256,1536]{1,0:T(8,128)(2,1)S(1)} copy-done((bf16[256,1536]{1,0:T(8,128)(2,1)S(1)}, bf16[256,1536]{1,0:T(8,128)(2,1)}, u32[]{:S(2)}) %copy-start.8) | copy-done | bytes 786456
  47.0 2.2 %shard_map.155 = (bf16[256,512]{1,0:T(8,128)(2,1)S(1)}, f32[256,1024]{1,0:T(8,128)S(1)}, bf16[256,1536]{1,0:T(8,128)(2,1)}) custom-call(bf16[256,1024]{1,0:T(8,128)(2,1)S(1)} %copy-done.2, bf16[256,512]{1,0:T(8,128)(2,1)S(1)} %copy-done.6, bf16[256,1536]{1,0:T(8,128)(2,1)S(1)} %copy-done.8, bf16[1024,512]{1,0:T(8,128)(2,1)S(1)} %bitcast.19), custom_call_target="tpu_custom_call" | custom-call | flops 2147483648 | bytes 3145728 | tf_op jit(solution)/shard_map/pallas_call | solution.py:92
  49.2 0.7 copy-done.3
  49.9 5.8 %collective-permute-start.1 = (bf16[256,1536]{1,0:T(8,128)(2,1)}, bf16[256,1536]{1,0:T(8,128)(2,1)}, u32[]{:S(2)}, u32[]{:S(2)}) collective-permute-start(bf16[256,1536]{1,0:T(8,128)(2,1)} %get-tuple-element.12), channel_id=1, source_target_pairs={{0,32},{32,0},{1,33},{33,1},{2,34},{34,2},{3,35},{35,3},{4,36},{36... | collective-permute-start | bytes 2359304 | tf_op jit(solution)/shard_map/ppermute | solution.py:34
  55.7 0.1 copy.20
  55.8 0.1 eq.69
  55.9 0.0 copy-start.12
  56.0 0.0 all-to-all-done.2.terms_ref
  56.0 0.9 x_sum.1
  56.9 11.3 %all-to-all-start.3 = ((bf16[8,32,512]{2,1,0:T(8,128)(2,1)}), bf16[8,32,512]{2,1,0:T(8,128)(2,1)S(1)}, u32[]{:S(2)}, u32[]{:S(2)}) async-start(bf16[8,32,512]{2,1,0:T(8,128)(2,1)} %bitcast.3), calls=%async_computation.3 | async-start | bytes 524288 | tf_op jit(solution)/shard_map/all_to_all | solution.py:235
  68.2 1.2 %convolution_convert_fusion.1 = bf16[128,1024]{1,0:T(8,128)(2,1)S(1)} fusion(bf16[128,1024]{1,0:T(8,128)(2,1)S(1)} %copy-done.16, bf16[128,1024]{1,0:T(8,128)(2,1)} %param.12, s32[128]{0:T(128)S(1)} %eq.69), kind=kOutput, calls=%fused_computation.3 | convolution fusion | flops 68321280 | bytes 786944 | tf_op jit(solution)/shard_map/dot_general | solution.py:30
  69.4 0.1 reshape.70
  69.6 0.0 collective-permute-done.1
  69.6 1.8 %fusion.6 = f32[384,1024]{1,0:T(8,128)S(1)} fusion(f32[256,1024]{1,0:T(8,128)S(1)} %get-tuple-element.13, bf16[256,1536]{1,0:T(8,128)(2,1)} %collective-permute-done.1, f32[48,8,2,128]{3,2,1,0:T(2,128)S(1)} %bitcast.21), kind=kOutput, calls=%fused_computation.12 | convolution fusion | flops 1208745984 | bytes 3538944 | tf_op jit(solution)/shard_map/dot_general | solution.py:222
  71.4 0.0 copy-start.9
  71.4 1.1 %copy-done.9 = f32[384,1024]{1,0:T(8,128)} copy-done((f32[384,1024]{1,0:T(8,128)}, f32[384,1024]{1,0:T(8,128)S(1)}, u32[]{:S(2)}) %copy-start.9) | copy-done | bytes 1572888
  72.6 0.1 reshape.71
  72.7 1.1 pad_maximum_fusion.2
  73.8 3.6 %all-to-all-done.3 = bf16[8,32,512]{2,1,0:T(8,128)(2,1)S(1)} async-done(((bf16[8,32,512]{2,1,0:T(8,128)(2,1)}), bf16[8,32,512]{2,1,0:T(8,128)(2,1)S(1)}, u32[]{:S(2)}, u32[]{:S(2)}) %all-to-all-start.3) | async-done | bytes 262176 | tf_op jit(solution)/shard_map/all_to_all | solution.py:235
  77.4 4.2 %all-to-all-start.4 = ((bf16[32,8,1024]{2,1,0:T(8,128)(2,1)}), bf16[32,8,1024]{2,1,0:T(8,128)(2,1)S(1)}, u32[]{:S(2)}, u32[]{:S(2)}) async-start(bf16[32,8,1024]{2,1,0:T(8,128)(2,1)} %pad_maximum_fusion.2), calls=%async_computation.4 | async-start | bytes 1048576 | tf_op jit(solution)/shard_map/all_to_all | solution.py:238
  81.6 0.0 copy-done.4
  81.6 1.0 broadcast_select_fusion.1
  82.6 0.9 pad_maximum_fusion.1
  83.4 0.0 copy-done
  83.4 1.1 fusion
  84.6 26.2 %all-gather = bf16[512,512]{1,0:T(8,128)(2,1)S(1)} all-gather(bf16[32,512]{1,0:T(8,128)(2,1)S(1)} %reduce_sum.32), channel_id=2, replica_groups=mesh['z'=8,'core'=2,'dx'=4,'dy'=8] {'z','core'}, dimensions={0}, use_global_device_ids=true | all-gather | bytes 557056 | tf_op jit(solution)/shard_map/all_gather | solution.py:237
  110.8 0.0 all-to-all-done.4
  110.8 1.1 shard_map.157
  (24 shorter events, 0.1 us)
Async XLA Ops:
  0.6 82.8 %copy-start = (bf16[128,1024]{1,0:T(8,128)(2,1)S(1)}, bf16[128,1024]{1,0:T(8,128)(2,1)}, u32[]{:S(2)}) copy-start(bf16[128,1024]{1,0:T(8,128)(2,1)} %param.22) | copy-start | bytes 786436
  0.6 12.2 %copy-start.18 = (f32[256]{0:T(256)S(1)}, f32[256]{0:T(256)}, u32[]{:S(2)}) copy-start(f32[256]{0:T(256)} %param.15) | copy-start | bytes 3076
  0.7 12.2 %copy-start.19 = (s32[128]{0:T(128)S(1)}, s32[128]{0:T(128)}, u32[]{:S(2)}) copy-start(s32[128]{0:T(128)} %param.14) | copy-start | bytes 1540
  0.7 12.4 %copy-start.14 = (bf16[128,1024]{1,0:T(8,128)(2,1)S(1)}, bf16[128,1024]{1,0:T(8,128)(2,1)}, u32[]{:S(2)}) copy-start(bf16[128,1024]{1,0:T(8,128)(2,1)} %param.13) | copy-start | bytes 786436
  2.2 11.4 %copy-start.20 = (bf16[128,1024]{1,0:T(8,128)(2,1)S(1)}, bf16[128,1024]{1,0:T(8,128)(2,1)}, u32[]{:S(2)}) copy-start(bf16[128,1024]{1,0:T(8,128)(2,1)} %param.16) | copy-start | bytes 786436
  2.2 11.4 %copy-start.21 = (bf16[128,1024]{1,0:T(8,128)(2,1)S(1)}, bf16[128,1024]{1,0:T(8,128)(2,1)}, u32[]{:S(2)}) copy-start(bf16[128,1024]{1,0:T(8,128)(2,1)} %param.12) | copy-start | bytes 786436
  2.2 18.2 %all-to-all-start = ((bf16[8,32,512]{2,1,0:T(8,128)(2,1)}), bf16[8,32,512]{2,1,0:T(8,128)(2,1)S(1)}, u32[]{:S(2)}, u32[]{:S(2)}) async-start(bf16[8,32,512]{2,1,0:T(8,128)(2,1)} %broadcast_in_dim.76), calls=%async_computation | async-start | bytes 524288 | tf_op jit(solution)/shard_map/all_to_all | solution.py:182
  12.9 0.7 copy-start.11
  12.9 1.8 %copy-start.13 = (bf16[256,1024]{1,0:T(8,128)(2,1)S(1)}, bf16[256,1024]{1,0:T(8,128)(2,1)}, u32[]{:S(2)}) copy-start(bf16[256,1024]{1,0:T(8,128)(2,1)} %param.21) | copy-start | bytes 1572868
  13.2 1.5 %copy-start.15 = (bf16[128,1024]{1,0:T(8,128)(2,1)}, bf16[128,1024]{1,0:T(8,128)(2,1)S(1)}, u32[]{:S(2)}) copy-start(bf16[128,1024]{1,0:T(8,128)(2,1)S(1)} %multiply_convert_fusion) | copy-start | bytes 786436
  14.7 23.2 %copy-start.1 = (bf16[256,1024]{1,0:T(8,128)(2,1)}, bf16[256,1024]{1,0:T(8,128)(2,1)S(1)}, u32[]{:S(2)}) copy-start(bf16[256,1024]{1,0:T(8,128)(2,1)S(1)} %convolution_convert_fusion.h_ref) | copy-start | bytes 1572868
  14.8 23.1 %copy-start.5 = (bf16[256,512]{1,0:T(8,128)(2,1)}, bf16[256,512]{1,0:T(8,128)(2,1)S(1)}, u32[]{:S(2)}) copy-start(bf16[256,512]{1,0:T(8,128)(2,1)S(1)} %get-tuple-element.20.g_ref) | copy-start | bytes 786436
  15.9 9.7 %collective-permute-start = (bf16[256,1536]{1,0:T(8,128)(2,1)}, bf16[256,1536]{1,0:T(8,128)(2,1)S(1)}, u32[]{:S(2)}, u32[]{:S(2)}) collective-permute-start(bf16[256,1536]{1,0:T(8,128)(2,1)} %pad_maximum_fusion), channel_id=1, source_target_pairs={{0,32},{32,0},{1,33},{33,1},{2,34},{34,2},{3,35},{35,3},{4,36},{36... | collective-permute-start | bytes 2359304 | tf_op jit(solution)/shard_map/ppermute | solution.py:34
  21.5 16.4 %all-to-all-start.1 = ((bf16[4,256,512]{2,1,0:T(8,128)(2,1)}), bf16[4,256,512]{2,1,0:T(8,128)(2,1)S(1)}, u32[]{:S(2)}, u32[]{:S(2)}) async-start(bf16[4,256,512]{2,1,0:T(8,128)(2,1)} %broadcast_in_dim.78), calls=%async_computation.1 | async-start | bytes 2097152 | tf_op jit(solution)/shard_map/all_to_all | solution.py:178
  25.6 14.8 %copy-start.7 = (bf16[256,1536]{1,0:T(8,128)(2,1)}, bf16[256,1536]{1,0:T(8,128)(2,1)S(1)}, u32[]{:S(2)}) copy-start(bf16[256,1536]{1,0:T(8,128)(2,1)S(1)} %collective-permute-done.peer_ref) | copy-start | bytes 2359300
  40.4 15.6 %all-to-all-start.2 = ((bf16[4,256,512]{2,1,0:T(8,128)(2,1)}), bf16[4,256,512]{2,1,0:T(8,128)(2,1)S(1)}, u32[]{:S(2)}, u32[]{:S(2)}) async-start(bf16[4,256,512]{2,1,0:T(8,128)(2,1)} %bitcast.2), calls=%async_computation.2 | async-start | bytes 2097152 | tf_op jit(solution)/shard_map/all_to_all | solution.py:212
  43.9 1.0 copy-start.2
  44.9 0.9 copy-start.6
  45.9 1.1 %copy-start.8 = (bf16[256,1536]{1,0:T(8,128)(2,1)S(1)}, bf16[256,1536]{1,0:T(8,128)(2,1)}, u32[]{:S(2)}) copy-start(bf16[256,1536]{1,0:T(8,128)(2,1)} %copy-done.7) | copy-start | bytes 2359300
  47.0 8.7 %copy-start.17 = (s32[32,4]{0,1:T(4,128)S(1)}, s32[32,4]{0,1:T(4,128)}, u32[]{:S(2)}) copy-start(s32[32,4]{0,1:T(4,128)} %param.23) | copy-start | bytes 1540
  49.2 0.7 copy-start.3
  49.9 18.3 %copy-start.16 = (bf16[128,1024]{1,0:T(8,128)(2,1)S(1)}, bf16[128,1024]{1,0:T(8,128)(2,1)}, u32[]{:S(2)}) copy-start(bf16[128,1024]{1,0:T(8,128)(2,1)} %copy-done.15) | copy-start | bytes 786436
  49.9 19.6 %collective-permute-start.1 = (bf16[256,1536]{1,0:T(8,128)(2,1)}, bf16[256,1536]{1,0:T(8,128)(2,1)}, u32[]{:S(2)}, u32[]{:S(2)}) collective-permute-start(bf16[256,1536]{1,0:T(8,128)(2,1)} %get-tuple-element.12), channel_id=1, source_target_pairs={{0,32},{32,0},{1,33},{33,1},{2,34},{34,2},{3,35},{35,3},{4,36},{36... | collective-permute-start | bytes 2359304 | tf_op jit(solution)/shard_map/ppermute | solution.py:34
  55.9 13.6 %copy-start.12 = (f32[2,128,3,128]{1,0,3,2:T(2,128)S(1)}, f32[2,128,3,128]{1,0,3,2:T(2,128)}, u32[]{:S(2)}) copy-start(f32[2,128,3,128]{1,0,3,2:T(2,128)} %copy-done.11) | copy-start | bytes 1179652
  56.9 20.5 %all-to-all-start.3 = ((bf16[8,32,512]{2,1,0:T(8,128)(2,1)}), bf16[8,32,512]{2,1,0:T(8,128)(2,1)S(1)}, u32[]{:S(2)}, u32[]{:S(2)}) async-start(bf16[8,32,512]{2,1,0:T(8,128)(2,1)} %bitcast.3), calls=%async_computation.3 | async-start | bytes 524288 | tf_op jit(solution)/shard_map/all_to_all | solution.py:235
  71.4 1.2 %copy-start.9 = (f32[384,1024]{1,0:T(8,128)}, f32[384,1024]{1,0:T(8,128)S(1)}, u32[]{:S(2)}) copy-start(f32[384,1024]{1,0:T(8,128)S(1)} %fusion.6) | copy-start | bytes 4718596
  72.6 9.0 %copy-start.4 = (bf16[256,512]{1,0:T(8,128)(2,1)S(1)}, bf16[256,512]{1,0:T(8,128)(2,1)}, u32[]{:S(2)}) copy-start(bf16[256,512]{1,0:T(8,128)(2,1)} %copy-done.3) | copy-start | bytes 786436
  73.8 9.7 %copy-start.10 = (f32[384,1024]{1,0:T(8,128)S(1)}, f32[384,1024]{1,0:T(8,128)}, u32[]{:S(2)}) copy-start(f32[384,1024]{1,0:T(8,128)} %copy-done.9) | copy-start | bytes 4718596
  77.4 33.4 %all-to-all-start.4 = ((bf16[32,8,1024]{2,1,0:T(8,128)(2,1)}), bf16[32,8,1024]{2,1,0:T(8,128)(2,1)S(1)}, u32[]{:S(2)}, u32[]{:S(2)}) async-start(bf16[32,8,1024]{2,1,0:T(8,128)(2,1)} %pad_maximum_fusion.2), calls=%async_computation.4 | async-start | bytes 1048576 | tf_op jit(solution)/shard_map/all_to_all | solution.py:238
